TPU v7x, 256 devices: a whole 4x4x8 slice. The times are simulated.
256 devices in a mesh: samp: 8 (over x, core), state: 32 (over z, y).
Axes of the slice: x: 4, y: 4, z: 8, core: 2. Of those that a mesh axis runs over, the one named last changes fastest.
Arguments:
- components: bfloat16 [64, 262144], P(None, 'samp'), may hold values from -96 to 96
- coefficients: bfloat16 [64, 4096], P(None, 'state'), may hold values from -1.5 to 1.5
- block_window: int32 [2048], P('samp'), may hold values from 0 to 4095
- block_fill: int32 [2048], P('samp'), may hold values from 1 to 128
Outputs:
- free_energy: float32 [4096], P('state')
- log_denom: float32 [262144], P('samp')
Inputs may be any that keep to these rules, and one draw needn't show every extreme that they name: `block_window`: blocks of one generating state may stand anywhere; some states generate no block.
All inputs are finite; a program needn't handle non-finite values.
Results may differ from a plain program's by a relative error of at most 0.0003.
Values may be sent and summed in bfloat16 or wider, within the bound.
No kernel may reach another device: no remote copies, remote signals or barrier semaphores. Data moves between devices by JAX's collectives and lax.ppermute only.
A program may use at most 128 MiB of HBM per device.

v0:
```python
import functools

import jax
import jax.numpy as jnp
from jax import lax
from jax.sharding import Mesh
from jax.sharding import PartitionSpec as P

BLOCK = 128
ITERS = 2
STATE = ("state_0", "state_1")
SAMP_STATE = ("samp_0", "samp_1", "state_0", "state_1")
SAMP = ("samp_0", "samp_1")


NEGATIVE = -1e30


def laid_out(pieces, dim):
    dims = list(pieces.shape[1:])
    dims[dim] *= pieces.shape[0]
    return jnp.moveaxis(pieces, 0, dim).reshape(dims)


def copy_for_each(x, axis):
    copies = jnp.broadcast_to(x, (lax.axis_size(axis), *x.shape))
    return lax.all_to_all(copies, axis, split_axis=0, concat_axis=0, tiled=True)


def gathered_copies(x, axis, dim):
    return laid_out(copy_for_each(x, axis), dim)


def over_axes(x, axes):
    return functools.reduce(lax.psum, axes, x)


def combined_by_axis(x, axes, combine):
    for axis in axes:
        pieces = jax.tree.map(lambda part: lax.all_gather(part, axis), x)
        x = jax.tree.map(lambda part: part[0], pieces)
        for k in range(1, lax.axis_size(axis)):
            x = combine(x, jax.tree.map(lambda part: part[k], pieces))
    return x


def combine_sums(former, latter):
    highest = jnp.maximum(former[0], latter[0])
    totals = former[1] * jnp.exp(former[0] - highest) + latter[1] * jnp.exp(latter[0] - highest)
    return (highest, totals)


def alive_slots(filled):
    return (jnp.arange(BLOCK, dtype=jnp.int32)[None, :] < filled[:, None]).reshape(-1)


def sample_partials(energy, logden, alive):
    exponents = jnp.where(alive[None, :], -energy - logden[None, :], NEGATIVE)
    highest = jnp.max(exponents, axis=1)
    totals = jnp.sum(jnp.exp(exponents - highest[:, None]), axis=1)
    return (highest, totals)


def logarithm_counts(counts):
    return jnp.where(counts > 0, jnp.log(jnp.maximum(counts, 1.0)), NEGATIVE)


def shards(components, coefficients, block_window, block_fill):
    state_count = lax.axis_size(STATE)
    position = lax.axis_index(STATE)
    own_states = coefficients.shape[1]
    row_count = components.shape[1] // state_count
    block_count = row_count // BLOCK
    component_rows = lax.dynamic_slice_in_dim(components, position * row_count, row_count, 1)
    window_rows = lax.dynamic_slice_in_dim(block_window, position * block_count, block_count, 0)
    fill_rows = lax.dynamic_slice_in_dim(block_fill, position * block_count, block_count, 0)
    energy = lax.dot_general(
        gathered_copies(coefficients, STATE, 1),
        component_rows,
        (((0,), (0,)), ((), ())),
        preferred_element_type=jnp.float32,
    )
    total_states = energy.shape[0]
    onehot = (window_rows[:, None] == jnp.arange(total_states, dtype=jnp.int32)[None, :]).astype(
        jnp.float32
    )
    partial_counts = jnp.sum(fill_rows.astype(jnp.float32)[:, None] * onehot, axis=0)
    counts = over_axes(partial_counts, SAMP_STATE)
    log_count = logarithm_counts(counts)
    alive = alive_slots(fill_rows)

    def local_denominator(free):
        exponents = (log_count + free)[:, None] - energy
        highest = jnp.max(exponents, axis=0)
        return highest + jnp.log(jnp.sum(jnp.exp(exponents - highest[None, :]), axis=0))

    free = jnp.zeros((total_states,), jnp.float32)
    for sweep in range(ITERS):
        logden = local_denominator(free)
        partials = sample_partials(energy, logden, alive)
        highest, totals = combined_by_axis(partials, SAMP_STATE, combine_sums)
        free = -(highest + jnp.log(totals))
        free = free - free[0]
    logden = local_denominator(free)
    log_denom = gathered_copies(logden, STATE, 0)
    free_energy = lax.dynamic_slice_in_dim(free, position * own_states, own_states, 0)
    return (free_energy, log_denom)


def solution(mesh):
    torus = Mesh(mesh.devices.reshape(4, 2, 8, 4), ("samp_0", "samp_1", "state_0", "state_1"))
    placed = (P(None, SAMP), P(None, STATE), P(SAMP), P(SAMP))
    return jax.shard_map(
        shards, mesh=torus, in_specs=placed, out_specs=(P(STATE), P(SAMP)), check_vma=False
    )
```

profile of v0, /device:TPU:2, one launch (start us, length us, event | category | flops | bytes accessed | tf_op | source)
XLA Modules:
  0.0 385.7 jit_solution(7878590312702239643)
XLA Ops:
  2.3 11.5 %all-to-all-start = ((bf16[32,64,128]{2,1,0:T(8,128)(2,1)}), bf16[32,64,128]{2,1,0:T(8,128)(2,1)S(1)}, u32[]{:S(2)}, u32[]{:S(2)}) async-start(bf16[32,64,128]{2,1,0:T(8,128)(2,1)} %broadcast_in_dim.25), calls=%async_computation | async-start | bytes 1048576 | tf_op jit(solution)/shard_map/all_to_all | solution.py:27
  15.4 13.9 %psum.28 = f32[4096]{0:T(1024)S(1)} all-reduce(f32[4096]{0:T(1024)S(1)} %select_reduce_fusion), channel_id=1, replica_groups=mesh['samp_0'=4,'samp_1'=2,'state_0'=8,'state_1'=4] {'samp_0'}, use_global_device_ids=true, to_apply=%region_1.0 | all-reduce | flops 4096 | bytes 32768 | tf_op jit(solution)/shard_map/psum | solution.py:35
  29.3 3.3 psum.29
  32.7 30.0 %psum.30 = f32[4096]{0:T(1024)S(1)} all-reduce(f32[4096]{0:T(1024)S(1)} %psum.29), channel_id=1, replica_groups=mesh['samp_0'=4,'samp_1'=2,'state_0'=8,'state_1'=4] {'state_0'}, use_global_device_ids=true, to_apply=%region_3.0 | all-reduce | flops 4096 | bytes 32768 | tf_op jit(solution)/shard_map/psum | solution.py:35
  62.6 16.8 %psum.31 = f32[4096]{0:T(1024)S(1)} all-reduce(f32[4096]{0:T(1024)S(1)} %psum.30), channel_id=1, replica_groups=mesh['samp_0'=4,'samp_1'=2,'state_0'=8,'state_1'=4] {'state_1'}, use_global_device_ids=true, to_apply=%region_4.0 | all-reduce | flops 4096 | bytes 32768 | tf_op jit(solution)/shard_map/psum | solution.py:35
  79.6 9.0 %subtract_reduce_fusion.2 = (f32[1024]{0:T(1024)S(1)}, f32[1024,4096]{1,0:T(8,128)}) fusion(f32[4096]{0:T(1024)S(1)} %log_select_fusion, bf16[64,32768]{1,0:T(8,128)(2,1)} %param.4, s32[]{:T(128)S(6)} %select_n.24, bf16[32,64,128]{2,1,0:T(8,128)(2,1)S(1)} %all-to-all-done), kind=kOutput, calls=%fused_computation.9 | convolution fusion | flops 545258496 | bytes 17453060 | tf_op jit(solution)/shard_map/dot_general | solution.py:77
  88.6 8.7 %exponential_reduce_fusion.4 = f32[1024]{0:T(1024)S(1)} fusion(f32[1024,4096]{1,0:T(8,128)} %get-tuple-element.47, f32[1024]{0:T(1024)S(1)} %get-tuple-element.46, f32[4096]{0:T(1024)S(1)} %log_select_fusion), kind=kLoop, calls=%fused_computation.6 | loop fusion | flops 12581888 | bytes 16801792 | tf_op jit(solution)/shard_map/reduce_sum | solution.py:95
  97.3 8.9 %fusion = f32[4096]{0:T(1024)S(1)} fusion(f32[1024,4096]{1,0:T(8,128)} %get-tuple-element.47, f32[1024]{0:T(1024)S(1)} %log_add_fusion.2, pred[1024]{0:T(1024)(128)(4,1)S(1)} %fusion.70), kind=kLoop, calls=%fused_computation.10 | loop fusion | flops 16773120 | bytes 16798720 | tf_op jit(solution)/shard_map/reduce_max | solution.py:59
  106.2 8.3 %exponential_reduce_fusion.1 = f32[4096]{0:T(1024)S(1)} fusion(f32[1024,4096]{1,0:T(8,128)} %get-tuple-element.47, f32[4096]{0:T(1024)S(1)} %fusion, f32[1024]{0:T(1024)S(1)} %log_add_fusion.2, pred[1024]{0:T(1024)(128)(4,1)S(1)} %fusion.70), kind=kLoop, calls=%fused_computation.1 | loop fusion | flops 20967424 | bytes 16815104 | tf_op jit(solution)/shard_map/reduce_sum | solution.py:60
  114.5 12.1 %all-gather = f32[16384]{0:T(1024)S(1)} all-gather(f32[4096]{0:T(1024)S(1)} %fusion), channel_id=2, replica_groups=mesh['samp_0'=4,'samp_1'=2,'state_0'=8,'state_1'=4] {'samp_0'}, dimensions={0}, use_global_device_ids=true | all-gather | bytes 81920 | tf_op jit(solution)/shard_map/all_gather | solution.py:40
  126.6 12.0 %all-gather.1 = f32[16384]{0:T(1024)S(1)} all-gather(f32[4096]{0:T(1024)S(1)} %exponential_reduce_fusion.1), channel_id=3, replica_groups=mesh['samp_0'=4,'samp_1'=2,'state_0'=8,'state_1'=4] {'samp_0'}, dimensions={0}, use_global_device_ids=true | all-gather | bytes 81920 | tf_op jit(solution)/shard_map/all_gather | solution.py:40
  138.8 1.8 all-gather.4
  140.6 1.8 all-gather.7
  142.5 24.6 %all-gather.5 = f32[8,1,4096]{2,1,0:T(1,128)S(1)} all-gather(f32[1,1,4096]{2,1,0:T(1,128)S(1)} %get-tuple-element.44), channel_id=1, replica_groups=mesh['samp_0'=4,'samp_1'=2,'state_0'=8,'state_1'=4] {'state_0'}, dimensions={0}, use_global_device_ids=true | all-gather | bytes 147456 | tf_op jit(solution)/shard_map/all_gather | solution.py:40
  167.1 24.6 %all-gather.8 = f32[8,1,4096]{2,1,0:T(1,128)S(1)} all-gather(f32[1,1,4096]{2,1,0:T(1,128)S(1)} %get-tuple-element.45), channel_id=1, replica_groups=mesh['samp_0'=4,'samp_1'=2,'state_0'=8,'state_1'=4] {'state_0'}, dimensions={0}, use_global_device_ids=true | all-gather | bytes 147456 | tf_op jit(solution)/shard_map/all_gather | solution.py:40
  192.0 11.9 %all-gather.9 = f32[4,1,4096]{2,1,0:T(1,128)S(1)} all-gather(f32[1,1,4096]{2,1,0:T(1,128)S(1)} %fusion.68), channel_id=1, replica_groups=mesh['samp_0'=4,'samp_1'=2,'state_0'=8,'state_1'=4] {'state_1'}, dimensions={0}, use_global_device_ids=true | all-gather | bytes 81920 | tf_op jit(solution)/shard_map/all_gather | solution.py:40
  203.9 11.9 %all-gather.6 = f32[4,1,4096]{2,1,0:T(1,128)S(1)} all-gather(f32[1,1,4096]{2,1,0:T(1,128)S(1)} %maximum_bitcast_fusion.3), channel_id=1, replica_groups=mesh['samp_0'=4,'samp_1'=2,'state_0'=8,'state_1'=4] {'state_1'}, dimensions={0}, use_global_device_ids=true | all-gather | bytes 81920 | tf_op jit(solution)/shard_map/all_gather | solution.py:40
  217.0 7.1 %subtract_reduce_fusion.1 = f32[1024]{0:T(1024)S(1)} fusion(f32[1024,4096]{1,0:T(8,128)} %get-tuple-element.47, f32[4096]{0:T(1024)S(1)} %subtract_add_fusion), kind=kLoop, calls=%fused_computation.8 | loop fusion | flops 8387584 | bytes 16797696 | tf_op jit(solution)/shard_map/reduce_max | solution.py:94
  224.0 8.7 %exponential_reduce_fusion.3 = f32[1024]{0:T(1024)S(1)} fusion(f32[1024,4096]{1,0:T(8,128)} %get-tuple-element.47, f32[1024]{0:T(1024)S(1)} %subtract_reduce_fusion.1, f32[4096]{0:T(1024)S(1)} %subtract_add_fusion), kind=kLoop, calls=%fused_computation.4 | loop fusion | flops 12581888 | bytes 16801792 | tf_op jit(solution)/shard_map/reduce_sum | solution.py:95
  232.8 8.9 %fusion.1 = f32[4096]{0:T(1024)S(1)} fusion(f32[1024,4096]{1,0:T(8,128)} %get-tuple-element.47, f32[1024]{0:T(1024)S(1)} %log_add_fusion.1, pred[1024]{0:T(1024)(128)(4,1)S(1)} %fusion.70), kind=kLoop, calls=%fused_computation.11 | loop fusion | flops 16773120 | bytes 16798720 | tf_op jit(solution)/shard_map/reduce_max | solution.py:59
  241.7 8.3 %exponential_reduce_fusion = f32[4096]{0:T(1024)S(1)} fusion(f32[1024,4096]{1,0:T(8,128)} %get-tuple-element.47, f32[4096]{0:T(1024)S(1)} %fusion.1, f32[1024]{0:T(1024)S(1)} %log_add_fusion.1, pred[1024]{0:T(1024)(128)(4,1)S(1)} %fusion.70), kind=kLoop, calls=%fused_computation | loop fusion | flops 20967424 | bytes 16815104 | tf_op jit(solution)/shard_map/reduce_sum | solution.py:60
  250.0 11.9 %all-gather.2 = f32[16384]{0:T(1024)S(1)} all-gather(f32[4096]{0:T(1024)S(1)} %fusion.1), channel_id=4, replica_groups=mesh['samp_0'=4,'samp_1'=2,'state_0'=8,'state_1'=4] {'samp_0'}, dimensions={0}, use_global_device_ids=true | all-gather | bytes 81920 | tf_op jit(solution)/shard_map/all_gather | solution.py:40
  261.8 11.9 %all-gather.3 = f32[16384]{0:T(1024)S(1)} all-gather(f32[4096]{0:T(1024)S(1)} %exponential_reduce_fusion), channel_id=5, replica_groups=mesh['samp_0'=4,'samp_1'=2,'state_0'=8,'state_1'=4] {'samp_0'}, dimensions={0}, use_global_device_ids=true | all-gather | bytes 81920 | tf_op jit(solution)/shard_map/all_gather | solution.py:40
  273.8 1.8 all-gather.10
  277.5 24.6 %all-gather.11 = f32[8,1,4096]{2,1,0:T(1,128)S(1)} all-gather(f32[1,1,4096]{2,1,0:T(1,128)S(1)} %get-tuple-element.42), channel_id=1, replica_groups=mesh['samp_0'=4,'samp_1'=2,'state_0'=8,'state_1'=4] {'state_0'}, dimensions={0}, use_global_device_ids=true | all-gather | bytes 147456 | tf_op jit(solution)/shard_map/all_gather | solution.py:40
  302.1 24.6 %all-gather.14 = f32[8,1,4096]{2,1,0:T(1,128)S(1)} all-gather(f32[1,1,4096]{2,1,0:T(1,128)S(1)} %get-tuple-element.43), channel_id=1, replica_groups=mesh['samp_0'=4,'samp_1'=2,'state_0'=8,'state_1'=4] {'state_0'}, dimensions={0}, use_global_device_ids=true | all-gather | bytes 147456 | tf_op jit(solution)/shard_map/all_gather | solution.py:40
  327.1 11.9 %all-gather.15 = f32[4,1,4096]{2,1,0:T(1,128)S(1)} all-gather(f32[1,1,4096]{2,1,0:T(1,128)S(1)} %fusion.69), channel_id=1, replica_groups=mesh['samp_0'=4,'samp_1'=2,'state_0'=8,'state_1'=4] {'state_1'}, dimensions={0}, use_global_device_ids=true | all-gather | bytes 81920 | tf_op jit(solution)/shard_map/all_gather | solution.py:40
  338.9 12.1 %all-gather.12 = f32[4,1,4096]{2,1,0:T(1,128)S(1)} all-gather(f32[1,1,4096]{2,1,0:T(1,128)S(1)} %maximum_bitcast_fusion), channel_id=1, replica_groups=mesh['samp_0'=4,'samp_1'=2,'state_0'=8,'state_1'=4] {'state_1'}, dimensions={0}, use_global_device_ids=true | all-gather | bytes 81920 | tf_op jit(solution)/shard_map/all_gather | solution.py:40
  352.2 7.1 %subtract_reduce_fusion = f32[1024]{0:T(1024)S(1)} fusion(f32[1024,4096]{1,0:T(8,128)} %get-tuple-element.47, f32[4096]{0:T(1024)S(1)} %get-tuple-element.2), kind=kLoop, calls=%fused_computation.7 | loop fusion | flops 8387584 | bytes 16797696 | tf_op jit(solution)/shard_map/reduce_max | solution.py:94
  359.3 8.7 %exponential_reduce_fusion.2 = f32[1024]{0:T(1024)S(1)} fusion(f32[1024,4096]{1,0:T(8,128)} %get-tuple-element.47, f32[1024]{0:T(1024)S(1)} %subtract_reduce_fusion, f32[4096]{0:T(1024)S(1)} %get-tuple-element.2), kind=kLoop, calls=%fused_computation.2 | loop fusion | flops 12581888 | bytes 16801792 | tf_op jit(solution)/shard_map/reduce_sum | solution.py:95
  368.8 5.8 %all-to-all-start.1 = ((f32[32,1,1024]{2,1,0:T(1,128)}), f32[32,1,1024]{2,1,0:T(1,128)S(1)}, u32[]{:S(2)}, u32[]{:S(2)}) async-start(f32[32,1,1024]{2,1,0:T(1,128)} %broadcast_in_dim.45), calls=%async_computation.1 | async-start | bytes 262144 | tf_op jit(solution)/shard_map/all_to_all | solution.py:27
  375.2 9.9 %all-to-all-done.1 = f32[32,1,1024]{2,1,0:T(1,128)S(1)} async-done(((f32[32,1,1024]{2,1,0:T(1,128)}), f32[32,1,1024]{2,1,0:T(1,128)S(1)}, u32[]{:S(2)}, u32[]{:S(2)}) %all-to-all-start.1) | async-done | bytes 131104 | tf_op jit(solution)/shard_map/all_to_all | solution.py:27
  (36 shorter events, 10.7 us)
Async XLA Ops:
  2.3 77.3 %all-to-all-start = ((bf16[32,64,128]{2,1,0:T(8,128)(2,1)}), bf16[32,64,128]{2,1,0:T(8,128)(2,1)S(1)}, u32[]{:S(2)}, u32[]{:S(2)}) async-start(bf16[32,64,128]{2,1,0:T(8,128)(2,1)} %broadcast_in_dim.25), calls=%async_computation | async-start | bytes 1048576 | tf_op jit(solution)/shard_map/all_to_all | solution.py:27
  368.8 16.3 %all-to-all-start.1 = ((f32[32,1,1024]{2,1,0:T(1,128)}), f32[32,1,1024]{2,1,0:T(1,128)S(1)}, u32[]{:S(2)}, u32[]{:S(2)}) async-start(f32[32,1,1024]{2,1,0:T(1,128)} %broadcast_in_dim.45), calls=%async_computation.1 | async-start | bytes 262144 | tf_op jit(solution)/shard_map/all_to_all | solution.py:27
where the time goes:
time: 388 us; the launch traced here: 386 us
  blocking collectives  265 us (68%)
  other arithmetic  78.2 us (20%)
  starting transfers between devices  17.3 us (4%)
  waiting for transfers between devices  9.91 us (3%)
  matrix products  9 us (2%)
  local copies, waits for them, and re-layouts  5.43 us (1%)
    all_gather x16, blocking collectives, combined_by_axis(): pieces = jax.tree.map(lambda part: lax.all_gather(part, axis), x)  201 us
    psum x4, blocking collectives, over_axes(): return functools.reduce(lax.psum, axes, x)  64.1 us
    reduce_sum x3, other arithmetic, local_denominator(): jnp.sum(jnp.exp(exponents - highest[None, :]), axis=0)  26.2 us
    reduce_max x2, other arithmetic, sample_partials(): highest = jnp.max(exponents, axis=1)  17.8 us
    all_to_all x2, starting transfers between devices, copy_for_each(): return lax.all_to_all(copies, axis, split_axis=0, concat_axis=0, tiled=True)  17.3 us
    reduce_sum x2, other arithmetic, sample_partials(): totals = jnp.sum(jnp.exp(exponents - highest[:, None]), axis=1)  16.6 us
    reduce_max x2, other arithmetic, local_denominator(): highest = jnp.max(exponents, axis=0)  14.2 us
    all_to_all x2, waiting for transfers between devices, copy_for_each(): return lax.all_to_all(copies, axis, split_axis=0, concat_axis=0, tiled=True)  9.91 us
  transfers between devices with their start and end apart: 2, of which 1 were waited for; matrix products, arithmetic and copies ran while one was open for 1% of the time, Pallas kernels for 0%

commit v1 on v0

v1 whole, which is shorter than its diff:
```python
import jax
import jax.numpy as jnp
from jax import lax
from jax.sharding import Mesh
from jax.sharding import PartitionSpec as P

BLOCK = 128
ITERS = 2
STATE = ("state_0", "state_1")
SAMP = ("samp_0", "samp_1")
NEGATIVE = -1e30


def copies_of_each(x, axes):
    copies = jnp.broadcast_to(x, (lax.axis_size(axes), *x.shape))
    return lax.all_to_all(copies, axes, split_axis=0, concat_axis=0, tiled=True)


def laid_out(pieces, dim):
    dims = list(pieces.shape[1:])
    dims[dim] *= pieces.shape[0]
    return jnp.moveaxis(pieces, 0, dim).reshape(dims)


def log_sum(logs):
    highest = jnp.max(logs, axis=0)
    return highest + jnp.log(jnp.sum(jnp.exp(logs - highest[None]), axis=0))


def shards(components, coefficients, block_window, block_fill):
    state_count = lax.axis_size(STATE)
    position = lax.axis_index(STATE)
    own_states = coefficients.shape[1]
    row_count = components.shape[1] // state_count
    block_count = row_count // BLOCK
    component_rows = lax.dynamic_slice_in_dim(components, position * row_count, row_count, 1)
    fill_rows = lax.dynamic_slice_in_dim(block_fill, position * block_count, block_count, 0)
    gathered = copies_of_each(coefficients, STATE)
    blocks = copies_of_each(jnp.stack([block_window, block_fill]), SAMP)
    windows, fills = blocks[:, 0].reshape(-1), blocks[:, 1].reshape(-1)
    energy = lax.dot_general(
        laid_out(gathered, 1), component_rows, (((0,), (0,)), ((), ())), preferred_element_type=jnp.float32
    )
    total_states = energy.shape[0]
    low = 128
    fills_high = jnp.where(
        windows[None, :] // low == jnp.arange(total_states // low, dtype=jnp.int32)[:, None], fills[None, :], 0
    ).astype(jnp.bfloat16)
    is_low = (windows[None, :] % low == jnp.arange(low, dtype=jnp.int32)[:, None]).astype(jnp.bfloat16)
    counts = lax.dot_general(
        fills_high, is_low, (((1,), (1,)), ((), ())), preferred_element_type=jnp.float32
    ).reshape(-1)
    log_count = jnp.where(counts > 0, jnp.log(jnp.maximum(counts, 1.0)), NEGATIVE)
    alive = (jnp.arange(BLOCK, dtype=jnp.int32)[None, :] < fill_rows[:, None]).reshape(-1)

    def local_denominator(free):
        exponents = (log_count + free)[:, None] - energy
        highest = jnp.max(exponents, axis=0)
        return highest + jnp.log(jnp.sum(jnp.exp(exponents - highest[None, :]), axis=0))

    free = jnp.zeros((total_states,), jnp.float32)
    for sweep in range(ITERS):
        logden = local_denominator(free)
        exponents = jnp.where(alive[None, :], -energy - logden[None, :], NEGATIVE)
        highest = jnp.max(exponents, axis=1)
        logs = highest + jnp.log(jnp.sum(jnp.exp(exponents - highest[:, None]), axis=1))
        for axes in (SAMP, STATE):
            logs = log_sum(copies_of_each(logs, axes))
        free = -logs
        free = free - free[0]
    logden = local_denominator(free)
    log_denom = laid_out(copies_of_each(logden, STATE), 0)
    free_energy = lax.dynamic_slice_in_dim(free, position * own_states, own_states, 0)
    return (free_energy, log_denom)


def solution(mesh):
    torus = Mesh(mesh.devices.reshape(4, 2, 8, 4), ("samp_0", "samp_1", "state_0", "state_1"))
    placed = (P(None, SAMP), P(None, STATE), P(SAMP), P(SAMP))
    return jax.shard_map(
        shards, mesh=torus, in_specs=placed, out_specs=(P(STATE), P(SAMP)), check_vma=False
    )
```

time: 388 us -> 208 us (0.54)
  blocking collectives: 265 us -> 69.5 us
  waiting for transfers between devices: 9.91 us -> 26.5 us
    all_gather x16 -> x0, blocking collectives: 201 us -> none  [combined_by_axis(): pieces = jax.tree.map(lambda part: lax.all_gather(part, axis), x)]
    all_to_all x0 -> x5, blocking collectives: none -> 69.5 us  [copies_of_each(): return lax.all_to_all(copies, axes, split_axis=0, concat_axis=0, tiled=True)]
    psum x4 -> x0, blocking collectives: 64.1 us -> none  [over_axes(): return functools.reduce(lax.psum, axes, x)]
    all_to_all x2, waiting for transfers between devices: 9.91 us -> 26.5 us  [copies_of_each(): return lax.all_to_all(copies, axes, split_axis=0, concat_axis=0, tiled=True)]
    reduce_max x2 -> x6, other arithmetic: 17.8 us -> 18.7 us  [the longest x2 17.8 us: shards(): highest = jnp.max(exponents, axis=1)]
    reduce_sum x3 -> x6, other arithmetic: 16.7 us -> 17.5 us  [the longest x2 16.6 us: shards(): jnp.sum(jnp.exp(exponents - highest[:, None]), axis=1)]
    dot_general x1 -> x2, matrix products: 9 us -> 9.3 us  [the longest x1 8.99 us: shards(): lax.dot_general(laid_out(gathered, 1), component_rows, (((0,), (0,)), (()...]
  transfers between devices with their start and end apart: 2 -> 2, of which waited for: 1 -> 2; matrix products, arithmetic and copies ran while one was open for 1% -> 1% of each run, Pallas kernels for 0% -> 0%
where the time goes in v1:
time: 208 us; the launch traced here: 207 us
  other arithmetic  78.6 us (38%)
  blocking collectives  69.5 us (33%)
  waiting for transfers between devices  26.5 us (13%)
  starting transfers between devices  16.2 us (8%)
  matrix products  9.3 us (4%)
  local copies, waits for them, and re-layouts  6.48 us (3%)
    all_to_all x5, blocking collectives, copies_of_each(): return lax.all_to_all(copies, axes, split_axis=0, concat_axis=0, tiled=True)  69.5 us
    all_to_all x2, waiting for transfers between devices, copies_of_each(): return lax.all_to_all(copies, axes, split_axis=0, concat_axis=0, tiled=True)  26.5 us
    reduce_sum x3, other arithmetic, local_denominator(): jnp.sum(jnp.exp(exponents - highest[None, :]), axis=0)  26.1 us
    reduce_max x2, other arithmetic, shards(): highest = jnp.max(exponents, axis=1)  17.8 us
    reduce_sum x2, other arithmetic, shards(): jnp.sum(jnp.exp(exponents - highest[:, None]), axis=1)  16.6 us
    all_to_all x2, starting transfers between devices, copies_of_each(): return lax.all_to_all(copies, axes, split_axis=0, concat_axis=0, tiled=True)  16.2 us
    reduce_max x2, other arithmetic, local_denominator(): highest = jnp.max(exponents, axis=0)  14.2 us
    dot_general x1, matrix products, shards(): lax.dot_general(laid_out(gathered, 1), component_rows, (((0,), (0,)), (()...  8.99 us
  transfers between devices with their start and end apart: 2, of which 2 were waited for; matrix products, arithmetic and copies ran while one was open for 1% of the time, Pallas kernels for 0%

profile of v1, /device:TPU:2, one launch (start us, length us, event | category | flops | bytes accessed | tf_op | source)
XLA Modules:
  0.0 207.5 jit_solution(5750359432041453677)
XLA Ops:
  0.6 0.7 pad_add_fusion
  1.4 8.5 %all_to_all.52 = s32[8,2,256]{2,1,0:T(2,128)S(1)} all-to-all(s32[8,2,256]{2,1,0:T(2,128)S(1)} %broadcast_in_dim.75), channel_id=1, replica_groups=mesh['samp_0'=4,'samp_1'=2,'state_0'=8,'state_1'=4] {'samp_0','samp_1'}, dimensions={0} | all-to-all | bytes 32768 | tf_op jit(solution)/shard_map/all_to_all | solution.py:16
  9.9 1.6 broadcast_in_dim.74
  11.5 11.5 %all-to-all-start = ((bf16[32,64,128]{2,1,0:T(8,128)(2,1)}), bf16[32,64,128]{2,1,0:T(8,128)(2,1)S(1)}, u32[]{:S(2)}, u32[]{:S(2)}) async-start(bf16[32,64,128]{2,1,0:T(8,128)(2,1)} %broadcast_in_dim.74), calls=%async_computation | async-start | bytes 1048576 | tf_op jit(solution)/shard_map/all_to_all | solution.py:16
  23.0 0.8 dynamic_slice.9
  24.2 16.5 %all-to-all-done = bf16[32,64,128]{2,1,0:T(8,128)(2,1)S(1)} async-done(((bf16[32,64,128]{2,1,0:T(8,128)(2,1)}), bf16[32,64,128]{2,1,0:T(8,128)(2,1)S(1)}, u32[]{:S(2)}, u32[]{:S(2)}) %all-to-all-start) | async-done | bytes 524320 | tf_op jit(solution)/shard_map/all_to_all | solution.py:16
  40.7 9.0 %subtract_reduce_fusion.2 = (f32[1024]{0:T(1024)S(1)}, f32[1024,4096]{1,0:T(8,128)}) fusion(f32[4096]{0:T(1024)S(1)} %select_bitcast_fusion, bf16[64,32768]{1,0:T(8,128)(2,1)} %param.4, s32[]{:T(128)S(6)} %select_n.62, bf16[32,64,128]{2,1,0:T(8,128)(2,1)S(1)} %all-to-all-done), kind=kOutput, calls=%fused_computation.9 | convolution fusion | flops 545258496 | bytes 17453060 | tf_op jit(solution)/shard_map/dot_general | solution.py:41
  49.7 8.6 %exponential_reduce_fusion.4 = f32[1024]{0:T(1024)S(1)} fusion(f32[1024,4096]{1,0:T(8,128)} %get-tuple-element.9, f32[1024]{0:T(1024)S(1)} %get-tuple-element.8, f32[4096]{0:T(1024)S(1)} %select_bitcast_fusion), kind=kLoop, calls=%fused_computation.6 | loop fusion | flops 12581888 | bytes 16801792 | tf_op jit(solution)/shard_map/reduce_sum | solution.py:59
  58.3 8.9 %fusion = f32[4096]{0:T(1024)S(1)} fusion(f32[1024,4096]{1,0:T(8,128)} %get-tuple-element.9, f32[1024]{0:T(1024)S(1)} %log_add_fusion.6, pred[1024]{0:T(1024)(128)(4,1)S(1)} %fusion.21), kind=kLoop, calls=%fused_computation.10 | loop fusion | flops 16773120 | bytes 16798720 | tf_op jit(solution)/shard_map/reduce_max | solution.py:65
  67.2 8.3 %exponential_reduce_fusion.1 = f32[4096]{0:T(1024)S(1)} fusion(f32[1024,4096]{1,0:T(8,128)} %get-tuple-element.9, f32[4096]{0:T(1024)S(1)} %fusion, f32[1024]{0:T(1024)S(1)} %log_add_fusion.6, pred[1024]{0:T(1024)(128)(4,1)S(1)} %fusion.21), kind=kLoop, calls=%fused_computation.1 | loop fusion | flops 20967424 | bytes 16815104 | tf_op jit(solution)/shard_map/reduce_sum | solution.py:66
  75.6 8.5 %all_to_all.53 = f32[8,1,4096]{2,1,0:T(1,128)S(1)} all-to-all(f32[8,1,4096]{2,1,0:T(1,128)S(1)} %broadcast_in_dim.81), channel_id=1, replica_groups=mesh['samp_0'=4,'samp_1'=2,'state_0'=8,'state_1'=4] {'samp_0','samp_1'}, dimensions={0} | all-to-all | bytes 262144 | tf_op jit(solution)/shard_map/all_to_all | solution.py:16
  84.3 0.5 broadcast_in_dim.82
  84.8 22.0 %all_to_all.54 = f32[32,1,4096]{2,1,0:T(1,128)S(1)} all-to-all(f32[32,1,4096]{2,1,0:T(1,128)S(1)} %broadcast_in_dim.82), channel_id=1, replica_groups=mesh['samp_0'=4,'samp_1'=2,'state_0'=8,'state_1'=4] {'state_0','state_1'}, dimensions={0} | all-to-all | bytes 1048576 | tf_op jit(solution)/shard_map/all_to_all | solution.py:16
  106.8 0.4 reduce_max.84
  107.6 0.5 slice.18
  108.1 0.6 subtract_add_fusion
  108.7 7.1 %subtract_reduce_fusion.1 = f32[1024]{0:T(1024)S(1)} fusion(f32[1024,4096]{1,0:T(8,128)} %get-tuple-element.9, f32[4096]{0:T(1024)S(1)} %subtract_add_fusion), kind=kLoop, calls=%fused_computation.8 | loop fusion | flops 8387584 | bytes 16797696 | tf_op jit(solution)/shard_map/reduce_max | solution.py:58
  115.8 8.7 %exponential_reduce_fusion.3 = f32[1024]{0:T(1024)S(1)} fusion(f32[1024,4096]{1,0:T(8,128)} %get-tuple-element.9, f32[1024]{0:T(1024)S(1)} %subtract_reduce_fusion.1, f32[4096]{0:T(1024)S(1)} %subtract_add_fusion), kind=kLoop, calls=%fused_computation.4 | loop fusion | flops 12581888 | bytes 16801792 | tf_op jit(solution)/shard_map/reduce_sum | solution.py:59
  124.6 8.9 %fusion.1 = f32[4096]{0:T(1024)S(1)} fusion(f32[1024,4096]{1,0:T(8,128)} %get-tuple-element.9, f32[1024]{0:T(1024)S(1)} %log_add_fusion.5, pred[1024]{0:T(1024)(128)(4,1)S(1)} %fusion.21), kind=kLoop, calls=%fused_computation.11 | loop fusion | flops 16773120 | bytes 16798720 | tf_op jit(solution)/shard_map/reduce_max | solution.py:65
  133.4 8.3 %exponential_reduce_fusion = f32[4096]{0:T(1024)S(1)} fusion(f32[1024,4096]{1,0:T(8,128)} %get-tuple-element.9, f32[4096]{0:T(1024)S(1)} %fusion.1, f32[1024]{0:T(1024)S(1)} %log_add_fusion.5, pred[1024]{0:T(1024)(128)(4,1)S(1)} %fusion.21), kind=kLoop, calls=%fused_computation | loop fusion | flops 20967424 | bytes 16815104 | tf_op jit(solution)/shard_map/reduce_sum | solution.py:66
  141.8 8.5 %all_to_all.55 = f32[8,1,4096]{2,1,0:T(1,128)S(1)} all-to-all(f32[8,1,4096]{2,1,0:T(1,128)S(1)} %broadcast_in_dim.83), channel_id=1, replica_groups=mesh['samp_0'=4,'samp_1'=2,'state_0'=8,'state_1'=4] {'samp_0','samp_1'}, dimensions={0} | all-to-all | bytes 262144 | tf_op jit(solution)/shard_map/all_to_all | solution.py:16
  150.6 0.5 broadcast_in_dim.84
  151.0 22.0 %all_to_all.56 = f32[32,1,4096]{2,1,0:T(1,128)S(1)} all-to-all(f32[32,1,4096]{2,1,0:T(1,128)S(1)} %broadcast_in_dim.84), channel_id=1, replica_groups=mesh['samp_0'=4,'samp_1'=2,'state_0'=8,'state_1'=4] {'state_0','state_1'}, dimensions={0} | all-to-all | bytes 1048576 | tf_op jit(solution)/shard_map/all_to_all | solution.py:16
  173.8 0.5 slice.19
  174.3 0.6 fusion.24
  174.9 7.1 %subtract_reduce_fusion = f32[1024]{0:T(1024)S(1)} fusion(f32[1024,4096]{1,0:T(8,128)} %get-tuple-element.9, f32[4096]{0:T(1024)S(1)} %get-tuple-element.2), kind=kLoop, calls=%fused_computation.7 | loop fusion | flops 8387584 | bytes 16797696 | tf_op jit(solution)/shard_map/reduce_max | solution.py:58
  182.0 8.7 %exponential_reduce_fusion.2 = f32[1024]{0:T(1024)S(1)} fusion(f32[1024,4096]{1,0:T(8,128)} %get-tuple-element.9, f32[1024]{0:T(1024)S(1)} %subtract_reduce_fusion, f32[4096]{0:T(1024)S(1)} %get-tuple-element.2), kind=kLoop, calls=%fused_computation.2 | loop fusion | flops 12581888 | bytes 16801792 | tf_op jit(solution)/shard_map/reduce_sum | solution.py:59
  190.8 0.7 broadcast_in_dim.85
  191.5 4.7 %all-to-all-start.6 = ((f32[32,1,1024]{2,1,0:T(1,128)}), f32[32,1,1024]{2,1,0:T(1,128)S(1)}, u32[]{:S(2)}, u32[]{:S(2)}) async-start(f32[32,1,1024]{2,1,0:T(1,128)} %broadcast_in_dim.85), calls=%async_computation.6 | async-start | bytes 262144 | tf_op jit(solution)/shard_map/all_to_all | solution.py:16
  196.2 0.6 dynamic_slice.11
  196.8 10.0 %all-to-all-done.6 = f32[32,1,1024]{2,1,0:T(1,128)S(1)} async-done(((f32[32,1,1024]{2,1,0:T(1,128)}), f32[32,1,1024]{2,1,0:T(1,128)S(1)}, u32[]{:S(2)}, u32[]{:S(2)}) %all-to-all-start.6) | async-done | bytes 131104 | tf_op jit(solution)/shard_map/all_to_all | solution.py:16
  206.8 0.7 copy.33
  (23 shorter events, 2.1 us)
Async XLA Ops:
  11.5 29.2 %all-to-all-start = ((bf16[32,64,128]{2,1,0:T(8,128)(2,1)}), bf16[32,64,128]{2,1,0:T(8,128)(2,1)S(1)}, u32[]{:S(2)}, u32[]{:S(2)}) async-start(bf16[32,64,128]{2,1,0:T(8,128)(2,1)} %broadcast_in_dim.74), calls=%async_computation | async-start | bytes 1048576 | tf_op jit(solution)/shard_map/all_to_all | solution.py:16
  191.5 15.3 %all-to-all-start.6 = ((f32[32,1,1024]{2,1,0:T(1,128)}), f32[32,1,1024]{2,1,0:T(1,128)S(1)}, u32[]{:S(2)}, u32[]{:S(2)}) async-start(f32[32,1,1024]{2,1,0:T(1,128)} %broadcast_in_dim.85), calls=%async_computation.6 | async-start | bytes 262144 | tf_op jit(solution)/shard_map/all_to_all | solution.py:16

commit v2 on v1

v2 whole, which is shorter than its diff:
```python
import jax
import jax.numpy as jnp
from jax import lax
from jax.experimental import pallas as pl
from jax.experimental.pallas import tpu as pltpu
from jax.sharding import Mesh
from jax.sharding import PartitionSpec as P

BLOCK = 128
LANES = 128
COMP = 64
TILE = 256
DEPTH = 128
CHUNK = 256
STATE = ("state_0", "state_1")
SAMP = ("samp_0", "samp_1")
NEGATIVE = -1e30
BF16 = jnp.bfloat16
F32 = jnp.float32


def exchanged(copies, axes):
    return lax.all_to_all(copies, axes, split_axis=0, concat_axis=0, tiled=True)


def copies_of_each(x, axes):
    return exchanged(jnp.broadcast_to(x, (lax.axis_size(axes), *x.shape)), axes)


def iota(shape, dim):
    return lax.broadcasted_iota(jnp.int32, shape, dim)


def dot_nt(a, b):
    return lax.dot_general(a, b, (((1,), (1,)), ((), ())), preferred_element_type=F32)


def dot(a, b):
    return jnp.dot(a, b, preferred_element_type=F32)


def three_parts(x):
    high = x.astype(BF16).astype(F32)
    rest = x - high
    middle = rest.astype(BF16).astype(F32)
    return high, middle, rest - middle


def log_sum_rows(logs):
    highest = jnp.max(logs, axis=0, keepdims=True)
    return highest + jnp.log(jnp.sum(jnp.exp(logs - highest), axis=0, keepdims=True))


def count_kernel(blocks_ref, place_ref, meta_ref, log_count_ref):
    groups = place_ref.shape[0]
    slots = log_count_ref.shape[0]
    width = blocks_ref.shape[2]
    counts = jnp.zeros((groups, LANES), F32)
    for s in range(blocks_ref.shape[0]):
        window = blocks_ref[s, 0:1, :]
        fill = blocks_ref[s, 1:2, :]
        of_group = jnp.where(iota((groups, width), 0) == window >> 7, fill, 0).astype(F32).astype(BF16)
        of_lane = jnp.where(iota((LANES, width), 0) == (window & 127), 1.0, 0.0).astype(BF16)
        counts = counts + dot_nt(of_group, of_lane)
    flag = jnp.where(counts > 0, 1.0, 0.0)
    packed = flag.astype(BF16)
    before = jnp.where(iota((LANES, LANES), 0) < iota((LANES, LANES), 1), 1.0, 0.0).astype(BF16)
    within = dot(packed, before)
    total = dot(packed, jnp.ones((LANES, LANES), BF16))
    earlier = jnp.where(iota((groups, groups), 1) < iota((groups, groups), 0), 1.0, 0.0).astype(BF16)
    offset = dot(earlier, total.astype(BF16))
    offset_int = offset.astype(jnp.int32)
    within_int = within.astype(jnp.int32)
    counted = counts > 0
    place_ref[...] = jnp.where(counted, (offset_int & 127) + within_int, -1)
    meta_ref[0:groups, :] = offset_int >> 7
    everything = jnp.sum(total, axis=0, keepdims=True).astype(jnp.int32)
    meta_ref[groups : groups + 8, :] = jnp.broadcast_to(everything, (8, LANES))
    whole = jnp.where(counted, offset_int + within_int, -1)
    counts_int = counts.astype(jnp.int32)
    digits = (counts_int >> 14, (counts_int >> 7) & 127, counts_int & 127)
    gathered = jnp.zeros((3 * slots, LANES), F32)
    for t in range(groups):
        row = whole[t : t + 1, :]
        slot = iota((slots, LANES), 0) == row >> 7
        parts = [jnp.where(slot, d[t : t + 1, :], 0).astype(F32) for d in digits]
        of_lane = jnp.where(iota((LANES, LANES), 0) == (row & 127), 1.0, 0.0).astype(BF16)
        gathered = gathered + dot_nt(jnp.concatenate(parts, 0).astype(BF16), of_lane)
    compact = gathered[0:slots] * 16384.0 + gathered[slots : 2 * slots] * 128.0 + gathered[2 * slots :]
    log_count_ref[...] = jnp.where(compact > 0, jnp.log(jnp.maximum(compact, 1.0)), NEGATIVE)


def tail_rows(log_weight):
    row = iota((DEPTH - COMP, TILE), 0)
    rows = jnp.where(row < 3, 1.0, 0.0)
    if log_weight is not None:
        for k, part in enumerate(three_parts(log_weight)):
            rows = jnp.where(row == 3 + k, part, rows)
    return rows.astype(BF16)


def denominator_chunk(c, points_ref, tiles_ref, tiles, energy_ref):
    points = points_ref[pl.ds(c * CHUNK, CHUNK), :]

    def find(j, highest):
        exponents = dot(points, tiles_ref[j])
        energy_ref[j] = exponents
        return jnp.maximum(highest, jnp.maximum(exponents[:, :LANES], exponents[:, LANES:]))

    highest = lax.fori_loop(0, tiles, find, jnp.full((CHUNK, LANES), 4 * NEGATIVE, F32))
    highest = jnp.max(highest, axis=1, keepdims=True)

    def add(j, totals):
        grown = jnp.exp(energy_ref[j] - highest)
        return totals + (grown[:, :LANES] + grown[:, LANES:])

    totals = lax.fori_loop(0, tiles, add, jnp.zeros((CHUNK, LANES), F32))
    return highest + jnp.log(jnp.sum(totals, axis=1, keepdims=True))


def live_points(c, logden, points_ref, live_ref, fill_ref, first_block):
    row = iota((BLOCK, 1), 0)
    alive = [row < fill_ref[first_block + c * (CHUNK // BLOCK) + b] for b in range(CHUNK // BLOCK)]
    shift = [
        jnp.where(a, -logden[b * BLOCK : (b + 1) * BLOCK, :], NEGATIVE) for b, a in enumerate(alive)
    ]
    shift = jnp.concatenate(shift, 0)
    lane = iota((CHUNK, DEPTH), 1)
    points = jnp.where(lane < COMP, points_ref[pl.ds(c * CHUNK, CHUNK), :].astype(F32), 0.0)
    for k, part in enumerate(three_parts(shift)):
        points = jnp.where(lane == COMP + k, part, points)
    live_ref[pl.ds(c * CHUNK, CHUNK), :] = points.astype(BF16)


def state_log_sum(tile, live_ref, exponent_ref):
    rows = live_ref.shape[0]
    highest = None
    for c in range(rows // CHUNK):
        exponents = dot(live_ref[c * CHUNK : (c + 1) * CHUNK, :], tile)
        exponent_ref[c * CHUNK : (c + 1) * CHUNK, :] = exponents
        top = jnp.max(exponents.reshape(CHUNK // 8, 8, TILE), axis=0)
        highest = top if highest is None else jnp.maximum(highest, top)
    highest = jnp.max(highest, axis=0, keepdims=True)
    totals = jnp.zeros((8, TILE), F32)
    for c in range(rows // CHUNK):
        grown = jnp.exp(exponent_ref[c * CHUNK : (c + 1) * CHUNK, :] - highest)
        totals = totals + jnp.sum(grown.reshape(CHUNK // 8, 8, TILE), axis=0)
    return highest + jnp.log(jnp.sum(totals, axis=0, keepdims=True))


def first_kernel(
    meta_ref, fill_ref, gathered_ref, components_ref, place_ref, log_count_ref,
    logs_ref, tiles_ref, points_ref,
    packed_ref, energy_ref, live_ref, exponent_ref,
):
    groups = gathered_ref.shape[0]
    rows = points_ref.shape[0]
    tiles = (meta_ref[groups] + TILE - 1) // TILE
    packed_ref[...] = jnp.zeros(packed_ref.shape, F32)
    for t in range(groups):
        chosen = jnp.where(iota((2 * LANES, LANES), 0) == place_ref[t : t + 1, :], 1.0, 0.0).astype(BF16)
        moved = dot_nt(gathered_ref[t], chosen)
        at = meta_ref[t]
        packed_ref[at] += moved[:, :LANES]
        packed_ref[at + 1] += moved[:, LANES:]
    for j in range(tiles_ref.shape[0]):
        tiles_ref[j, 0:COMP, :] = jnp.concatenate([packed_ref[2 * j], packed_ref[2 * j + 1]], 1).astype(BF16)
        weight = jnp.concatenate([log_count_ref[2 * j : 2 * j + 1, :], log_count_ref[2 * j + 1 : 2 * j + 2, :]], 1)
        tiles_ref[j, COMP:DEPTH, :] = tail_rows(weight)
    lane = iota((LANES, DEPTH - COMP), 1)
    ones = jnp.where((lane >= 3) & (lane < 6), 1.0, 0.0)
    for b in range(rows // LANES):
        turned = -components_ref[:, b * LANES : (b + 1) * LANES].astype(F32).T
        points_ref[b * LANES : (b + 1) * LANES, :] = jnp.concatenate([turned, ones], 1).astype(BF16)
    first_block = meta_ref[groups + 1] * (rows // BLOCK)
    for c in range(rows // CHUNK):
        logden = denominator_chunk(c, points_ref, tiles_ref, tiles, energy_ref)
        live_points(c, logden, points_ref, live_ref, fill_ref, first_block)
    logs_ref[...] = jnp.zeros(logs_ref.shape, F32)

    def one(j, carry):
        logs = state_log_sum(tiles_ref[j], live_ref, exponent_ref)
        logs_ref[:, pl.ds(pl.multiple_of(j * TILE, TILE), TILE)] = jnp.broadcast_to(logs, (8, TILE))
        return carry

    lax.fori_loop(0, tiles, one, 0)


def second_kernel(
    meta_ref, fill_ref, logs_in_ref, gathered_ref, tiles_in_ref, points_ref, log_count_ref,
    logs_ref,
    tiles_ref, energy_ref, live_ref, exponent_ref,
):
    groups = gathered_ref.shape[0]
    rows = points_ref.shape[0]
    tiles = (meta_ref[groups] + TILE - 1) // TILE
    slots = tiles_ref.shape[0] * TILE
    weighted_tiles(logs_in_ref, tiles_in_ref, log_count_ref, tiles_ref, None)
    first_block = meta_ref[groups + 1] * (rows // BLOCK)
    for c in range(rows // CHUNK):
        logden = denominator_chunk(c, points_ref, tiles_ref, tiles, energy_ref)
        live_points(c, logden, points_ref, live_ref, fill_ref, first_block)
    logs_ref[:, 0:slots] = jnp.zeros((8, slots), F32)

    def one(j, carry):
        logs = state_log_sum(tiles_ref[j], live_ref, exponent_ref)
        logs_ref[:, pl.ds(pl.multiple_of(j * TILE, TILE), TILE)] = jnp.broadcast_to(logs, (8, TILE))
        return carry

    lax.fori_loop(0, tiles, one, 0)
    tail = tail_rows(None)

    def every(t, carry):
        head = jnp.concatenate([gathered_ref[2 * t], gathered_ref[2 * t + 1]], 1)
        logs = state_log_sum(jnp.concatenate([head, tail], 0), live_ref, exponent_ref)
        logs_ref[:, pl.ds(pl.multiple_of(slots + t * TILE, TILE), TILE)] = jnp.broadcast_to(logs, (8, TILE))
        return carry

    lax.fori_loop(0, groups * LANES // TILE, every, 0)


def weighted_tiles(logs_in_ref, tiles_in_ref, log_count_ref, tiles_ref, base):
    for j in range(tiles_ref.shape[0]):
        free = -log_sum_rows(logs_in_ref[:, j * TILE : (j + 1) * TILE])
        if base is not None:
            free = free + base
        weight = jnp.concatenate([log_count_ref[2 * j : 2 * j + 1, :], log_count_ref[2 * j + 1 : 2 * j + 2, :]], 1)
        tiles_ref[j, 0:COMP, :] = tiles_in_ref[j, 0:COMP, :]
        tiles_ref[j, COMP:DEPTH, :] = tail_rows(weight + free)


def third_kernel(
    meta_ref, logs_in_ref, tiles_in_ref, points_ref, log_count_ref,
    free_ref, logden_ref,
    tiles_ref, energy_ref,
):
    copies, rows = logden_ref.shape
    slots = tiles_ref.shape[0] * TILE
    tiles = (meta_ref[copies] + TILE - 1) // TILE
    base = log_sum_rows(logs_in_ref[:, slots + LANES : slots + 2 * LANES])[:, 0:1]
    own = log_sum_rows(logs_in_ref[:, slots : slots + LANES])
    free_ref[...] = jnp.broadcast_to(base - own, free_ref.shape)
    weighted_tiles(logs_in_ref, tiles_in_ref, log_count_ref, tiles_ref, base)
    for c in range(rows // CHUNK):
        logden = denominator_chunk(c, points_ref, tiles_ref, tiles, energy_ref)
        for b in range(CHUNK // LANES):
            turned = jnp.broadcast_to(logden[b * LANES : (b + 1) * LANES, :], (LANES, LANES)).T
            at = c * CHUNK + b * LANES
            logden_ref[:, at : at + LANES] = turned[0:copies, :]


def merge_kernel(logs_ref, copies_ref):
    for j in range(logs_ref.shape[1] // TILE):
        logs = log_sum_rows(logs_ref[:, j * TILE : (j + 1) * TILE])
        copies_ref[:, j * TILE : (j + 1) * TILE] = jnp.broadcast_to(logs, (copies_ref.shape[0], TILE))


def merge_last_kernel(logs_ref, copies_ref):
    copies = copies_ref.shape[0]
    slots = copies_ref.shape[1] - 2 * LANES
    for j in range(slots // TILE):
        logs = log_sum_rows(logs_ref[:, j * TILE : (j + 1) * TILE])
        copies_ref[:, j * TILE : (j + 1) * TILE] = jnp.broadcast_to(logs, (copies, TILE))
    for t in range(copies):
        at = slots + t * LANES
        logs = log_sum_rows(logs_ref[:, at : at + LANES])
        copies_ref[t : t + 1, slots : slots + LANES] = logs
        if t == 0:
            copies_ref[:, slots + LANES :] = jnp.broadcast_to(logs, (copies, LANES))


def shards(components, coefficients, block_window, block_fill):
    groups = lax.axis_size(STATE)
    samps = lax.axis_size(SAMP)
    position = lax.axis_index(STATE)
    rows = components.shape[1] // groups
    slots = min(samps * block_window.shape[0], groups * LANES)
    slot_rows = slots // LANES
    tile_count = slots // TILE
    shape = jax.ShapeDtypeStruct
    vmem = pl.BlockSpec(memory_space=pltpu.VMEM)
    smem = pl.BlockSpec(memory_space=pltpu.SMEM)
    params = pltpu.CompilerParams(vmem_limit_bytes=50 << 20)

    blocks = copies_of_each(jnp.stack([block_window, block_fill]), SAMP)
    gathered = copies_of_each(coefficients, STATE)
    place, meta, log_count = pl.pallas_call(
        count_kernel,
        out_shape=(
            shape((groups, LANES), jnp.int32), shape((groups + 8, LANES), jnp.int32), shape((slot_rows, LANES), F32),
        ),
        in_specs=[vmem], out_specs=(vmem, vmem, vmem), compiler_params=params, name="count",
    )(blocks)
    meta = jnp.concatenate([meta[: groups + 1, 0], position.astype(jnp.int32)[None]])

    work = [
        pltpu.VMEM((tile_count, CHUNK, TILE), F32), pltpu.VMEM((rows, DEPTH), BF16), pltpu.VMEM((rows, TILE), F32),
    ]
    full = lambda dims: pl.BlockSpec(dims, lambda i, m, f: (0,) * len(dims))
    logs, tiles, points = pl.pallas_call(
        first_kernel,
        out_shape=(shape((samps, slots), F32), shape((tile_count, DEPTH, TILE), BF16), shape((rows, DEPTH), BF16)),
        grid_spec=pltpu.PrefetchScalarGridSpec(
            num_scalar_prefetch=2, grid=(1,),
            in_specs=[
                full(gathered.shape), pl.BlockSpec((COMP, rows), lambda i, m, f: (0, m[groups + 1])),
                full(place.shape), full(log_count.shape),
            ],
            out_specs=(full((samps, slots)), full((tile_count, DEPTH, TILE)), full((rows, DEPTH))),
            scratch_shapes=[pltpu.VMEM((slot_rows + 2, COMP, LANES), F32), *work],
        ),
        compiler_params=params, name="first",
    )(meta, block_fill, gathered, components, place, log_count)
    logs = exchanged(logs, SAMP)
    logs = pl.pallas_call(
        merge_kernel, out_shape=shape((groups, slots), F32), in_specs=[vmem], out_specs=vmem, name="merge",
    )(logs)
    logs = exchanged(logs, STATE)
    logs = pl.pallas_call(
        second_kernel,
        out_shape=shape((samps, slots + groups * LANES), F32),
        in_specs=[smem, smem, vmem, vmem, vmem, vmem, vmem], out_specs=vmem,
        scratch_shapes=[pltpu.VMEM((tile_count, DEPTH, TILE), BF16), *work],
        compiler_params=params, name="second",
    )(meta, block_fill, logs, gathered, tiles, points, log_count)
    logs = exchanged(logs, SAMP)
    logs = pl.pallas_call(
        merge_last_kernel, out_shape=shape((groups, slots + 2 * LANES), F32), in_specs=[vmem], out_specs=vmem,
        name="merge_last",
    )(logs)
    logs = exchanged(logs, STATE)
    free, logden = pl.pallas_call(
        third_kernel,
        out_shape=(shape((8, LANES), F32), shape((groups, rows), F32)),
        in_specs=[smem, vmem, vmem, vmem, vmem], out_specs=(vmem, vmem),
        scratch_shapes=[pltpu.VMEM((tile_count, DEPTH, TILE), BF16), pltpu.VMEM((tile_count, CHUNK, TILE), F32)],
        compiler_params=params, name="third",
    )(meta, logs, tiles, points, log_count)
    return free[0], exchanged(logden, STATE).reshape(-1)


def solution(mesh):
    torus = Mesh(mesh.devices.reshape(4, 2, 8, 4), ("samp_0", "samp_1", "state_0", "state_1"))
    placed = (P(None, SAMP), P(None, STATE), P(SAMP), P(SAMP))
    return jax.shard_map(
        shards, mesh=torus, in_specs=placed, out_specs=(P(STATE), P(SAMP)), check_vma=False
    )
```

time: 208 us -> 143 us (0.69)
  other arithmetic: 78.6 us -> 0.78 us
  Pallas kernels: 0 us -> 30.9 us
  blocking collectives: 69.5 us -> 59.7 us
  matrix products: 9.3 us -> 0 us
  local copies, waits for them, and re-layouts: 6.48 us -> 8.66 us
    reduce_sum x9 -> x0, other arithmetic: 43.6 us -> none  [the longest x3 26.1 us: local_denominator(): jnp.sum(jnp.exp(exponents - highest[None, :]), axis=0)]
    reduce_max x8 -> x0, other arithmetic: 32.9 us -> none  [the longest x2 17.8 us: shards(): highest = jnp.max(exponents, axis=1)]
    pallas_call x0 -> x6, Pallas kernels: none -> 30.9 us  [the longest x1 13.6 us: shards(): pl.pallas_call(second_kernel, out_shape=shape((samps, slots + groups * LA...]
    all_to_all x5, blocking collectives: 69.5 us -> 59.7 us  [exchanged(): return lax.all_to_all(copies, axes, split_axis=0, concat_axis=0, tiled=True)]
    dot_general x2 -> x0, matrix products: 9.3 us -> none  [the longest x1 8.99 us: shards(): lax.dot_general(laid_out(gathered, 1), component_rows, (((0,), (0,)), (()...]
    all_to_all x0 -> x5, local copies, waits for them, and re-layouts: none -> 3.56 us  [exchanged(): return lax.all_to_all(copies, axes, split_axis=0, concat_axis=0, tiled=True)]
    unnamed x1 -> x9, local copies, waits for them, and re-layouts: 0.66 us -> 2.84 us
  transfers between devices with their start and end apart: 2 -> 2, of which waited for: 2 -> 2; matrix products, arithmetic and copies ran while one was open for 1% -> 0% of each run, Pallas kernels for 0% -> 1%
where the time goes in v2:
time: 143 us
  blocking collectives  59.7 us (42%)
  Pallas kernels  30.9 us (22%)
  waiting for transfers between devices  26.1 us (18%)
  starting transfers between devices  15.8 us (11%)
  local copies, waits for them, and re-layouts  8.66 us (6%)
    all_to_all x5, blocking collectives, exchanged(): return lax.all_to_all(copies, axes, split_axis=0, concat_axis=0, tiled=True)  59.7 us
    all_to_all x2, waiting for transfers between devices, exchanged(): return lax.all_to_all(copies, axes, split_axis=0, concat_axis=0, tiled=True)  26.1 us
    all_to_all x2, starting transfers between devices, exchanged(): return lax.all_to_all(copies, axes, split_axis=0, concat_axis=0, tiled=True)  15.8 us
    pallas_call x1, Pallas kernels, shards(): pl.pallas_call(second_kernel, out_shape=shape((samps, slots + groups * LA...  13.6 us
    pallas_call x1, Pallas kernels, shards(): pl.pallas_call(first_kernel, out_shape=(shape((samps, slots), F32), shape...  8 us
    pallas_call x1, Pallas kernels, shards(): pl.pallas_call(third_kernel, out_shape=(shape((8, LANES), F32), shape((gr...  4.46 us
    all_to_all x5, local copies, waits for them, and re-layouts, exchanged(): return lax.all_to_all(copies, axes, split_axis=0, concat_axis=0, tiled=True)  3.56 us
  transfers between devices with their start and end apart: 2, of which 2 were waited for; matrix products, arithmetic and copies ran while one was open for 0% of the time, Pallas kernels for 1%

profile of v2, /device:TPU:2, one launch (start us, length us, event | category | flops | bytes accessed | tf_op | source)
XLA Modules:
  0.0 142.6 jit_solution(3015405202762329816)
XLA Ops:
  0.6 0.7 pad_add_fusion
  1.3 8.5 %all_to_all.63.blocks_ref = s32[8,2,256]{2,1,0:T(2,128)S(1)} all-to-all(s32[8,2,256]{2,1,0:T(2,128)S(1)} %broadcast_in_dim.9), channel_id=1, replica_groups=mesh['samp_0'=4,'samp_1'=2,'state_0'=8,'state_1'=4] {'samp_0','samp_1'}, dimensions={0} | all-to-all | bytes 32768 | tf_op jit(solution)/shard_map/all_to_all | solution.py:23
  9.9 1.6 %broadcast_in_dim.11 = bf16[32,64,128]{2,1,0:T(8,128)(2,1)} broadcast(bf16[64,128]{1,0:T(8,128)(2,1)} %param.5), dimensions={1,2} | broadcast | bytes 540672 | tf_op jit(solution)/shard_map/broadcast_in_dim | solution.py:27
  11.5 0.0 copy-start.1
  11.5 11.6 %all-to-all-start.1 = ((bf16[32,64,128]{2,1,0:T(8,128)(2,1)}), bf16[32,64,128]{2,1,0:T(8,128)(2,1)S(1)}, u32[]{:S(2)}, u32[]{:S(2)}) async-start(bf16[32,64,128]{2,1,0:T(8,128)(2,1)} %broadcast_in_dim.11), calls=%async_computation.1 | async-start | bytes 1048576 | tf_op jit(solution)/shard_map/all_to_all | solution.py:23
  23.1 1.6 %count.1 = (s32[32,128]{1,0:T(8,128)S(1)}, s32[40,128]{1,0:T(8,128)S(1)}, f32[16,128]{1,0:T(8,128)S(1)}) custom-call(s32[8,2,256]{2,1,0:T(2,128)S(1)} %all_to_all.63.blocks_ref), custom_call_target="tpu_custom_call" | custom-call | tf_op jit(solution)/shard_map/count/pallas_call | solution.py:287
  24.7 0.1 slice_reduce_fusion
  24.8 0.1 pad_add_fusion.1.meta_ref
  24.9 15.9 %all-to-all-done.1.gathered_ref = bf16[32,64,128]{2,1,0:T(8,128)(2,1)S(1)} async-done(((bf16[32,64,128]{2,1,0:T(8,128)(2,1)}), bf16[32,64,128]{2,1,0:T(8,128)(2,1)S(1)}, u32[]{:S(2)}, u32[]{:S(2)}) %all-to-all-start.1) | async-done | bytes 524320 | tf_op jit(solution)/shard_map/all_to_all | solution.py:23
  40.8 0.7 copy-done
  41.5 8.0 %first.1 = (f32[8,2048]{1,0:T(8,128)S(1)}, bf16[8,128,256]{2,1,0:T(8,128)(2,1)S(1)}, bf16[1024,128]{1,0:T(8,128)(2,1)S(1)}) custom-call(s32[34]{0:T(128)S(1)} %pad_add_fusion.1.meta_ref, s32[256]{0:T(256)S(1)} %copy-done, bf16[32,64,128]{2,1,0:T(8,128)(2,1)S(1)} %all-to-all-done.1.gathered_ref, bf16[64,32768]{1,0:T(8,128)(2,1)} %components_ref.1, ...), custom_call_target="tpu_custom_call" | custom-call | tf_op jit(solution)/shard_map/first/pallas_call | solution.py:300
  49.5 0.1 copy.6
  49.6 8.0 %all_to_all.64 = f32[8,1,2048]{2,1,0:T(1,128)S(1)} all-to-all(f32[8,1,2048]{2,1,0:T(1,128)S(1)} %copy.6), channel_id=1, replica_groups=mesh['samp_0'=4,'samp_1'=2,'state_0'=8,'state_1'=4] {'samp_0','samp_1'}, dimensions={0} | all-to-all | bytes 131072 | tf_op jit(solution)/shard_map/all_to_all | solution.py:23
  57.6 0.7 copy.22
  58.2 1.6 %merge.1 = f32[32,2048]{1,0:T(8,128)} custom-call(f32[8,2048]{1,0:T(8,128)} %bitcast.33), custom_call_target="tpu_custom_call" | custom-call | tf_op jit(solution)/shard_map/merge/pallas_call | solution.py:315
  59.8 1.2 copy.7
  61.1 17.0 %all_to_all.65 = f32[32,1,2048]{2,1,0:T(1,128)S(1)} all-to-all(f32[32,1,2048]{2,1,0:T(1,128)S(1)} %copy.7), channel_id=1, replica_groups=mesh['samp_0'=4,'samp_1'=2,'state_0'=8,'state_1'=4] {'state_0','state_1'}, dimensions={0} | all-to-all | bytes 524288 | tf_op jit(solution)/shard_map/all_to_all | solution.py:23
  78.1 0.1 copy.20
  78.2 0.0 copy-done.1
  78.2 13.6 %second.1 = f32[8,6144]{1,0:T(8,128)S(1)} custom-call(s32[34]{0:T(128)S(1)} %pad_add_fusion.1.meta_ref, s32[256]{0:T(256)S(1)} %copy-done.1, f32[32,2048]{1,0:T(8,128)S(1)} %bitcast.24, bf16[32,64,128]{2,1,0:T(8,128)(2,1)S(1)} %all-to-all-done.1.gathered_ref, bf16[8,128,256]{2,1,0:T(8,128)(2,1)S(1)} %get-tuple-element.14.tiles_in_ref, ...), custom_call_target="tpu_custom_call" | custom-call | tf_op jit(solution)/shard_map/second/pallas_call | solution.py:319
  91.7 0.2 copy.8
  92.0 9.2 %all_to_all.66 = f32[8,1,6144]{2,1,0:T(1,128)S(1)} all-to-all(f32[8,1,6144]{2,1,0:T(1,128)S(1)} %copy.8), channel_id=1, replica_groups=mesh['samp_0'=4,'samp_1'=2,'state_0'=8,'state_1'=4] {'samp_0','samp_1'}, dimensions={0} | all-to-all | bytes 393216 | tf_op jit(solution)/shard_map/all_to_all | solution.py:23
  101.2 0.7 copy.21
  101.9 1.8 %merge_last.1 = f32[32,2304]{1,0:T(8,128)} custom-call(f32[8,6144]{1,0:T(8,128)} %bitcast.31), custom_call_target="tpu_custom_call" | custom-call | tf_op jit(solution)/shard_map/merge_last/pallas_call | solution.py:327
  103.7 1.3 copy.9
  104.9 17.0 %all_to_all.67 = f32[32,1,2304]{2,1,0:T(1,128)S(1)} all-to-all(f32[32,1,2304]{2,1,0:T(1,128)S(1)} %copy.9), channel_id=1, replica_groups=mesh['samp_0'=4,'samp_1'=2,'state_0'=8,'state_1'=4] {'state_0','state_1'}, dimensions={0} | all-to-all | bytes 589824 | tf_op jit(solution)/shard_map/all_to_all | solution.py:23
  121.9 4.5 %third.1 = (f32[8,128]{1,0:T(8,128)S(1)}, f32[32,1024]{1,0:T(8,128)S(1)}) custom-call(s32[34]{0:T(128)S(1)} %pad_add_fusion.1.meta_ref, f32[32,2304]{1,0:T(8,128)S(1)} %bitcast.23, bf16[8,128,256]{2,1,0:T(8,128)(2,1)S(1)} %get-tuple-element.14.tiles_in_ref, bf16[1024,128]{1,0:T(8,128)(2,1)S(1)} %get-tuple-element.15.points_ref, ...), custom_call_target="tpu_custom_call" | custom-call | tf_op jit(solution)/shard_map/third/pallas_call | solution.py:332
  126.4 0.8 copy.10
  127.2 4.1 %all-to-all-start.6 = ((f32[32,1,1024]{2,1,0:T(1,128)}), f32[32,1,1024]{2,1,0:T(1,128)S(1)}, u32[]{:S(2)}, u32[]{:S(2)}) async-start(f32[32,1,1024]{2,1,0:T(1,128)} %copy.10), calls=%async_computation.6 | async-start | bytes 262144 | tf_op jit(solution)/shard_map/all_to_all | solution.py:23
  131.3 0.5 slice_bitcast_fusion
  131.8 10.1 %all-to-all-done.6 = f32[32,1,1024]{2,1,0:T(1,128)S(1)} async-done(((f32[32,1,1024]{2,1,0:T(1,128)}), f32[32,1,1024]{2,1,0:T(1,128)S(1)}, u32[]{:S(2)}, u32[]{:S(2)}) %all-to-all-start.6) | async-done | bytes 131104 | tf_op jit(solution)/shard_map/all_to_all | solution.py:23
  142.0 0.7 copy.24
  (3 shorter events, 0.0 us)
Async XLA Ops:
  11.5 66.7 %copy-start.1 = (s32[256]{0:T(256)S(1)}, s32[256]{0:T(256)}, u32[]{:S(2)}) copy-start(s32[256]{0:T(256)} %fill_ref.3) | copy-start | bytes 3076
  11.5 29.3 %all-to-all-start.1 = ((bf16[32,64,128]{2,1,0:T(8,128)(2,1)}), bf16[32,64,128]{2,1,0:T(8,128)(2,1)S(1)}, u32[]{:S(2)}, u32[]{:S(2)}) async-start(bf16[32,64,128]{2,1,0:T(8,128)(2,1)} %broadcast_in_dim.11), calls=%async_computation.1 | async-start | bytes 1048576 | tf_op jit(solution)/shard_map/all_to_all | solution.py:23
  40.8 0.7 copy-start
  127.2 14.8 %all-to-all-start.6 = ((f32[32,1,1024]{2,1,0:T(1,128)}), f32[32,1,1024]{2,1,0:T(1,128)S(1)}, u32[]{:S(2)}, u32[]{:S(2)}) async-start(f32[32,1,1024]{2,1,0:T(1,128)} %copy.10), calls=%async_computation.6 | async-start | bytes 262144 | tf_op jit(solution)/shard_map/all_to_all | solution.py:23

commit v3 on v1

v3 whole, which is shorter than its diff:
```python
import functools

import jax
import jax.numpy as jnp
from jax import lax
from jax.experimental import pallas as pl
from jax.experimental.pallas import tpu as pltpu
from jax.sharding import Mesh
from jax.sharding import PartitionSpec as P


BLOCK = 128
LANES = 128
COMP = 64
TILE = 256
DEPTH = 128
CHUNK = 256
TAIL = 16
LEAST = 1e-25
SPREAD = 50.0
STATE = ("state_0", "state_1")
SAMP = ("samp_0", "samp_1")
NEGATIVE = -1e30
BF16 = jnp.bfloat16
F32 = jnp.float32


def exchanged(copies, axes):
    return lax.all_to_all(copies, axes, split_axis=0, concat_axis=0, tiled=True)


def copies_of_each(x, axes):
    return exchanged(jnp.broadcast_to(x, (lax.axis_size(axes), *x.shape)), axes)


def iota(shape, dim):
    return lax.broadcasted_iota(jnp.int32, shape, dim)


def dot_nt(a, b):
    return lax.dot_general(a, b, (((1,), (1,)), ((), ())), preferred_element_type=F32)


def dot(a, b):
    return jnp.dot(a, b, preferred_element_type=F32)


def three_parts(x):
    high = x.astype(BF16).astype(F32)
    rest = x - high
    middle = rest.astype(BF16).astype(F32)
    return high, middle, rest - middle


def log_sum(logs):
    highest = jnp.max(logs, axis=0)
    return highest + jnp.log(jnp.sum(jnp.exp(logs - highest[None]), axis=0))


def log_sum_pieces(logs_ref):
    pieces = logs_ref.shape[0]
    highest = functools.reduce(jnp.maximum, [logs_ref[p] for p in range(pieces)])
    totals = functools.reduce(jnp.add, [jnp.exp(logs_ref[p] - highest) for p in range(pieces)])
    return highest + jnp.log(totals)


def chunk(c):
    return pl.ds(c * CHUNK, CHUNK)


def halves(combine, x):
    return combine(x[:, :LANES], x[:, LANES:])


def count_kernel(
    spot_ref, blocks_ref, components_ref, place_ref, meta_ref, log_count_ref, points_ref,
):
    groups = place_ref.shape[0]
    slots = log_count_ref.shape[0]
    rows = points_ref.shape[0]
    width = blocks_ref.shape[2]
    counts = jnp.zeros((groups, LANES), F32)
    for s in range(blocks_ref.shape[0]):
        window = blocks_ref[s, 0:1, :]
        fill = blocks_ref[s, 1:2, :]
        of_group = jnp.where(iota((groups, width), 0) == window >> 7, fill, 0).astype(F32).astype(BF16)
        of_lane = jnp.where(iota((LANES, width), 0) == (window & 127), 1.0, 0.0).astype(BF16)
        counts = counts + dot_nt(of_group, of_lane)
    counted = counts > 0
    packed = jnp.where(counted, 1.0, 0.0).astype(BF16)
    before = jnp.where(iota((LANES, LANES), 0) < iota((LANES, LANES), 1), 1.0, 0.0).astype(BF16)
    within = dot(packed, before)
    total = dot(packed, jnp.ones((LANES, LANES), BF16))
    earlier = jnp.where(iota((groups, groups), 1) < iota((groups, groups), 0), 1.0, 0.0).astype(BF16)
    offset_int = dot(earlier, total.astype(BF16)).astype(jnp.int32)
    within_int = within.astype(jnp.int32)
    place_ref[...] = jnp.where(counted, (offset_int & 127) + within_int, -1)
    meta_ref[0:groups, :] = offset_int >> 7
    everything = jnp.sum(total, axis=0, keepdims=True).astype(jnp.int32)
    meta_ref[groups : groups + 8, :] = jnp.broadcast_to(everything, (8, LANES))
    whole = jnp.where(counted, offset_int + within_int, -1)
    counts_int = counts.astype(jnp.int32)
    digits = (counts_int >> 14, (counts_int >> 7) & 127, counts_int & 127)
    gathered = jnp.zeros((3 * slots, LANES), F32)
    for t in range(groups):
        row = whole[t : t + 1, :]
        slot = iota((slots, LANES), 0) == row >> 7
        parts = [jnp.where(slot, d[t : t + 1, :], 0).astype(F32) for d in digits]
        of_lane = jnp.where(iota((LANES, LANES), 0) == (row & 127), 1.0, 0.0).astype(BF16)
        gathered = gathered + dot_nt(jnp.concatenate(parts, 0).astype(BF16), of_lane)
    compact = gathered[0:slots] * 16384.0 + gathered[slots : 2 * slots] * 128.0 + gathered[2 * slots :]
    log_count_ref[...] = jnp.where(compact > 0, jnp.log(jnp.maximum(compact, 1.0)), NEGATIVE)
    half = COMP // 2
    own = pl.multiple_of(spot_ref[1] * half, half)
    lane = iota((LANES, DEPTH - COMP), 1)
    ones = jnp.where((lane >= 3) & (lane < 6), 1.0, 0.0)
    for b in range(rows // LANES):
        at = slice(b * LANES, (b + 1) * LANES)
        mine = components_ref[pl.ds(own, half), at].astype(F32)
        other = components_ref[pl.ds(pl.multiple_of(half - own, half), half), at].astype(F32)
        turned = -jnp.concatenate([mine, other], 0).T
        points_ref[at, :] = jnp.concatenate([turned, ones], 1).astype(BF16)


def tail_rows(weight):
    row = iota((TAIL, TILE), 0)
    rows = jnp.where(row < 3, 1.0, 0.0)
    if weight is not None:
        for k, part in enumerate(three_parts(weight)):
            rows = jnp.where(row == 3 + k, part, rows)
    return rows.astype(BF16)


def with_shift(points, shift):
    lane = iota(points.shape, 1)
    for k, part in enumerate(three_parts(shift)):
        points = jnp.where(lane == COMP + k, part, points)
    return points


def tile_row(rows, j):
    return jnp.concatenate([rows[2 * j : 2 * j + 1, :], rows[2 * j + 1 : 2 * j + 2, :]], 1)


def find_denominators(points_ref, tiles_ref, pairs, energy_ref, highest_ref, totals_ref):
    rows = points_ref.shape[0]
    highest_ref[...] = jnp.full(highest_ref.shape, 4 * NEGATIVE, F32)
    totals_ref[...] = jnp.zeros(totals_ref.shape, F32)

    def find(i, carry):
        for c in range(rows // CHUNK):
            top = highest_ref[chunk(c), :]
            for k in range(2):
                exponents = dot(points_ref[chunk(c), :], tiles_ref[2 * i + k])
                energy_ref[2 * i + k, chunk(c), :] = exponents
                top = jnp.maximum(top, halves(jnp.maximum, exponents))
            highest_ref[chunk(c), :] = top
        return carry

    lax.fori_loop(0, pairs, find, 0)
    for c in range(rows // CHUNK):
        top = jnp.max(highest_ref[chunk(c), :], axis=1, keepdims=True)
        highest_ref[chunk(c), :] = jnp.broadcast_to(top, (CHUNK, LANES))

    def add(i, carry):
        for c in range(rows // CHUNK):
            top = highest_ref[chunk(c), :]
            top = jnp.concatenate([top, top], 1)
            sums = totals_ref[chunk(c), :]
            for k in range(2):
                sums = sums + halves(jnp.add, jnp.exp(energy_ref[2 * i + k, chunk(c), :] - top))
            totals_ref[chunk(c), :] = sums
        return carry

    lax.fori_loop(0, pairs, add, 0)
    for c in range(rows // CHUNK):
        sums = jnp.sum(totals_ref[chunk(c), :], axis=1, keepdims=True)
        logden = highest_ref[chunk(c), :][:, 0:1] + jnp.log(sums)
        totals_ref[chunk(c), :] = jnp.broadcast_to(logden, (CHUNK, LANES))


def denominators_near(base_ref, anchored_ref, tiles_ref, pairs, totals_ref):
    rows = anchored_ref.shape[0]
    totals_ref[...] = jnp.zeros(totals_ref.shape, F32)

    def add(i, carry):
        for c in range(rows // CHUNK):
            sums = totals_ref[chunk(c), :]
            for k in range(2):
                sums = sums + halves(jnp.add, jnp.exp(dot(anchored_ref[chunk(c), :], tiles_ref[2 * i + k])))
            totals_ref[chunk(c), :] = sums
        return carry

    lax.fori_loop(0, pairs, add, 0)
    for c in range(rows // CHUNK):
        sums = jnp.sum(totals_ref[chunk(c), :], axis=1, keepdims=True)
        logden = base_ref[chunk(c), :][:, 0:1] + jnp.log(sums)
        totals_ref[chunk(c), :] = jnp.broadcast_to(logden, (CHUNK, LANES))


def put_live(points_ref, totals_ref, live_ref, fill_ref, first_block, anchored_ref=None):
    row = iota((BLOCK, LANES), 0)
    for b in range(points_ref.shape[0] // BLOCK):
        at = pl.ds(b * BLOCK, BLOCK)
        points = points_ref[at, :].astype(F32)
        logden = totals_ref[at, :]
        if anchored_ref is not None:
            anchored_ref[at, :] = with_shift(points, -logden).astype(BF16)
        shift = jnp.where(row < fill_ref[first_block + b], -logden, NEGATIVE)
        live_ref[at, :] = with_shift(points, shift).astype(BF16)


def exponents_and_highest(tile, live_ref, exponent_ref):
    highest = None
    for c in range(live_ref.shape[0] // CHUNK):
        exponents = dot(live_ref[chunk(c), :], tile)
        exponent_ref[chunk(c), :] = exponents
        top = jnp.max(exponents.reshape(CHUNK // 8, 8, TILE), axis=0)
        highest = top if highest is None else jnp.maximum(highest, top)
    return jnp.max(highest, axis=0, keepdims=True)


def log_of_sum(highest, exponent_ref):
    totals = jnp.zeros((8, TILE), F32)
    for c in range(exponent_ref.shape[0] // CHUNK):
        grown = jnp.exp(exponent_ref[chunk(c), :] - highest)
        totals = totals + jnp.sum(grown.reshape(CHUNK // 8, 8, TILE), axis=0)
    return highest + jnp.log(jnp.sum(totals, axis=0, keepdims=True))


def put_rows(logs_ref, first, logs):
    logs_ref[pl.ds(first, 1), :] = logs[:, :LANES]
    logs_ref[pl.ds(first + 1, 1), :] = logs[:, LANES:]


def counted_log_sums(total, weight_ref, tiles_ref, pairs, live_ref, exponent_ref, logs_ref, low_ref):
    low_ref[...] = jnp.zeros(low_ref.shape, F32)
    logs_ref[0 : weight_ref.shape[0], :] = jnp.zeros(weight_ref.shape, F32)

    def finish(j, logs):
        weight = jnp.concatenate([weight_ref[pl.ds(2 * j, 1), :], weight_ref[pl.ds(2 * j + 1, 1), :]], 1)
        valid = iota((1, TILE), 1) < total - j * TILE
        put_rows(logs_ref, 2 * j, jnp.where(valid, logs - weight, 0.0))
        return valid

    def one(i, carry):
        for k in range(2):
            j = 2 * i + k
            totals = jnp.zeros((8, TILE), F32)
            for c in range(live_ref.shape[0] // CHUNK):
                grown = jnp.exp(dot(live_ref[chunk(c), :], tiles_ref[j]))
                totals = totals + jnp.sum(grown.reshape(CHUNK // 8, 8, TILE), axis=0)
            totals = jnp.sum(totals, axis=0, keepdims=True)
            valid = finish(j, jnp.log(totals))
            low_ref[0:1, :] = jnp.maximum(low_ref[0:1, :], jnp.where(valid & (totals < LEAST), 1.0, 0.0))
        return carry

    lax.fori_loop(0, pairs, one, 0)

    @pl.when(jnp.max(low_ref[...]) > 0)
    def _():
        def again(j, carry):
            highest = exponents_and_highest(tiles_ref[j], live_ref, exponent_ref)
            finish(j, log_of_sum(highest, exponent_ref))
            return carry

        lax.fori_loop(0, 2 * pairs, again, 0)


def weighted_tiles(total, logs, log_count_ref, tiles_in_ref, tiles_ref, weight_ref):
    valid = iota(logs.shape, 0) * LANES + iota(logs.shape, 1) < total
    free = jnp.where(valid, -logs, 4 * NEGATIVE)
    highest = jnp.max(jnp.max(free, axis=0, keepdims=True), axis=1, keepdims=True)
    free = jnp.where(valid, free - highest, 0.0)
    weight = log_count_ref[...] + free
    weight_ref[...] = weight
    for j in range(tiles_ref.shape[0]):
        tiles_ref[j, 0:COMP, :] = tiles_in_ref[j, 0:COMP, :]
        tiles_ref[j, COMP : COMP + TAIL, :] = tail_rows(tile_row(weight, j))
        tiles_ref[j, COMP + TAIL : DEPTH, :] = jnp.zeros((DEPTH - COMP - TAIL, TILE), BF16)
    return highest, jnp.min(free)


def first_kernel(
    meta_ref, fill_ref, mine_ref, other_ref, place_ref, log_count_ref, points_ref,
    logs_ref, tiles_ref, anchored_ref, base_ref,
    packed_ref, energy_ref, highest_ref, live_ref, exponent_ref, low_ref, rows_ref,
):
    groups = mine_ref.shape[0]
    total = meta_ref[groups]
    pairs = (total + 2 * TILE - 1) // (2 * TILE)
    packed_ref[...] = jnp.zeros(packed_ref.shape, F32)
    for t in range(groups):
        chosen = jnp.where(iota((2 * LANES, LANES), 0) == place_ref[t : t + 1, :], 1.0, 0.0).astype(BF16)
        moved = dot_nt(jnp.concatenate([mine_ref[t], other_ref[t]], 0), chosen)
        at = meta_ref[t]
        packed_ref[at] += moved[:, :LANES]
        packed_ref[at + 1] += moved[:, LANES:]
    log_count = log_count_ref[...]
    for j in range(tiles_ref.shape[0]):
        tiles_ref[j, 0:COMP, :] = jnp.concatenate([packed_ref[2 * j], packed_ref[2 * j + 1]], 1).astype(BF16)
        tiles_ref[j, COMP : COMP + TAIL, :] = tail_rows(tile_row(log_count, j))
        tiles_ref[j, COMP + TAIL : DEPTH, :] = jnp.zeros((DEPTH - COMP - TAIL, TILE), BF16)
    find_denominators(points_ref, tiles_ref, pairs, energy_ref, highest_ref, base_ref)
    first_block = meta_ref[groups + 1] * (points_ref.shape[0] // BLOCK)
    put_live(points_ref, base_ref, live_ref, fill_ref, first_block, anchored_ref)
    counted_log_sums(total, log_count_ref, tiles_ref, pairs, live_ref, exponent_ref, rows_ref, low_ref)
    logs_ref[...] = jnp.broadcast_to(rows_ref[...][None], logs_ref.shape)


def new_denominators(least, base_ref, anchored_ref, points_ref, tiles_ref, pairs, energy_ref, highest_ref, totals_ref):
    near = least > -SPREAD

    @pl.when(near)
    def _():
        denominators_near(base_ref, anchored_ref, tiles_ref, pairs, totals_ref)

    @pl.when(jnp.logical_not(near))
    def _():
        find_denominators(points_ref, tiles_ref, pairs, energy_ref, highest_ref, totals_ref)


def second_kernel(
    meta_ref, fill_ref, logs_in_ref, mine_ref, other_ref, log_count_ref, tiles_in_ref, points_ref, anchored_ref, base_ref,
    logs_ref,
    tiles_ref, weight_ref, energy_ref, highest_ref, totals_ref, live_ref, exponent_ref, second_ref, low_ref, rows_ref,
):
    groups = mine_ref.shape[0]
    slot_rows = weight_ref.shape[0]
    total = meta_ref[groups]
    pairs = (total + 2 * TILE - 1) // (2 * TILE)
    logs = log_sum_pieces(logs_in_ref)
    _, least = weighted_tiles(total, logs, log_count_ref, tiles_in_ref, tiles_ref, weight_ref)
    new_denominators(
        least, base_ref, anchored_ref, points_ref, tiles_ref, pairs, energy_ref, highest_ref, totals_ref
    )
    first_block = meta_ref[groups + 1] * (points_ref.shape[0] // BLOCK)
    put_live(points_ref, totals_ref, live_ref, fill_ref, first_block)
    counted_log_sums(total, weight_ref, tiles_ref, pairs, live_ref, exponent_ref, rows_ref, low_ref)
    rest = jnp.concatenate([tail_rows(None), jnp.zeros((DEPTH - COMP - TAIL, TILE), BF16)], 0)
    last = groups * LANES // TILE - 1

    def every_tile(t):
        parts = [jnp.concatenate([mine_ref[2 * t + k], other_ref[2 * t + k]], 0) for k in range(2)]
        tile = jnp.concatenate([jnp.concatenate(parts, 1), rest], 0)
        return tile

    def two(i, highest):
        after = exponents_and_highest(every_tile(2 * i + 1), live_ref, second_ref)
        put_rows(rows_ref, slot_rows + 4 * i, log_of_sum(highest, exponent_ref))
        highest = exponents_and_highest(every_tile(jnp.minimum(2 * i + 2, last)), live_ref, exponent_ref)
        put_rows(rows_ref, slot_rows + 4 * i + 2, log_of_sum(after, second_ref))
        return highest

    start = exponents_and_highest(every_tile(0), live_ref, exponent_ref)
    lax.fori_loop(0, (last + 1) // 2, two, start)
    logs_ref[...] = jnp.broadcast_to(rows_ref[...][None], logs_ref.shape)


def third_kernel(
    meta_ref, logs_in_ref, log_count_ref, tiles_in_ref, points_ref, anchored_ref, base_ref,
    free_ref, logden_ref,
    tiles_ref, weight_ref, energy_ref, highest_ref, totals_ref,
):
    copies = logden_ref.shape[0]
    slot_rows = weight_ref.shape[0]
    total = meta_ref[copies]
    pairs = (total + 2 * TILE - 1) // (2 * TILE)
    logs = log_sum_pieces(logs_in_ref)
    zero = logs[slot_rows + 1 : slot_rows + 2, 0:1]
    free_ref[...] = jnp.broadcast_to(zero - logs[slot_rows : slot_rows + 1, :], free_ref.shape)
    highest, least = weighted_tiles(
        total, logs[:slot_rows], log_count_ref, tiles_in_ref, tiles_ref, weight_ref
    )
    new_denominators(
        least, base_ref, anchored_ref, points_ref, tiles_ref, pairs, energy_ref, highest_ref, totals_ref
    )
    turned = [totals_ref[pl.ds(b * LANES, LANES), :].T[0:1, :] for b in range(points_ref.shape[0] // LANES)]
    logden = jnp.concatenate(turned, 0) + (highest + zero)
    logden_ref[...] = jnp.broadcast_to(logden[None], logden_ref.shape)


def shards(components, coefficients, block_window, block_fill):
    groups = lax.axis_size(STATE)
    samps = lax.axis_size(SAMP)
    position = lax.axis_index(STATE)
    core = lax.axis_index(SAMP[1])
    rows = components.shape[1] // groups
    slots = min(samps * block_window.shape[0], groups * LANES)
    slot_rows = slots // LANES
    tile_count = slots // TILE
    shape = jax.ShapeDtypeStruct
    vmem = pl.BlockSpec(memory_space=pltpu.VMEM)
    smem = pl.BlockSpec(memory_space=pltpu.SMEM)
    params = pltpu.CompilerParams(vmem_limit_bytes=24 << 20)
    whole = lambda dims: pl.BlockSpec(dims, lambda i, m: (0,) * len(dims))

    half = COMP // 2
    mine = copies_of_each(lax.dynamic_slice_in_dim(coefficients, core * half, half, 0), STATE)
    blocks = jnp.stack([block_window, block_fill])[None]
    blocks = jnp.concatenate([blocks, lax.ppermute(blocks, SAMP[1], [(0, 1), (1, 0)])], 0)
    along = lax.axis_size(SAMP[0])
    turns = [[(i, (i + k) % along) for i in range(along)] for k in range(1, along)]
    blocks = jnp.concatenate([blocks] + [lax.ppermute(blocks, SAMP[0], turn) for turn in turns], 0)
    other = lax.ppermute(mine, SAMP[1], [(0, 1), (1, 0)])
    spot = jnp.stack([position, core]).astype(jnp.int32)
    place, meta, log_count, points = pl.pallas_call(
        count_kernel,
        out_shape=(
            shape((groups, LANES), jnp.int32), shape((groups + 8, LANES), jnp.int32), shape((slot_rows, LANES), F32),
            shape((rows, DEPTH), BF16),
        ),
        grid_spec=pltpu.PrefetchScalarGridSpec(
            num_scalar_prefetch=1, grid=(1,),
            in_specs=[whole(blocks.shape), pl.BlockSpec((COMP, rows), lambda i, m: (0, m[0]))],
            out_specs=(whole((groups, LANES)), whole((groups + 8, LANES)), whole((slot_rows, LANES)), whole((rows, DEPTH))),
        ),
        compiler_params=params, name="count",
    )(spot, blocks, components)
    meta = jnp.concatenate([meta[: groups + 1, 0], spot[:1]])

    tiles_work = pltpu.VMEM((tile_count, DEPTH, TILE), BF16)
    weight_work = pltpu.VMEM((slot_rows, LANES), F32)
    energy_work = pltpu.VMEM((tile_count, rows, TILE), F32)
    column_work = pltpu.VMEM((rows, LANES), F32)
    live_work = pltpu.VMEM((rows, DEPTH), BF16)
    exponent_work = pltpu.VMEM((rows, TILE), F32)
    low_work = pltpu.VMEM((8, TILE), F32)
    logs, tiles, anchored, base = pl.pallas_call(
        first_kernel,
        out_shape=(
            shape((samps, slot_rows, LANES), F32), shape((tile_count, DEPTH, TILE), BF16), shape((rows, DEPTH), BF16),
            shape((rows, LANES), F32),
        ),
        in_specs=[smem, smem, vmem, vmem, vmem, vmem, vmem], out_specs=(vmem,) * 4,
        scratch_shapes=[
            pltpu.VMEM((slot_rows + 2, COMP, LANES), F32), energy_work, column_work, live_work, exponent_work, low_work,
            weight_work,
        ],
        compiler_params=params, name="first",
    )(meta, block_fill, mine, other, place, log_count, points)
    logs = log_sum(exchanged(logs, SAMP))
    logs = copies_of_each(logs, STATE)
    logs = pl.pallas_call(
        second_kernel,
        out_shape=shape((samps, slot_rows + groups, LANES), F32),
        in_specs=[smem, smem] + [vmem] * 8, out_specs=vmem,
        scratch_shapes=[
            tiles_work, weight_work, energy_work, column_work, column_work, live_work, exponent_work, exponent_work,
            low_work, pltpu.VMEM((slot_rows + groups, LANES), F32),
        ],
        compiler_params=params, name="second",
    )(meta, block_fill, logs, mine, other, log_count, tiles, points, anchored, base)
    logs = log_sum(exchanged(logs, SAMP))
    every = logs[slot_rows:]
    logs = jnp.concatenate(
        [
            jnp.broadcast_to(logs[None, :slot_rows], (groups, slot_rows, LANES)), every[:, None, :],
            jnp.broadcast_to(every[0], (groups, 1, LANES)), jnp.zeros((groups, 6, LANES), F32),
        ],
        1,
    )
    logs = exchanged(logs, STATE)
    free, logden = pl.pallas_call(
        third_kernel,
        out_shape=(shape((8, LANES), F32), shape((groups, rows // LANES, LANES), F32)),
        in_specs=[smem] + [vmem] * 6, out_specs=(vmem, vmem),
        scratch_shapes=[tiles_work, weight_work, energy_work, column_work, column_work],
        compiler_params=params, name="third",
    )(meta, logs, log_count, tiles, points, anchored, base)
    return free[0], exchanged(logden, STATE).reshape(-1)


def solution(mesh):
    torus = Mesh(mesh.devices.reshape(4, 2, 8, 4), ("samp_0", "samp_1", "state_0", "state_1"))
    placed = (P(None, SAMP), P(None, STATE), P(SAMP), P(SAMP))
    return jax.shard_map(
        shards, mesh=torus, in_specs=placed, out_specs=(P(STATE), P(SAMP)), check_vma=False
    )
```

time: 208 us -> 120 us (0.58)
  other arithmetic: 78.6 us -> 1.82 us
  blocking collectives: 69.5 us -> 44.6 us
  Pallas kernels: 0 us -> 19.4 us
  matrix products: 9.3 us -> 0 us
  starting transfers between devices: 16.2 us -> 25.3 us
  waiting for transfers between devices: 26.5 us -> 23.4 us
  local copies, waits for them, and re-layouts: 6.48 us -> 4.38 us
    reduce_sum x5 -> x0, other arithmetic: 42.7 us -> none  [the longest x3 26.1 us: local_denominator(): jnp.sum(jnp.exp(exponents - highest[None, :]), axis=0)]
    reduce_max x4 -> x0, other arithmetic: 31.9 us -> none  [the longest x2 17.8 us: shards(): highest = jnp.max(exponents, axis=1)]
    all_to_all x5 -> x3, blocking collectives: 69.5 us -> 44.6 us  [exchanged(): return lax.all_to_all(copies, axes, split_axis=0, concat_axis=0, tiled=True)]
    pallas_call x0 -> x4, Pallas kernels: none -> 19.4 us  [the longest x1 9.6 us: shards(): pl.pallas_call(second_kernel, out_shape=shape((samps, slot_rows + groups,...]
    dot_general x2 -> x0, matrix products: 9.3 us -> none  [the longest x1 8.99 us: shards(): lax.dot_general(laid_out(gathered, 1), component_rows, (((0,), (0,)), (()...]
    all_to_all x2 -> x3, waiting for transfers between devices: 26.5 us -> 21.6 us  [exchanged(): return lax.all_to_all(copies, axes, split_axis=0, concat_axis=0, tiled=True)]
    ppermute x0 -> x5, starting transfers between devices: none -> 4.79 us  [the longest x3 4.78 us: shards(): lax.ppermute(blocks, SAMP[0], turn)]
    all_to_all x2 -> x3, starting transfers between devices: 16.2 us -> 20.5 us  [exchanged(): return lax.all_to_all(copies, axes, split_axis=0, concat_axis=0, tiled=True)]
  transfers between devices with their start and end apart: 2 -> 8, of which waited for: 2 -> 4; matrix products, arithmetic and copies ran while one was open for 1% -> 2% of each run, Pallas kernels for 0% -> 2%
where the time goes in v3:
time: 120 us
  blocking collectives  44.6 us (37%)
  starting transfers between devices  25.3 us (21%)
  waiting for transfers between devices  23.4 us (20%)
  Pallas kernels  19.4 us (16%)
  local copies, waits for them, and re-layouts  4.38 us (4%)
  other arithmetic  1.82 us (2%)
    all_to_all x3, blocking collectives, exchanged(): return lax.all_to_all(copies, axes, split_axis=0, concat_axis=0, tiled=True)  44.6 us
    all_to_all x3, waiting for transfers between devices, exchanged(): return lax.all_to_all(copies, axes, split_axis=0, concat_axis=0, tiled=True)  21.6 us
    all_to_all x3, starting transfers between devices, exchanged(): return lax.all_to_all(copies, axes, split_axis=0, concat_axis=0, tiled=True)  20.5 us
    pallas_call x1, Pallas kernels, shards(): pl.pallas_call(second_kernel, out_shape=shape((samps, slot_rows + groups,...  9.6 us
    ppermute x3, starting transfers between devices, shards(): lax.ppermute(blocks, SAMP[0], turn)  4.78 us
    pallas_call x1, Pallas kernels, shards(): pl.pallas_call(first_kernel, out_shape=(shape((samps, slot_rows, LANES),...  4.76 us
    pallas_call x1, Pallas kernels, shards(): pl.pallas_call(third_kernel, out_shape=(shape((8, LANES), F32), shape((gr...  2.95 us
    unnamed x10, local copies, waits for them, and re-layouts  2.88 us
  transfers between devices with their start and end apart: 8, of which 4 were waited for; matrix products, arithmetic and copies ran while one was open for 2% of the time, Pallas kernels for 2%

profile of v3, /device:TPU:2, one launch (start us, length us, event | category | flops | bytes accessed | tf_op | source)
XLA Modules:
  0.0 119.6 jit_solution(13276914172226218536)
XLA Ops:
  0.6 0.0 copy-start
  0.6 0.0 copy-start.2
  0.7 0.8 add_bitcast_fusion
  1.4 0.7 broadcast_in_dim.27
  2.2 11.5 %all-to-all-start = ((bf16[32,32,128]{2,1,0:T(8,128)(2,1)}), bf16[32,32,128]{2,1,0:T(8,128)(2,1)S(1)}, u32[]{:S(2)}, u32[]{:S(2)}) async-start(bf16[32,32,128]{2,1,0:T(8,128)(2,1)} %broadcast_in_dim.27), calls=%async_computation | async-start | bytes 524288 | tf_op jit(solution)/shard_map/all_to_all | solution.py:29
  13.7 0.7 constant_dynamic-update-slice_fusion.4
  14.4 0.1 pad_add_fusion.1.spot_ref
  14.4 0.0 collective-permute-done
  14.5 1.5 %collective-permute-start.1 = (s32[2,2,256]{2,1,0:T(2,128)S(1)}, s32[2,2,256]{2,1,0:T(2,128)S(1)}, u32[]{:S(2)}, u32[]{:S(2)}) collective-permute-start(s32[2,2,256]{2,1,0:T(2,128)S(1)} %pad_add_fusion), channel_id=1, source_target_pairs={{0,64},{64,128},{128,192},{192,0},{1,65},{65,129},{129,193},{193,1... | collective-permute-start | bytes 12296 | tf_op jit(solution)/shard_map/ppermute | solution.py:404
  16.0 1.1 collective-permute-start.2
  17.1 2.2 %collective-permute-start.3 = (s32[2,2,256]{2,1,0:T(2,128)S(1)}, s32[2,2,256]{2,1,0:T(2,128)S(1)}, u32[]{:S(2)}, u32[]{:S(2)}) collective-permute-start(s32[2,2,256]{2,1,0:T(2,128)S(1)} %pad_add_fusion), channel_id=1, source_target_pairs={{0,192},{64,0},{128,64},{192,128},{1,193},{65,1},{129,65},{193,129... | collective-permute-start | bytes 12296 | tf_op jit(solution)/shard_map/ppermute | solution.py:404
  19.2 0.0 collective-permute-done.1
  19.3 1.8 %collective-permute-done.2 = s32[2,2,256]{2,1,0:T(2,128)S(1)} collective-permute-done((s32[2,2,256]{2,1,0:T(2,128)S(1)}, s32[2,2,256]{2,1,0:T(2,128)S(1)}, u32[]{:S(2)}, u32[]{:S(2)}) %collective-permute-start.2) | collective-permute-done | bytes 4128 | tf_op jit(solution)/shard_map/ppermute | solution.py:404
  21.1 6.2 %all-to-all-done.mine_ref = bf16[32,32,128]{2,1,0:T(8,128)(2,1)S(1)} async-done(((bf16[32,32,128]{2,1,0:T(8,128)(2,1)}), bf16[32,32,128]{2,1,0:T(8,128)(2,1)S(1)}, u32[]{:S(2)}, u32[]{:S(2)}) %all-to-all-start) | async-done | bytes 262176 | tf_op jit(solution)/shard_map/all_to_all | solution.py:29
  27.4 2.2 %copy-done.1 = bf16[64,32768]{1,0:T(8,128)(2,1)S(1)} copy-done((bf16[64,32768]{1,0:T(8,128)(2,1)S(1)}, bf16[64,32768]{1,0:T(8,128)(2,1)}, u32[]{:S(2)}) %copy-start.1) | copy-done | bytes 4194328
  29.5 2.1 %count.1 = (s32[32,128]{1,0:T(8,128)S(1)}, s32[40,128]{1,0:T(8,128)S(1)}, f32[16,128]{1,0:T(8,128)S(1)}, bf16[1024,128]{1,0:T(8,128)(2,1)S(1)}) custom-call(s32[2]{0:T(128)S(1)} %pad_add_fusion.1.spot_ref, s32[8,2,256]{2,1,0:T(2,128)S(1)} %constant_dynamic-update-slice_fusion.blocks_ref, bf16[64,32768]{1,0:T(8,128)(2,1)S(1)} %copy-done.1), custom_call_target="tpu_custom_call" | custom-call | tf_op jit(solution)/shard_map/count/pallas_call | solution.py:407
  31.6 0.1 slice_reduce_fusion
  31.8 0.1 pad_add_fusion.2.meta_ref
  31.8 4.8 %first.1 = (f32[8,16,128]{2,1,0:T(8,128)S(1)}, bf16[8,128,256]{2,1,0:T(8,128)(2,1)S(1)}, bf16[1024,128]{1,0:T(8,128)(2,1)S(1)}, f32[1024,128]{1,0:T(8,128)S(1)}) custom-call(s32[34]{0:T(128)S(1)} %pad_add_fusion.2.meta_ref, s32[256]{0:T(256)S(1)} %copy-done.2, bf16[32,32,128]{2,1,0:T(8,128)(2,1)S(1)} %all-to-all-done.mine_ref, ...), custom_call_target="tpu_custom_call" | custom-call | tf_op jit(solution)/shard_map/first/pallas_call | solution.py:429
  36.6 8.9 %all_to_all.30 = f32[8,16,128]{2,1,0:T(8,128)S(1)} all-to-all(f32[8,16,128]{2,1,0:T(8,128)S(1)} %get-tuple-element.16), channel_id=1, replica_groups=mesh['samp_0'=4,'samp_1'=2,'state_0'=8,'state_1'=4] {'samp_0','samp_1'}, dimensions={0} | all-to-all | bytes 131072 | tf_op jit(solution)/shard_map/all_to_all | solution.py:29
  45.6 16.6 %all_to_all.31.logs_in_ref = f32[32,16,128]{2,1,0:T(8,128)S(1)} all-to-all(f32[32,16,128]{2,1,0:T(8,128)S(1)} %broadcast_in_dim.28), channel_id=1, replica_groups=mesh['samp_0'=4,'samp_1'=2,'state_0'=8,'state_1'=4] {'state_0','state_1'}, dimensions={0} | all-to-all | bytes 524288 | tf_op jit(solution)/shard_map/all_to_all | solution.py:29
  62.2 9.6 %second.1 = f32[8,48,128]{2,1,0:T(8,128)} custom-call(s32[34]{0:T(128)S(1)} %pad_add_fusion.2.meta_ref, s32[256]{0:T(256)S(1)} %copy-done.2, f32[32,16,128]{2,1,0:T(8,128)S(1)} %all_to_all.31.logs_in_ref, bf16[32,32,128]{2,1,0:T(8,128)(2,1)S(1)} %all-to-all-done.mine_ref, bf16[32,32,128]{2,1,0:T(8,128)(2,1)S(1)} %collective-permute-done.4.other_ref, ...), custom_call_target="tpu_custom_call" | custom-call | tf_op jit(solution)/shard_map/second/pallas_call | solution.py:444
  71.8 4.8 %all-to-all-start.3 = ((f32[8,48,128]{2,1,0:T(8,128)}), f32[8,48,128]{2,1,0:T(8,128)S(1)}, u32[]{:S(2)}, u32[]{:S(2)}) async-start(f32[8,48,128]{2,1,0:T(8,128)} %second.1), calls=%async_computation.3 | async-start | bytes 393216 | tf_op jit(solution)/shard_map/all_to_all | solution.py:29
  76.6 0.1 pad.3.clone
  76.7 5.3 %all-to-all-done.3 = f32[8,48,128]{2,1,0:T(8,128)S(1)} async-done(((f32[8,48,128]{2,1,0:T(8,128)}), f32[8,48,128]{2,1,0:T(8,128)S(1)}, u32[]{:S(2)}, u32[]{:S(2)}) %all-to-all-start.3) | async-done | bytes 196640 | tf_op jit(solution)/shard_map/all_to_all | solution.py:29
  82.2 0.1 maximum_maximum_fusion
  82.3 19.0 %all_to_all.32.logs_in_ref = f32[32,24,128]{2,1,0:T(8,128)S(1)} all-to-all(f32[32,24,128]{2,1,0:T(8,128)S(1)} %maximum_maximum_fusion), channel_id=1, replica_groups=mesh['samp_0'=4,'samp_1'=2,'state_0'=8,'state_1'=4] {'state_0','state_1'}, dimensions={0} | all-to-all | bytes 786432 | tf_op jit(solution)/shard_map/all_to_all | solution.py:29
  101.3 2.9 %third.1 = (f32[8,128]{1,0:T(8,128)S(1)}, f32[32,8,128]{2,1,0:T(8,128)}) custom-call(s32[34]{0:T(128)S(1)} %pad_add_fusion.2.meta_ref, f32[32,24,128]{2,1,0:T(8,128)S(1)} %all_to_all.32.logs_in_ref, f32[16,128]{1,0:T(8,128)S(1)} %get-tuple-element.14.log_count_ref, bf16[8,128,256]{2,1,0:T(8,128)(2,1)S(1)} %get-tuple-element.17.tiles_in_ref, ...), custom_call_target="tpu_custom_call" | custom-call | tf_op jit(solution)/shard_map/third/pallas_call | solution.py:464
  104.2 4.2 %all-to-all-start.5 = ((f32[32,8,128]{2,1,0:T(8,128)}), f32[32,8,128]{2,1,0:T(8,128)S(1)}, u32[]{:S(2)}, u32[]{:S(2)}) async-start(f32[32,8,128]{2,1,0:T(8,128)} %get-tuple-element.21), calls=%async_computation.5 | async-start | bytes 262144 | tf_op jit(solution)/shard_map/all_to_all | solution.py:29
  108.4 0.5 slice_bitcast_fusion.1
  108.9 10.0 %all-to-all-done.5 = f32[32,8,128]{2,1,0:T(8,128)S(1)} async-done(((f32[32,8,128]{2,1,0:T(8,128)}), f32[32,8,128]{2,1,0:T(8,128)S(1)}, u32[]{:S(2)}, u32[]{:S(2)}) %all-to-all-start.5) | async-done | bytes 131104 | tf_op jit(solution)/shard_map/all_to_all | solution.py:29
  119.0 0.7 copy.11
  (26 shorter events, 0.2 us)
Async XLA Ops:
  0.6 0.8 copy-start
  0.6 31.2 %copy-start.2 = (s32[256]{0:T(256)S(1)}, s32[256]{0:T(256)}, u32[]{:S(2)}) copy-start(s32[256]{0:T(256)} %fill_ref.3) | copy-start | bytes 3076
  1.4 13.0 %collective-permute-start = (s32[1,2,256]{2,1,0:T(2,128)S(1)}, s32[1,2,256]{2,1,0:T(2,128)S(1)}, u32[]{:S(2)}, u32[]{:S(2)}) collective-permute-start(s32[1,2,256]{2,1,0:T(2,128)S(1)} %add_bitcast_fusion), channel_id=1, source_target_pairs={{0,32},{32,0},{1,33},{33,1},{2,34},{34,2},{3,35},{35,3},{4,36},{36... | collective-permute-start | bytes 6152 | tf_op jit(solution)/shard_map/ppermute | solution.py:401
  2.2 25.2 %all-to-all-start = ((bf16[32,32,128]{2,1,0:T(8,128)(2,1)}), bf16[32,32,128]{2,1,0:T(8,128)(2,1)S(1)}, u32[]{:S(2)}, u32[]{:S(2)}) async-start(bf16[32,32,128]{2,1,0:T(8,128)(2,1)} %broadcast_in_dim.27), calls=%async_computation | async-start | bytes 524288 | tf_op jit(solution)/shard_map/all_to_all | solution.py:29
  14.5 4.8 %collective-permute-start.1 = (s32[2,2,256]{2,1,0:T(2,128)S(1)}, s32[2,2,256]{2,1,0:T(2,128)S(1)}, u32[]{:S(2)}, u32[]{:S(2)}) collective-permute-start(s32[2,2,256]{2,1,0:T(2,128)S(1)} %pad_add_fusion), channel_id=1, source_target_pairs={{0,64},{64,128},{128,192},{192,0},{1,65},{65,129},{129,193},{193,1... | collective-permute-start | bytes 12296 | tf_op jit(solution)/shard_map/ppermute | solution.py:404
  16.0 5.1 %collective-permute-start.2 = (s32[2,2,256]{2,1,0:T(2,128)S(1)}, s32[2,2,256]{2,1,0:T(2,128)S(1)}, u32[]{:S(2)}, u32[]{:S(2)}) collective-permute-start(s32[2,2,256]{2,1,0:T(2,128)S(1)} %pad_add_fusion), channel_id=1, source_target_pairs={{0,128},{64,192},{128,0},{192,64},{1,129},{65,193},{129,1},{193,65... | collective-permute-start | bytes 12296 | tf_op jit(solution)/shard_map/ppermute | solution.py:404
  17.1 10.3 %collective-permute-start.3 = (s32[2,2,256]{2,1,0:T(2,128)S(1)}, s32[2,2,256]{2,1,0:T(2,128)S(1)}, u32[]{:S(2)}, u32[]{:S(2)}) collective-permute-start(s32[2,2,256]{2,1,0:T(2,128)S(1)} %pad_add_fusion), channel_id=1, source_target_pairs={{0,192},{64,0},{128,64},{192,128},{1,193},{65,1},{129,65},{193,129... | collective-permute-start | bytes 12296 | tf_op jit(solution)/shard_map/ppermute | solution.py:404
  27.3 4.5 %collective-permute-start.4 = (bf16[32,32,128]{2,1,0:T(8,128)(2,1)S(1)}, bf16[32,32,128]{2,1,0:T(8,128)(2,1)S(1)}, u32[]{:S(2)}, u32[]{:S(2)}) collective-permute-start(bf16[32,32,128]{2,1,0:T(8,128)(2,1)S(1)} %all-to-all-done.mine_ref), channel_id=1, source_target_pairs={{0,32},{32,0},{1,33},{33,1},{2,34},{34,2},{3,35},{35,3},{4,36},{36... | collective-permute-start | bytes 786440 | tf_op jit(solution)/shard_map/ppermute | solution.py:405
  27.4 2.2 %copy-start.1 = (bf16[64,32768]{1,0:T(8,128)(2,1)S(1)}, bf16[64,32768]{1,0:T(8,128)(2,1)}, u32[]{:S(2)}) copy-start(bf16[64,32768]{1,0:T(8,128)(2,1)} %components_ref.1) | copy-start | bytes 12582916
  71.8 10.2 %all-to-all-start.3 = ((f32[8,48,128]{2,1,0:T(8,128)}), f32[8,48,128]{2,1,0:T(8,128)S(1)}, u32[]{:S(2)}, u32[]{:S(2)}) async-start(f32[8,48,128]{2,1,0:T(8,128)} %second.1), calls=%async_computation.3 | async-start | bytes 393216 | tf_op jit(solution)/shard_map/all_to_all | solution.py:29
  104.2 14.7 %all-to-all-start.5 = ((f32[32,8,128]{2,1,0:T(8,128)}), f32[32,8,128]{2,1,0:T(8,128)S(1)}, u32[]{:S(2)}, u32[]{:S(2)}) async-start(f32[32,8,128]{2,1,0:T(8,128)} %get-tuple-element.21), calls=%async_computation.5 | async-start | bytes 262144 | tf_op jit(solution)/shard_map/all_to_all | solution.py:29

commit v4 on v3

--- a/solution.py
+++ b/solution.py
@@ -18,6 +18,8 @@
 TAIL = 16
 LEAST = 1e-25
 SPREAD = 50.0
+SMALL_ROWS = 8
+SMALL = (SMALL_ROWS - 1) * LANES - 1
 STATE = ("state_0", "state_1")
 SAMP = ("samp_0", "samp_1")
 NEGATIVE = -1e30
@@ -72,15 +74,27 @@
     return combine(x[:, :LANES], x[:, LANES:])
 
 
-def count_kernel(
-    spot_ref, blocks_ref, components_ref, place_ref, meta_ref, log_count_ref, points_ref,
-):
+def points_kernel(spot_ref, block_ref, points_ref):
+    rows = points_ref.shape[0]
+    half = COMP // 2
+    own = pl.multiple_of(spot_ref[1] * half, half)
+    lane = iota((LANES, DEPTH - COMP), 1)
+    ones = jnp.where((lane >= 3) & (lane < 6), 1.0, 0.0)
+    for b in range(rows // LANES):
+        at = slice(b * LANES, (b + 1) * LANES)
+        mine = block_ref[pl.ds(own, half), at].astype(F32)
+        other = block_ref[pl.ds(pl.multiple_of(half - own, half), half), at].astype(F32)
+        turned = -jnp.concatenate([mine, other], 0).T
+        points_ref[at, :] = jnp.concatenate([turned, ones], 1).astype(BF16)
+
+
+def count_kernel(*refs):
+    blocks_refs, (place_ref, meta_ref, log_count_ref) = refs[:-3], refs[-3:]
     groups = place_ref.shape[0]
     slots = log_count_ref.shape[0]
-    rows = points_ref.shape[0]
-    width = blocks_ref.shape[2]
+    width = blocks_refs[0].shape[2]
     counts = jnp.zeros((groups, LANES), F32)
-    for s in range(blocks_ref.shape[0]):
+    for blocks_ref, s in [(r, s) for r in blocks_refs for s in range(r.shape[0])]:
         window = blocks_ref[s, 0:1, :]
         fill = blocks_ref[s, 1:2, :]
         of_group = jnp.where(iota((groups, width), 0) == window >> 7, fill, 0).astype(F32).astype(BF16)
@@ -110,16 +124,6 @@
         gathered = gathered + dot_nt(jnp.concatenate(parts, 0).astype(BF16), of_lane)
     compact = gathered[0:slots] * 16384.0 + gathered[slots : 2 * slots] * 128.0 + gathered[2 * slots :]
     log_count_ref[...] = jnp.where(compact > 0, jnp.log(jnp.maximum(compact, 1.0)), NEGATIVE)
-    half = COMP // 2
-    own = pl.multiple_of(spot_ref[1] * half, half)
-    lane = iota((LANES, DEPTH - COMP), 1)
-    ones = jnp.where((lane >= 3) & (lane < 6), 1.0, 0.0)
-    for b in range(rows // LANES):
-        at = slice(b * LANES, (b + 1) * LANES)
-        mine = components_ref[pl.ds(own, half), at].astype(F32)
-        other = components_ref[pl.ds(pl.multiple_of(half - own, half), half), at].astype(F32)
-        turned = -jnp.concatenate([mine, other], 0).T
-        points_ref[at, :] = jnp.concatenate([turned, ones], 1).astype(BF16)
 
 
 def tail_rows(weight):
@@ -272,7 +276,7 @@
     free = jnp.where(valid, -logs, 4 * NEGATIVE)
     highest = jnp.max(jnp.max(free, axis=0, keepdims=True), axis=1, keepdims=True)
     free = jnp.where(valid, free - highest, 0.0)
-    weight = log_count_ref[...] + free
+    weight = log_count_ref[0 : weight_ref.shape[0], :] + free
     weight_ref[...] = weight
     for j in range(tiles_ref.shape[0]):
         tiles_ref[j, 0:COMP, :] = tiles_in_ref[j, 0:COMP, :]
@@ -284,7 +288,7 @@
 def first_kernel(
     meta_ref, fill_ref, mine_ref, other_ref, place_ref, log_count_ref, points_ref,
     logs_ref, tiles_ref, anchored_ref, base_ref,
-    packed_ref, energy_ref, highest_ref, live_ref, exponent_ref, low_ref, rows_ref,
+    packed_ref, energy_ref, highest_ref, live_ref, exponent_ref, low_ref, rows_ref, weight_ref,
 ):
     groups = mine_ref.shape[0]
     total = meta_ref[groups]
@@ -296,7 +300,8 @@
         at = meta_ref[t]
         packed_ref[at] += moved[:, :LANES]
         packed_ref[at + 1] += moved[:, LANES:]
-    log_count = log_count_ref[...]
+    log_count = log_count_ref[0 : logs_ref.shape[1], :]
+    weight_ref[...] = log_count
     for j in range(tiles_ref.shape[0]):
         tiles_ref[j, 0:COMP, :] = jnp.concatenate([packed_ref[2 * j], packed_ref[2 * j + 1]], 1).astype(BF16)
         tiles_ref[j, COMP : COMP + TAIL, :] = tail_rows(tile_row(log_count, j))
@@ -304,7 +309,7 @@
     find_denominators(points_ref, tiles_ref, pairs, energy_ref, highest_ref, base_ref)
     first_block = meta_ref[groups + 1] * (points_ref.shape[0] // BLOCK)
     put_live(points_ref, base_ref, live_ref, fill_ref, first_block, anchored_ref)
-    counted_log_sums(total, log_count_ref, tiles_ref, pairs, live_ref, exponent_ref, rows_ref, low_ref)
+    counted_log_sums(total, weight_ref, tiles_ref, pairs, live_ref, exponent_ref, rows_ref, low_ref)
     logs_ref[...] = jnp.broadcast_to(rows_ref[...][None], logs_ref.shape)
 
 
@@ -345,16 +350,33 @@
         tile = jnp.concatenate([jnp.concatenate(parts, 1), rest], 0)
         return tile
 
+    def step(t, here_ref, highest, next_ref):
+        tile = every_tile(jnp.minimum(t + 1, last))
+        totals = jnp.zeros((8, TILE), F32)
+        tops = []
+        for c in range(live_ref.shape[0] // CHUNK):
+            exponents = dot(live_ref[chunk(c), :], tile)
+            next_ref[chunk(c), :] = exponents
+            tops.append(jnp.max(exponents.reshape(CHUNK // 8, 8, TILE), axis=0))
+            grown = jnp.exp(here_ref[chunk(c), :] - highest)
+            totals = totals + jnp.sum(grown.reshape(CHUNK // 8, 8, TILE), axis=0)
+        logs = highest + jnp.log(jnp.sum(totals, axis=0, keepdims=True))
+        put_rows(rows_ref, slot_rows + 2 * t, logs)
+        return jnp.max(functools.reduce(jnp.maximum, tops), axis=0, keepdims=True)
+
     def two(i, highest):
-        after = exponents_and_highest(every_tile(2 * i + 1), live_ref, second_ref)
-        put_rows(rows_ref, slot_rows + 4 * i, log_of_sum(highest, exponent_ref))
-        highest = exponents_and_highest(every_tile(jnp.minimum(2 * i + 2, last)), live_ref, exponent_ref)
-        put_rows(rows_ref, slot_rows + 4 * i + 2, log_of_sum(after, second_ref))
-        return highest
+        highest = step(2 * i, exponent_ref, highest, second_ref)
+        return step(2 * i + 1, second_ref, highest, exponent_ref)
 
     start = exponents_and_highest(every_tile(0), live_ref, exponent_ref)
     lax.fori_loop(0, (last + 1) // 2, two, start)
     logs_ref[...] = jnp.broadcast_to(rows_ref[...][None], logs_ref.shape)
+
+
+def places(slot_rows):
+    if slot_rows == SMALL_ROWS:
+        return (slot_rows - 1, slot_rows - 2), LANES - 1
+    return (slot_rows, slot_rows + 1), 0
 
 
 def third_kernel(
@@ -367,8 +389,9 @@
     total = meta_ref[copies]
     pairs = (total + 2 * TILE - 1) // (2 * TILE)
     logs = log_sum_pieces(logs_in_ref)
-    zero = logs[slot_rows + 1 : slot_rows + 2, 0:1]
-    free_ref[...] = jnp.broadcast_to(zero - logs[slot_rows : slot_rows + 1, :], free_ref.shape)
+    (own_row, zero_row), zero_lane = places(slot_rows)
+    zero = logs[zero_row : zero_row + 1, zero_lane : zero_lane + 1]
+    free_ref[...] = jnp.broadcast_to(zero - logs[own_row : own_row + 1, :], free_ref.shape)
     highest, least = weighted_tiles(
         total, logs[:slot_rows], log_count_ref, tiles_in_ref, tiles_ref, weight_ref
     )
@@ -380,45 +403,30 @@
     logden_ref[...] = jnp.broadcast_to(logden[None], logden_ref.shape)
 
 
-def shards(components, coefficients, block_window, block_fill):
-    groups = lax.axis_size(STATE)
+def last_message(logs, slot_rows, groups):
+    counted, every = logs[:slot_rows], logs[slot_rows:]
+    row, lane = iota(counted.shape, 0), iota(counted.shape, 1)
+    if slot_rows == SMALL_ROWS:
+        counted = jnp.where((row == slot_rows - 2) & (lane == LANES - 1), every[0, 0], counted)
+        return jnp.where(row == slot_rows - 1, every[:, None, :], counted[None])
+    return jnp.concatenate(
+        [
+            jnp.broadcast_to(counted[None], (groups, slot_rows, LANES)), every[:, None, :],
+            jnp.broadcast_to(every[0], (groups, 1, LANES)), jnp.zeros((groups, 6, LANES), F32),
+        ],
+        1,
+    )
+
+
+def iterated(slot_rows, meta, block_fill, mine, other, place, log_count, points):
     samps = lax.axis_size(SAMP)
-    position = lax.axis_index(STATE)
-    core = lax.axis_index(SAMP[1])
-    rows = components.shape[1] // groups
-    slots = min(samps * block_window.shape[0], groups * LANES)
-    slot_rows = slots // LANES
-    tile_count = slots // TILE
+    groups = mine.shape[0]
+    rows = points.shape[0]
+    tile_count = slot_rows * LANES // TILE
     shape = jax.ShapeDtypeStruct
     vmem = pl.BlockSpec(memory_space=pltpu.VMEM)
     smem = pl.BlockSpec(memory_space=pltpu.SMEM)
     params = pltpu.CompilerParams(vmem_limit_bytes=24 << 20)
-    whole = lambda dims: pl.BlockSpec(dims, lambda i, m: (0,) * len(dims))
-
-    half = COMP // 2
-    mine = copies_of_each(lax.dynamic_slice_in_dim(coefficients, core * half, half, 0), STATE)
-    blocks = jnp.stack([block_window, block_fill])[None]
-    blocks = jnp.concatenate([blocks, lax.ppermute(blocks, SAMP[1], [(0, 1), (1, 0)])], 0)
-    along = lax.axis_size(SAMP[0])
-    turns = [[(i, (i + k) % along) for i in range(along)] for k in range(1, along)]
-    blocks = jnp.concatenate([blocks] + [lax.ppermute(blocks, SAMP[0], turn) for turn in turns], 0)
-    other = lax.ppermute(mine, SAMP[1], [(0, 1), (1, 0)])
-    spot = jnp.stack([position, core]).astype(jnp.int32)
-    place, meta, log_count, points = pl.pallas_call(
-        count_kernel,
-        out_shape=(
-            shape((groups, LANES), jnp.int32), shape((groups + 8, LANES), jnp.int32), shape((slot_rows, LANES), F32),
-            shape((rows, DEPTH), BF16),
-        ),
-        grid_spec=pltpu.PrefetchScalarGridSpec(
-            num_scalar_prefetch=1, grid=(1,),
-            in_specs=[whole(blocks.shape), pl.BlockSpec((COMP, rows), lambda i, m: (0, m[0]))],
-            out_specs=(whole((groups, LANES)), whole((groups + 8, LANES)), whole((slot_rows, LANES)), whole((rows, DEPTH))),
-        ),
-        compiler_params=params, name="count",
-    )(spot, blocks, components)
-    meta = jnp.concatenate([meta[: groups + 1, 0], spot[:1]])
-
     tiles_work = pltpu.VMEM((tile_count, DEPTH, TILE), BF16)
     weight_work = pltpu.VMEM((slot_rows, LANES), F32)
     energy_work = pltpu.VMEM((tile_count, rows, TILE), F32)
@@ -435,7 +443,7 @@
         in_specs=[smem, smem, vmem, vmem, vmem, vmem, vmem], out_specs=(vmem,) * 4,
         scratch_shapes=[
             pltpu.VMEM((slot_rows + 2, COMP, LANES), F32), energy_work, column_work, live_work, exponent_work, low_work,
-            weight_work,
+            weight_work, weight_work,
         ],
         compiler_params=params, name="first",
     )(meta, block_fill, mine, other, place, log_count, points)
@@ -451,15 +459,7 @@
         ],
         compiler_params=params, name="second",
     )(meta, block_fill, logs, mine, other, log_count, tiles, points, anchored, base)
-    logs = log_sum(exchanged(logs, SAMP))
-    every = logs[slot_rows:]
-    logs = jnp.concatenate(
-        [
-            jnp.broadcast_to(logs[None, :slot_rows], (groups, slot_rows, LANES)), every[:, None, :],
-            jnp.broadcast_to(every[0], (groups, 1, LANES)), jnp.zeros((groups, 6, LANES), F32),
-        ],
-        1,
-    )
+    logs = last_message(log_sum(exchanged(logs, SAMP)), slot_rows, groups)
     logs = exchanged(logs, STATE)
     free, logden = pl.pallas_call(
         third_kernel,
@@ -471,6 +471,49 @@
     return free[0], exchanged(logden, STATE).reshape(-1)
 
 
+def shards(components, coefficients, block_window, block_fill):
+    groups = lax.axis_size(STATE)
+    samps = lax.axis_size(SAMP)
+    position = lax.axis_index(STATE)
+    core = lax.axis_index(SAMP[1])
+    rows = components.shape[1] // groups
+    slot_rows = min(samps * block_window.shape[0] // LANES, groups)
+    shape = jax.ShapeDtypeStruct
+    vmem = pl.BlockSpec(memory_space=pltpu.VMEM)
+    params = pltpu.CompilerParams(vmem_limit_bytes=24 << 20)
+    spot = jnp.stack([position, core]).astype(jnp.int32)
+
+    half = COMP // 2
+    mine = copies_of_each(lax.dynamic_slice_in_dim(coefficients, core * half, half, 0), STATE)
+    blocks = jnp.stack([block_window, block_fill])[None]
+    blocks = jnp.concatenate([blocks, lax.ppermute(blocks, SAMP[1], [(0, 1), (1, 0)])], 0)
+    along = lax.axis_size(SAMP[0])
+    turns = [[(i, (i + k) % along) for i in range(along)] for k in range(1, along)]
+    pieces = [blocks] + [lax.ppermute(blocks, SAMP[0], turn) for turn in turns]
+    points = pl.pallas_call(
+        points_kernel,
+        out_shape=shape((rows, DEPTH), BF16),
+        in_specs=[pl.BlockSpec(memory_space=pltpu.SMEM), vmem], out_specs=vmem,
+        compiler_params=params, name="points",
+    )(spot, lax.dynamic_slice_in_dim(components, position * rows, rows, 1))
+    other = lax.ppermute(mine, SAMP[1], [(0, 1), (1, 0)])
+    place, meta, log_count = pl.pallas_call(
+        count_kernel,
+        out_shape=(
+            shape((groups, LANES), jnp.int32), shape((groups + 8, LANES), jnp.int32),
+            shape((slot_rows, LANES), F32),
+        ),
+        in_specs=[vmem] * len(pieces), out_specs=(vmem, vmem, vmem), compiler_params=params, name="count",
+    )(*pieces)
+    total = meta[groups, 0]
+    meta = jnp.concatenate([meta[: groups + 1, 0], spot[:1]])
+    return lax.cond(
+        total <= SMALL,
+        functools.partial(iterated, SMALL_ROWS), functools.partial(iterated, slot_rows),
+        meta, block_fill, mine, other, place, log_count, points,
+    )
+
+
 def solution(mesh):
     torus = Mesh(mesh.devices.reshape(4, 2, 8, 4), ("samp_0", "samp_1", "state_0", "state_1"))
     placed = (P(None, SAMP), P(None, STATE), P(SAMP), P(SAMP))

time: 120 us -> 115 us (0.958)
  blocking collectives: 44.6 us -> 22.6 us
  waiting for transfers between devices: 23.4 us -> 32.4 us
  starting transfers between devices: 25.3 us -> 30.4 us
  local copies, waits for them, and re-layouts: 4.38 us -> 5.74 us
    all_to_all x3 -> x2, blocking collectives: 44.6 us -> 22.6 us  [exchanged(): return lax.all_to_all(copies, axes, split_axis=0, concat_axis=0, tiled=True)]
    all_to_all x3 -> x4, waiting for transfers between devices: 21.6 us -> 32.2 us  [exchanged(): return lax.all_to_all(copies, axes, split_axis=0, concat_axis=0, tiled=True)]
    all_to_all x3 -> x4, starting transfers between devices: 20.5 us -> 25.7 us  [exchanged(): return lax.all_to_all(copies, axes, split_axis=0, concat_axis=0, tiled=True)]
    ppermute x3, waiting for transfers between devices: 1.83 us -> 0.01 us  [shards(): pieces = [blocks] + [lax.ppermute(blocks, SAMP[0], turn) for turn in turns]]
    pallas_call x3 -> x4, Pallas kernels: 17.3 us -> 18.3 us  [the longest x1 9.71 us: iterated(): pl.pallas_call(second_kernel, out_shape=shape((samps, slot_rows + groups,...]
    unnamed x10 -> x5, local copies, waits for them, and re-layouts: 2.88 us -> 2.28 us
  transfers between devices with their start and end apart: 8 -> 9, of which waited for: 4 -> 5; matrix products, arithmetic and copies ran while one was open for 2% -> 2% of each run, Pallas kernels for 2% -> 2%
where the time goes in v4:
time: 115 us; the launch traced here: 114 us
  waiting for transfers between devices  32.4 us (28%)
  starting transfers between devices  30.4 us (26%)
  blocking collectives  22.6 us (20%)
  Pallas kernels  19.9 us (17%)
  local copies, waits for them, and re-layouts  5.74 us (5%)
  other arithmetic  1.77 us (2%)
  between operations  1.36 us (1%)
    all_to_all x4, waiting for transfers between devices, exchanged(): return lax.all_to_all(copies, axes, split_axis=0, concat_axis=0, tiled=True)  32.2 us
    all_to_all x4, starting transfers between devices, exchanged(): return lax.all_to_all(copies, axes, split_axis=0, concat_axis=0, tiled=True)  25.7 us
    all_to_all x2, blocking collectives, exchanged(): return lax.all_to_all(copies, axes, split_axis=0, concat_axis=0, tiled=True)  22.6 us
    pallas_call x1, Pallas kernels, iterated(): pl.pallas_call(second_kernel, out_shape=shape((samps, slot_rows + groups,...  9.71 us
    pallas_call x1, Pallas kernels, iterated(): pl.pallas_call(first_kernel, out_shape=(shape((samps, slot_rows, LANES),...  4.91 us
    ppermute x3, starting transfers between devices, shards(): pieces = [blocks] + [lax.ppermute(blocks, SAMP[0], turn) for turn in turns]  4.76 us
    pallas_call x1, Pallas kernels, iterated(): pl.pallas_call(third_kernel, out_shape=(shape((8, LANES), F32), shape((gr...  2.98 us
  transfers between devices with their start and end apart: 9, of which 5 were waited for; matrix products, arithmetic and copies ran while one was open for 2% of the time, Pallas kernels for 2%

profile of v4, /device:TPU:2, one launch (start us, length us, event | category | flops | bytes accessed | tf_op | source)
XLA Modules:
  0.0 114.4 jit_solution(4440896299260580256)
XLA Ops:
  0.7 0.7 copy-done
  1.4 0.7 broadcast_in_dim.55
  2.1 11.5 %all-to-all-start.10 = ((bf16[32,32,128]{2,1,0:T(8,128)(2,1)}), bf16[32,32,128]{2,1,0:T(8,128)(2,1)S(1)}, u32[]{:S(2)}, u32[]{:S(2)}) async-start(bf16[32,32,128]{2,1,0:T(8,128)(2,1)} %broadcast_in_dim.55), calls=%async_computation.10 | async-start | bytes 524288 | tf_op jit(solution)/shard_map/all_to_all | solution.py:31
  13.6 0.7 add_bitcast_fusion
  14.3 0.9 constant_dynamic-slice_fusion.block_ref
  15.2 0.2 collective-permute-done
  15.5 0.5 collective-permute-start.3
  16.0 2.4 %collective-permute-start.2 = (s32[2,2,256]{2,1,0:T(2,128)S(1)}, s32[2,2,256]{2,1,0:T(2,128)S(1)}, u32[]{:S(2)}, u32[]{:S(2)}) collective-permute-start(s32[2,2,256]{2,1,0:T(2,128)S(1)} %pad_add_fusion.refs_0_), channel_id=1, source_target_pairs={{0,128},{64,192},{128,0},{192,64},{1,129},{65,193},{129,1},{193,65... | collective-permute-start | bytes 12296 | tf_op jit(solution)/shard_map/ppermute | solution.py:492
  18.4 1.8 %collective-permute-start.1 = (s32[2,2,256]{2,1,0:T(2,128)S(1)}, s32[2,2,256]{2,1,0:T(2,128)S(1)}, u32[]{:S(2)}, u32[]{:S(2)}) collective-permute-start(s32[2,2,256]{2,1,0:T(2,128)S(1)} %pad_add_fusion.refs_0_), channel_id=1, source_target_pairs={{0,64},{64,128},{128,192},{192,0},{1,65},{65,129},{129,193},{193,1... | collective-permute-start | bytes 12296 | tf_op jit(solution)/shard_map/ppermute | solution.py:492
  20.2 6.2 %all-to-all-done.10 = bf16[32,32,128]{2,1,0:T(8,128)(2,1)S(1)} async-done(((bf16[32,32,128]{2,1,0:T(8,128)(2,1)}), bf16[32,32,128]{2,1,0:T(8,128)(2,1)S(1)}, u32[]{:S(2)}, u32[]{:S(2)}) %all-to-all-start.10) | async-done | bytes 262176 | tf_op jit(solution)/shard_map/all_to_all | solution.py:31
  26.5 0.7 points.1
  27.2 1.6 %count.1 = (s32[32,128]{1,0:T(8,128)S(1)}, s32[40,128]{1,0:T(8,128)S(1)}, f32[16,128]{1,0:T(8,128)S(1)}) custom-call(s32[2,2,256]{2,1,0:T(2,128)S(1)} %pad_add_fusion.refs_0_, s32[2,2,256]{2,1,0:T(2,128)S(1)} %collective-permute-done.1.refs_1_, s32[2,2,256]{2,1,0:T(2,128)S(1)} %collective-permute-done.2.refs_2_, s32[2,2,256]{2,1,0:T(2,128)S(1)} %collective-permute-done.3.refs_3_), custom_call_target="tpu_custom_call" | custom-call | tf_op jit(solution)/shard_map/count/pallas_call | solution.py:500
  28.8 0.5 slice.32
  29.9 0.1 slice_reduce_fusion
  30.1 0.1 pad_add_fusion.1
  30.1 82.7 %conditional.1 = (f32[128]{0:T(128)S(1)}, f32[32768]{0:T(1024)}) conditional(s32[]{:T(128)} %bitcast.10, (s32[34]{0:T(128)S(1)}, s32[256]{0:T(256)}, bf16[32,32,128]{2,1,0:T(8,128)(2,1)S(1)}, bf16[32,32,128]{2,1,0:T(8,128)(2,1)S(1)}, s32[32,128]{1,0:T(8,128)S(1)}, /*index=5*/f32[16,128]{1,0:T(8,128)S(1)}, bf16[1024,128]{1,0:T(8,128)(2,1)S(1)}) %tuple.15, ...), branch_computations={%region_0.0_spmd, %region_5.10_spmd} | conditional | flops 483328 | bytes 4442960 | solution.py:510
  30.3 4.9 %first.3 = (f32[8,8,128]{2,1,0:T(8,128)S(1)}, bf16[4,128,256]{2,1,0:T(8,128)(2,1)S(1)}, bf16[1024,128]{1,0:T(8,128)(2,1)S(1)}, f32[1024,128]{1,0:T(8,128)S(1)}) custom-call(s32[34]{0:T(128)S(1)} %get-tuple-element.41.meta_ref, s32[256]{0:T(256)} %get-tuple-element.42.fill_ref, bf16[32,32,128]{2,1,0:T(8,128)(2,1)S(1)} %get-tuple-element.43.mine_ref, ...), custom_call_target="tpu_custom_call" | custom-call | tf_op jit(solution)/shard_map/cond/branch_1_fun/first/pallas_call | solution.py:437
  35.2 8.7 %all_to_all.48 = f32[8,8,128]{2,1,0:T(8,128)S(1)} all-to-all(f32[8,8,128]{2,1,0:T(8,128)S(1)} %get-tuple-element.48), channel_id=1, replica_groups=mesh['samp_0'=4,'samp_1'=2,'state_0'=8,'state_1'=4] {'samp_0','samp_1'}, dimensions={0} | all-to-all | bytes 65536 | tf_op jit(solution)/shard_map/cond/branch_1_fun/all_to_all | solution.py:31
  44.0 0.7 broadcast_in_dim.48
  44.7 4.8 %all-to-all-start.6 = ((f32[32,8,128]{2,1,0:T(8,128)}), f32[32,8,128]{2,1,0:T(8,128)S(1)}, u32[]{:S(2)}, u32[]{:S(2)}) async-start(f32[32,8,128]{2,1,0:T(8,128)} %broadcast_in_dim.48), calls=%async_computation.6 | async-start | bytes 262144 | tf_op jit(solution)/shard_map/cond/branch_1_fun/all_to_all | solution.py:31
  49.5 10.5 %all-to-all-done.6.logs_in_ref = f32[32,8,128]{2,1,0:T(8,128)S(1)} async-done(((f32[32,8,128]{2,1,0:T(8,128)}), f32[32,8,128]{2,1,0:T(8,128)S(1)}, u32[]{:S(2)}, u32[]{:S(2)}) %all-to-all-start.6) | async-done | bytes 131104 | tf_op jit(solution)/shard_map/cond/branch_1_fun/all_to_all | solution.py:31
  60.0 9.7 %second.3 = f32[8,40,128]{2,1,0:T(8,128)} custom-call(s32[34]{0:T(128)S(1)} %get-tuple-element.41.meta_ref, s32[256]{0:T(256)} %get-tuple-element.42.fill_ref, f32[32,8,128]{2,1,0:T(8,128)S(1)} %all-to-all-done.6.logs_in_ref, bf16[32,32,128]{2,1,0:T(8,128)(2,1)S(1)} %get-tuple-element.43.mine_ref, bf16[32,32,128]{2,1,0:T(8,128)(2,1)S(1)} %get-tuple-element.44.other_ref, ...), custom_call_target="tpu_custom_call" | custom-call | tf_op jit(solution)/shard_map/cond/branch_1_fun/second/pallas_call | solution.py:452
  69.7 4.8 %all-to-all-start.7 = ((f32[8,40,128]{2,1,0:T(8,128)}), f32[8,40,128]{2,1,0:T(8,128)S(1)}, u32[]{:S(2)}, u32[]{:S(2)}) async-start(f32[8,40,128]{2,1,0:T(8,128)} %second.3), calls=%async_computation.7 | async-start | bytes 327680 | tf_op jit(solution)/shard_map/cond/branch_1_fun/all_to_all | solution.py:31
  74.5 5.0 %all-to-all-done.7 = f32[8,40,128]{2,1,0:T(8,128)S(1)} async-done(((f32[8,40,128]{2,1,0:T(8,128)}), f32[8,40,128]{2,1,0:T(8,128)S(1)}, u32[]{:S(2)}, u32[]{:S(2)}) %all-to-all-start.7) | async-done | bytes 163872 | tf_op jit(solution)/shard_map/cond/branch_1_fun/all_to_all | solution.py:31
  79.6 0.5 slice.38
  80.1 0.7 slice_select_fusion
  80.8 0.1 broadcast_select_fusion
  80.9 13.8 %all_to_all.49.logs_in_ref = f32[32,8,128]{2,1,0:T(8,128)S(1)} all-to-all(f32[32,8,128]{2,1,0:T(8,128)S(1)} %broadcast_select_fusion), channel_id=1, replica_groups=mesh['samp_0'=4,'samp_1'=2,'state_0'=8,'state_1'=4] {'state_0','state_1'}, dimensions={0} | all-to-all | bytes 262144 | tf_op jit(solution)/shard_map/cond/branch_1_fun/all_to_all | solution.py:31
  94.7 3.0 %third.3 = (f32[8,128]{1,0:T(8,128)S(1)}, f32[32,8,128]{2,1,0:T(8,128)}) custom-call(s32[34]{0:T(128)S(1)} %get-tuple-element.41.meta_ref, f32[32,8,128]{2,1,0:T(8,128)S(1)} %all_to_all.49.logs_in_ref, f32[16,128]{1,0:T(8,128)S(1)} %get-tuple-element.46.log_count_ref, bf16[4,128,256]{2,1,0:T(8,128)(2,1)S(1)} %get-tuple-element.49.tiles_in_ref, ...), custom_call_target="tpu_custom_call" | custom-call | tf_op jit(solution)/shard_map/cond/branch_1_fun/third/pallas_call | solution.py:464
  97.7 4.6 %all-to-all-start.9 = ((f32[32,8,128]{2,1,0:T(8,128)}), f32[32,8,128]{2,1,0:T(8,128)}, u32[]{:S(2)}, u32[]{:S(2)}) async-start(f32[32,8,128]{2,1,0:T(8,128)} %get-tuple-element.53), calls=%async_computation.9 | async-start | bytes 262144 | tf_op jit(solution)/shard_map/cond/branch_1_fun/all_to_all | solution.py:31
  102.3 10.5 %all-to-all-done.9 = f32[32,8,128]{2,1,0:T(8,128)} async-done(((f32[32,8,128]{2,1,0:T(8,128)}), f32[32,8,128]{2,1,0:T(8,128)}, u32[]{:S(2)}, u32[]{:S(2)}) %all-to-all-start.9) | async-done | bytes 131104 | tf_op jit(solution)/shard_map/cond/branch_1_fun/all_to_all | solution.py:31
  112.8 1.6 %copy.15 = f32[32768]{0:T(1024)} copy(f32[32768]{0:T(1024)} %get-tuple-element.71) | data formatting | bytes 262144
  (23 shorter events, 0.2 us)
Async XLA Ops:
  0.6 0.7 copy-start
  2.1 24.3 %all-to-all-start.10 = ((bf16[32,32,128]{2,1,0:T(8,128)(2,1)}), bf16[32,32,128]{2,1,0:T(8,128)(2,1)S(1)}, u32[]{:S(2)}, u32[]{:S(2)}) async-start(bf16[32,32,128]{2,1,0:T(8,128)(2,1)} %broadcast_in_dim.55), calls=%async_computation.10 | async-start | bytes 524288 | tf_op jit(solution)/shard_map/all_to_all | solution.py:31
  14.3 1.2 %collective-permute-start = (s32[1,2,256]{2,1,0:T(2,128)S(1)}, s32[1,2,256]{2,1,0:T(2,128)S(1)}, u32[]{:S(2)}, u32[]{:S(2)}) collective-permute-start(s32[1,2,256]{2,1,0:T(2,128)S(1)} %add_bitcast_fusion), channel_id=1, source_target_pairs={{0,32},{32,0},{1,33},{33,1},{2,34},{34,2},{3,35},{35,3},{4,36},{36... | collective-permute-start | bytes 6152 | tf_op jit(solution)/shard_map/ppermute | solution.py:489
  15.5 11.7 %collective-permute-start.3 = (s32[2,2,256]{2,1,0:T(2,128)S(1)}, s32[2,2,256]{2,1,0:T(2,128)S(1)}, u32[]{:S(2)}, u32[]{:S(2)}) collective-permute-start(s32[2,2,256]{2,1,0:T(2,128)S(1)} %pad_add_fusion.refs_0_), channel_id=1, source_target_pairs={{0,192},{64,0},{128,64},{192,128},{1,193},{65,1},{129,65},{193,129... | collective-permute-start | bytes 12296 | tf_op jit(solution)/shard_map/ppermute | solution.py:492
  16.0 11.2 %collective-permute-start.2 = (s32[2,2,256]{2,1,0:T(2,128)S(1)}, s32[2,2,256]{2,1,0:T(2,128)S(1)}, u32[]{:S(2)}, u32[]{:S(2)}) collective-permute-start(s32[2,2,256]{2,1,0:T(2,128)S(1)} %pad_add_fusion.refs_0_), channel_id=1, source_target_pairs={{0,128},{64,192},{128,0},{192,64},{1,129},{65,193},{129,1},{193,65... | collective-permute-start | bytes 12296 | tf_op jit(solution)/shard_map/ppermute | solution.py:492
  18.4 8.8 %collective-permute-start.1 = (s32[2,2,256]{2,1,0:T(2,128)S(1)}, s32[2,2,256]{2,1,0:T(2,128)S(1)}, u32[]{:S(2)}, u32[]{:S(2)}) collective-permute-start(s32[2,2,256]{2,1,0:T(2,128)S(1)} %pad_add_fusion.refs_0_), channel_id=1, source_target_pairs={{0,64},{64,128},{128,192},{192,0},{1,65},{65,129},{129,193},{193,1... | collective-permute-start | bytes 12296 | tf_op jit(solution)/shard_map/ppermute | solution.py:492
  26.4 3.7 %collective-permute-start.4 = (bf16[32,32,128]{2,1,0:T(8,128)(2,1)S(1)}, bf16[32,32,128]{2,1,0:T(8,128)(2,1)S(1)}, u32[]{:S(2)}, u32[]{:S(2)}) collective-permute-start(bf16[32,32,128]{2,1,0:T(8,128)(2,1)S(1)} %all-to-all-done.10), channel_id=1, source_target_pairs={{0,32},{32,0},{1,33},{33,1},{2,34},{34,2},{3,35},{35,3},{4,36},{36... | collective-permute-start | bytes 786440 | tf_op jit(solution)/shard_map/ppermute | solution.py:499
  44.7 15.3 %all-to-all-start.6 = ((f32[32,8,128]{2,1,0:T(8,128)}), f32[32,8,128]{2,1,0:T(8,128)S(1)}, u32[]{:S(2)}, u32[]{:S(2)}) async-start(f32[32,8,128]{2,1,0:T(8,128)} %broadcast_in_dim.48), calls=%async_computation.6 | async-start | bytes 262144 | tf_op jit(solution)/shard_map/cond/branch_1_fun/all_to_all | solution.py:31
  69.7 9.8 %all-to-all-start.7 = ((f32[8,40,128]{2,1,0:T(8,128)}), f32[8,40,128]{2,1,0:T(8,128)S(1)}, u32[]{:S(2)}, u32[]{:S(2)}) async-start(f32[8,40,128]{2,1,0:T(8,128)} %second.3), calls=%async_computation.7 | async-start | bytes 327680 | tf_op jit(solution)/shard_map/cond/branch_1_fun/all_to_all | solution.py:31
  97.7 15.1 %all-to-all-start.9 = ((f32[32,8,128]{2,1,0:T(8,128)}), f32[32,8,128]{2,1,0:T(8,128)}, u32[]{:S(2)}, u32[]{:S(2)}) async-start(f32[32,8,128]{2,1,0:T(8,128)} %get-tuple-element.53), calls=%async_computation.9 | async-start | bytes 262144 | tf_op jit(solution)/shard_map/cond/branch_1_fun/all_to_all | solution.py:31
  112.8 1.6 %copy-start.1 = (f32[128]{0:T(128)}, f32[128]{0:T(128)S(1)}, u32[]{:S(2)}) copy-start(f32[128]{0:T(128)S(1)} %get-tuple-element.70) | copy-start | bytes 1540

commit v5 on v4

--- a/solution.py
+++ b/solution.py
@@ -373,6 +373,22 @@
     logs_ref[...] = jnp.broadcast_to(rows_ref[...][None], logs_ref.shape)
 
 
+def message_kernel(logs_ref, message_ref):
+    groups = message_ref.shape[0]
+    slot_rows = logs_ref.shape[1] - groups
+    (own_row, zero_row), zero_lane = places(slot_rows)
+    logs = log_sum_pieces(logs_ref)
+    rows = message_ref.shape[1]
+    common = logs[0:slot_rows, :]
+    if rows > slot_rows:
+        common = jnp.concatenate([common, jnp.zeros((rows - slot_rows, LANES), F32)], 0)
+    row, lane = iota(common.shape, 0), iota(common.shape, 1)
+    common = jnp.where((row == zero_row) & (lane == zero_lane), logs[slot_rows : slot_rows + 1, 0:1], common)
+    for t in range(groups):
+        own = logs[slot_rows + t : slot_rows + t + 1, :]
+        message_ref[t] = jnp.where(row == own_row, own, common)
+
+
 def places(slot_rows):
     if slot_rows == SMALL_ROWS:
         return (slot_rows - 1, slot_rows - 2), LANES - 1
@@ -391,7 +407,7 @@
     logs = log_sum_pieces(logs_in_ref)
     (own_row, zero_row), zero_lane = places(slot_rows)
     zero = logs[zero_row : zero_row + 1, zero_lane : zero_lane + 1]
-    free_ref[...] = jnp.broadcast_to(zero - logs[own_row : own_row + 1, :], free_ref.shape)
+    free_ref[...] = zero - logs[own_row : own_row + 1, :]
     highest, least = weighted_tiles(
         total, logs[:slot_rows], log_count_ref, tiles_in_ref, tiles_ref, weight_ref
     )
@@ -401,21 +417,6 @@
     turned = [totals_ref[pl.ds(b * LANES, LANES), :].T[0:1, :] for b in range(points_ref.shape[0] // LANES)]
     logden = jnp.concatenate(turned, 0) + (highest + zero)
     logden_ref[...] = jnp.broadcast_to(logden[None], logden_ref.shape)
-
-
-def last_message(logs, slot_rows, groups):
-    counted, every = logs[:slot_rows], logs[slot_rows:]
-    row, lane = iota(counted.shape, 0), iota(counted.shape, 1)
-    if slot_rows == SMALL_ROWS:
-        counted = jnp.where((row == slot_rows - 2) & (lane == LANES - 1), every[0, 0], counted)
-        return jnp.where(row == slot_rows - 1, every[:, None, :], counted[None])
-    return jnp.concatenate(
-        [
-            jnp.broadcast_to(counted[None], (groups, slot_rows, LANES)), every[:, None, :],
-            jnp.broadcast_to(every[0], (groups, 1, LANES)), jnp.zeros((groups, 6, LANES), F32),
-        ],
-        1,
-    )
 
 
 def iterated(slot_rows, meta, block_fill, mine, other, place, log_count, points):
@@ -459,16 +460,19 @@
         ],
         compiler_params=params, name="second",
     )(meta, block_fill, logs, mine, other, log_count, tiles, points, anchored, base)
-    logs = last_message(log_sum(exchanged(logs, SAMP)), slot_rows, groups)
+    logs = pl.pallas_call(
+        message_kernel,
+        out_shape=shape((groups, slot_rows if slot_rows == SMALL_ROWS else slot_rows + 8, LANES), F32),
+        in_specs=[vmem], out_specs=vmem, compiler_params=params, name="message",
+    )(exchanged(logs, SAMP))
     logs = exchanged(logs, STATE)
-    free, logden = pl.pallas_call(
+    return pl.pallas_call(
         third_kernel,
-        out_shape=(shape((8, LANES), F32), shape((groups, rows // LANES, LANES), F32)),
+        out_shape=(shape((1, LANES), F32), shape((groups, rows // LANES, LANES), F32)),
         in_specs=[smem] + [vmem] * 6, out_specs=(vmem, vmem),
         scratch_shapes=[tiles_work, weight_work, energy_work, column_work, column_work],
         compiler_params=params, name="third",
     )(meta, logs, log_count, tiles, points, anchored, base)
-    return free[0], exchanged(logden, STATE).reshape(-1)
 
 
 def shards(components, coefficients, block_window, block_fill):
@@ -507,11 +511,12 @@
     )(*pieces)
     total = meta[groups, 0]
     meta = jnp.concatenate([meta[: groups + 1, 0], spot[:1]])
-    return lax.cond(
+    free, logden = lax.cond(
         total <= SMALL,
         functools.partial(iterated, SMALL_ROWS), functools.partial(iterated, slot_rows),
         meta, block_fill, mine, other, place, log_count, points,
     )
+    return free.reshape(-1), exchanged(logden, STATE).reshape(-1)
 
 
 def solution(mesh):

time: 115 us -> 109 us (0.948)
  blocking collectives: 22.6 us -> 60.3 us
  waiting for transfers between devices: 32.4 us -> 6.42 us
  starting transfers between devices: 30.4 us -> 16.2 us
  local copies, waits for them, and re-layouts: 5.74 us -> 3.66 us
    all_to_all x2 -> x5, blocking collectives: 22.6 us -> 60.3 us  [exchanged(): return lax.all_to_all(copies, axes, split_axis=0, concat_axis=0, tiled=True)]
    all_to_all x4 -> x1, waiting for transfers between devices: 32.2 us -> 6.18 us  [exchanged(): return lax.all_to_all(copies, axes, split_axis=0, concat_axis=0, tiled=True)]
    all_to_all x4 -> x1, starting transfers between devices: 25.7 us -> 11.5 us  [exchanged(): return lax.all_to_all(copies, axes, split_axis=0, concat_axis=0, tiled=True)]
    pallas_call x1 -> x2, Pallas kernels: 2.98 us -> 2.69 us  [the longest x1 2.61 us: iterated(): pl.pallas_call(third_kernel, out_shape=(shape((1, LANES), F32), shape((gr...]
  transfers between devices with their start and end apart: 9 -> 6, of which waited for: 5 -> 2; matrix products, arithmetic and copies ran while one was open for 2% -> 2% of each run, Pallas kernels for 2% -> 2%
where the time goes in v5:
time: 109 us; the launch traced here: 108 us
  blocking collectives  60.3 us (55%)
  Pallas kernels  19 us (17%)
  starting transfers between devices  16.2 us (15%)
  waiting for transfers between devices  6.42 us (6%)
  local copies, waits for them, and re-layouts  3.66 us (3%)
  between operations  1.36 us (1%)
    all_to_all x5, blocking collectives, exchanged(): return lax.all_to_all(copies, axes, split_axis=0, concat_axis=0, tiled=True)  60.3 us
    all_to_all x1, starting transfers between devices, exchanged(): return lax.all_to_all(copies, axes, split_axis=0, concat_axis=0, tiled=True)  11.5 us
    pallas_call x1, Pallas kernels, iterated(): pl.pallas_call(second_kernel, out_shape=shape((samps, slot_rows + groups,...  9.11 us
    all_to_all x1, waiting for transfers between devices, exchanged(): return lax.all_to_all(copies, axes, split_axis=0, concat_axis=0, tiled=True)  6.18 us
    pallas_call x1, Pallas kernels, iterated(): pl.pallas_call(first_kernel, out_shape=(shape((samps, slot_rows, LANES),...  4.89 us
    ppermute x3, starting transfers between devices, shards(): pieces = [blocks] + [lax.ppermute(blocks, SAMP[0], turn) for turn in turns]  4.76 us
    pallas_call x1, Pallas kernels, iterated(): pl.pallas_call(third_kernel, out_shape=(shape((1, LANES), F32), shape((gr...  2.61 us
  transfers between devices with their start and end apart: 6, of which 2 were waited for; matrix products, arithmetic and copies ran while one was open for 2% of the time, Pallas kernels for 2%

profile of v5, /device:TPU:2, one launch (start us, length us, event | category | flops | bytes accessed | tf_op | source)
XLA Modules:
  0.0 108.0 jit_solution(16706134910801107457)
XLA Ops:
  0.6 0.0 copy-start
  0.7 0.7 copy-done
  1.4 0.7 broadcast_in_dim.15
  2.1 11.5 %all-to-all-start.8 = ((bf16[32,32,128]{2,1,0:T(8,128)(2,1)}), bf16[32,32,128]{2,1,0:T(8,128)(2,1)S(1)}, u32[]{:S(2)}, u32[]{:S(2)}) async-start(bf16[32,32,128]{2,1,0:T(8,128)(2,1)} %broadcast_in_dim.15), calls=%async_computation.8 | async-start | bytes 524288 | tf_op jit(solution)/shard_map/all_to_all | solution.py:31
  13.6 0.7 add_bitcast_fusion
  14.3 0.0 collective-permute-start
  14.3 0.9 constant_dynamic-slice_fusion.block_ref
  15.2 0.2 collective-permute-done
  15.5 0.5 collective-permute-start.3
  16.0 2.4 %collective-permute-start.2 = (s32[2,2,256]{2,1,0:T(2,128)S(1)}, s32[2,2,256]{2,1,0:T(2,128)S(1)}, u32[]{:S(2)}, u32[]{:S(2)}) collective-permute-start(s32[2,2,256]{2,1,0:T(2,128)S(1)} %pad_add_fusion.refs_0_), channel_id=1, source_target_pairs={{0,128},{64,192},{128,0},{192,64},{1,129},{65,193},{129,1},{193,65... | collective-permute-start | bytes 12296 | tf_op jit(solution)/shard_map/ppermute | solution.py:496
  18.4 1.8 %collective-permute-start.1 = (s32[2,2,256]{2,1,0:T(2,128)S(1)}, s32[2,2,256]{2,1,0:T(2,128)S(1)}, u32[]{:S(2)}, u32[]{:S(2)}) collective-permute-start(s32[2,2,256]{2,1,0:T(2,128)S(1)} %pad_add_fusion.refs_0_), channel_id=1, source_target_pairs={{0,64},{64,128},{128,192},{192,0},{1,65},{65,129},{129,193},{193,1... | collective-permute-start | bytes 12296 | tf_op jit(solution)/shard_map/ppermute | solution.py:496
  20.2 6.2 %all-to-all-done.8 = bf16[32,32,128]{2,1,0:T(8,128)(2,1)S(1)} async-done(((bf16[32,32,128]{2,1,0:T(8,128)(2,1)}), bf16[32,32,128]{2,1,0:T(8,128)(2,1)S(1)}, u32[]{:S(2)}, u32[]{:S(2)}) %all-to-all-start.8) | async-done | bytes 262176 | tf_op jit(solution)/shard_map/all_to_all | solution.py:31
  26.4 0.0 collective-permute-start.4
  26.4 0.1 pad_add_fusion.2.spot_ref
  26.5 0.7 points.1
  27.2 0.0 collective-permute-done.2.refs_2_
  27.2 0.0 collective-permute-done.1.refs_1_
  27.2 1.6 %count.1 = (s32[32,128]{1,0:T(8,128)S(1)}, s32[40,128]{1,0:T(8,128)S(1)}, f32[16,128]{1,0:T(8,128)S(1)}) custom-call(s32[2,2,256]{2,1,0:T(2,128)S(1)} %pad_add_fusion.refs_0_, s32[2,2,256]{2,1,0:T(2,128)S(1)} %collective-permute-done.1.refs_1_, s32[2,2,256]{2,1,0:T(2,128)S(1)} %collective-permute-done.2.refs_2_, s32[2,2,256]{2,1,0:T(2,128)S(1)} %collective-permute-done.3.refs_3_), custom_call_target="tpu_custom_call" | custom-call | tf_op jit(solution)/shard_map/count/pallas_call | solution.py:504
  28.8 0.5 slice.6
  29.9 0.1 slice_reduce_fusion
  30.1 0.1 pad_add_fusion.1
  30.1 63.5 %conditional.1 = (f32[32,8,128]{2,1,0:T(8,128)S(1)}, f32[128]{0:T(128)}) conditional(s32[]{:T(128)} %bitcast.5, (s32[34]{0:T(128)S(1)}, s32[256]{0:T(256)}, bf16[32,32,128]{2,1,0:T(8,128)(2,1)S(1)}, bf16[32,32,128]{2,1,0:T(8,128)(2,1)S(1)}, s32[32,128]{1,0:T(8,128)S(1)}, /*index=5*/f32[16,128]{1,0:T(8,128)S(1)}, ...), branch_computations={%region_0.0_spmd, %region_3.0_spmd} | conditional | flops 47104 | bytes 2285588 | solution.py:514
  30.3 4.9 %first.3 = (f32[8,8,128]{2,1,0:T(8,128)S(1)}, bf16[4,128,256]{2,1,0:T(8,128)(2,1)S(1)}, bf16[1024,128]{1,0:T(8,128)(2,1)S(1)}, f32[1024,128]{1,0:T(8,128)S(1)}) custom-call(s32[34]{0:T(128)S(1)} %get-tuple-element.46.meta_ref, s32[256]{0:T(256)} %get-tuple-element.47.fill_ref, bf16[32,32,128]{2,1,0:T(8,128)(2,1)S(1)} %get-tuple-element.48.mine_ref, ...), custom_call_target="tpu_custom_call" | custom-call | tf_op jit(solution)/shard_map/cond/branch_1_fun/first/pallas_call | solution.py:438
  35.2 8.7 %all_to_all.46 = f32[8,8,128]{2,1,0:T(8,128)S(1)} all-to-all(f32[8,8,128]{2,1,0:T(8,128)S(1)} %get-tuple-element.53), channel_id=1, replica_groups=mesh['samp_0'=4,'samp_1'=2,'state_0'=8,'state_1'=4] {'samp_0','samp_1'}, dimensions={0} | all-to-all | bytes 65536 | tf_op jit(solution)/shard_map/cond/branch_1_fun/all_to_all | solution.py:31
  44.0 15.1 %all_to_all.47.logs_in_ref = f32[32,8,128]{2,1,0:T(8,128)S(1)} all-to-all(f32[32,8,128]{2,1,0:T(8,128)S(1)} %broadcast_in_dim.2), channel_id=1, replica_groups=mesh['samp_0'=4,'samp_1'=2,'state_0'=8,'state_1'=4] {'state_0','state_1'}, dimensions={0} | all-to-all | bytes 262144 | tf_op jit(solution)/shard_map/cond/branch_1_fun/all_to_all | solution.py:31
  59.1 9.1 %second.3 = f32[8,40,128]{2,1,0:T(8,128)S(1)} custom-call(s32[34]{0:T(128)S(1)} %get-tuple-element.46.meta_ref, s32[256]{0:T(256)} %get-tuple-element.47.fill_ref, f32[32,8,128]{2,1,0:T(8,128)S(1)} %all_to_all.47.logs_in_ref, bf16[32,32,128]{2,1,0:T(8,128)(2,1)S(1)} %get-tuple-element.48.mine_ref, bf16[32,32,128]{2,1,0:T(8,128)(2,1)S(1)} %get-tuple-element.49.other_ref, ...), custom_call_target="tpu_custom_call" | custom-call | tf_op jit(solution)/shard_map/cond/branch_1_fun/second/pallas_call | solution.py:453
  68.2 8.8 %all_to_all.48.logs_ref = f32[8,40,128]{2,1,0:T(8,128)S(1)} all-to-all(f32[8,40,128]{2,1,0:T(8,128)S(1)} %second.3), channel_id=1, replica_groups=mesh['samp_0'=4,'samp_1'=2,'state_0'=8,'state_1'=4] {'samp_0','samp_1'}, dimensions={0} | all-to-all | bytes 327680 | tf_op jit(solution)/shard_map/cond/branch_1_fun/all_to_all | solution.py:31
  77.1 0.1 message.3
  77.1 13.8 %all_to_all.49.logs_in_ref = f32[32,8,128]{2,1,0:T(8,128)S(1)} all-to-all(f32[32,8,128]{2,1,0:T(8,128)S(1)} %message.3), channel_id=1, replica_groups=mesh['samp_0'=4,'samp_1'=2,'state_0'=8,'state_1'=4] {'state_0','state_1'}, dimensions={0} | all-to-all | bytes 262144 | tf_op jit(solution)/shard_map/cond/branch_1_fun/all_to_all | solution.py:31
  91.0 2.6 %third.3 = (f32[1,128]{1,0:T(1,128)}, f32[32,8,128]{2,1,0:T(8,128)S(1)}) custom-call(s32[34]{0:T(128)S(1)} %get-tuple-element.46.meta_ref, f32[32,8,128]{2,1,0:T(8,128)S(1)} %all_to_all.49.logs_in_ref, f32[16,128]{1,0:T(8,128)S(1)} %get-tuple-element.51.log_count_ref, bf16[4,128,256]{2,1,0:T(8,128)(2,1)S(1)} %get-tuple-element.54.tiles_in_ref, ...), custom_call_target="tpu_custom_call" | custom-call | tf_op jit(solution)/shard_map/cond/branch_1_fun/third/pallas_call | solution.py:469
  93.6 13.8 %all_to_all.50 = f32[32,8,128]{2,1,0:T(8,128)S(1)} all-to-all(f32[32,8,128]{2,1,0:T(8,128)S(1)} %get-tuple-element.70), channel_id=1, replica_groups=mesh['samp_0'=4,'samp_1'=2,'state_0'=8,'state_1'=4] {'state_0','state_1'}, dimensions={0} | all-to-all | bytes 262144 | tf_op jit(solution)/shard_map/all_to_all | solution.py:31
  107.4 0.7 copy.11
  (8 shorter events, 0.1 us)
Async XLA Ops:
  0.6 0.7 copy-start
  2.1 24.3 %all-to-all-start.8 = ((bf16[32,32,128]{2,1,0:T(8,128)(2,1)}), bf16[32,32,128]{2,1,0:T(8,128)(2,1)S(1)}, u32[]{:S(2)}, u32[]{:S(2)}) async-start(bf16[32,32,128]{2,1,0:T(8,128)(2,1)} %broadcast_in_dim.15), calls=%async_computation.8 | async-start | bytes 524288 | tf_op jit(solution)/shard_map/all_to_all | solution.py:31
  14.3 1.2 %collective-permute-start = (s32[1,2,256]{2,1,0:T(2,128)S(1)}, s32[1,2,256]{2,1,0:T(2,128)S(1)}, u32[]{:S(2)}, u32[]{:S(2)}) collective-permute-start(s32[1,2,256]{2,1,0:T(2,128)S(1)} %add_bitcast_fusion), channel_id=1, source_target_pairs={{0,32},{32,0},{1,33},{33,1},{2,34},{34,2},{3,35},{35,3},{4,36},{36... | collective-permute-start | bytes 6152 | tf_op jit(solution)/shard_map/ppermute | solution.py:493
  15.5 11.7 %collective-permute-start.3 = (s32[2,2,256]{2,1,0:T(2,128)S(1)}, s32[2,2,256]{2,1,0:T(2,128)S(1)}, u32[]{:S(2)}, u32[]{:S(2)}) collective-permute-start(s32[2,2,256]{2,1,0:T(2,128)S(1)} %pad_add_fusion.refs_0_), channel_id=1, source_target_pairs={{0,192},{64,0},{128,64},{192,128},{1,193},{65,1},{129,65},{193,129... | collective-permute-start | bytes 12296 | tf_op jit(solution)/shard_map/ppermute | solution.py:496
  16.0 11.2 %collective-permute-start.2 = (s32[2,2,256]{2,1,0:T(2,128)S(1)}, s32[2,2,256]{2,1,0:T(2,128)S(1)}, u32[]{:S(2)}, u32[]{:S(2)}) collective-permute-start(s32[2,2,256]{2,1,0:T(2,128)S(1)} %pad_add_fusion.refs_0_), channel_id=1, source_target_pairs={{0,128},{64,192},{128,0},{192,64},{1,129},{65,193},{129,1},{193,65... | collective-permute-start | bytes 12296 | tf_op jit(solution)/shard_map/ppermute | solution.py:496
  18.4 8.8 %collective-permute-start.1 = (s32[2,2,256]{2,1,0:T(2,128)S(1)}, s32[2,2,256]{2,1,0:T(2,128)S(1)}, u32[]{:S(2)}, u32[]{:S(2)}) collective-permute-start(s32[2,2,256]{2,1,0:T(2,128)S(1)} %pad_add_fusion.refs_0_), channel_id=1, source_target_pairs={{0,64},{64,128},{128,192},{192,0},{1,65},{65,129},{129,193},{193,1... | collective-permute-start | bytes 12296 | tf_op jit(solution)/shard_map/ppermute | solution.py:496
  26.4 3.7 %collective-permute-start.4 = (bf16[32,32,128]{2,1,0:T(8,128)(2,1)S(1)}, bf16[32,32,128]{2,1,0:T(8,128)(2,1)S(1)}, u32[]{:S(2)}, u32[]{:S(2)}) collective-permute-start(bf16[32,32,128]{2,1,0:T(8,128)(2,1)S(1)} %all-to-all-done.8), channel_id=1, source_target_pairs={{0,32},{32,0},{1,33},{33,1},{2,34},{34,2},{3,35},{35,3},{4,36},{36... | collective-permute-start | bytes 786440 | tf_op jit(solution)/shard_map/ppermute | solution.py:503

commit v6 on v5

v6 whole, which is shorter than its diff:
```python
import functools

import jax
import jax.numpy as jnp
from jax import lax
from jax.experimental import pallas as pl
from jax.experimental.pallas import tpu as pltpu
from jax.sharding import Mesh
from jax.sharding import PartitionSpec as P


BLOCK = 128
LANES = 128
COMP = 64
TILE = 256
PARTS = 3
LOG2E = 1.4426950408889634
LN2 = 0.6931471805599453
CHUNK = 512
TAIL = 16
LEAST = 1e-25
SPREAD = 72.0
SMALL_ROWS = 8
SMALL = (SMALL_ROWS - 1) * LANES - 1
STATE = ("state_0", "state_1")
SAMP = ("samp_0", "samp_1")
NEGATIVE = -1e30
BF16 = jnp.bfloat16
F32 = jnp.float32


def exchanged(copies, axes):
    return lax.all_to_all(copies, axes, split_axis=0, concat_axis=0, tiled=True)


def copies_of_each(x, axes):
    return exchanged(jnp.broadcast_to(x, (lax.axis_size(axes), *x.shape)), axes)


def iota(shape, dim):
    return lax.broadcasted_iota(jnp.int32, shape, dim)


def dot_nt(a, b):
    return lax.dot_general(a, b, (((1,), (1,)), ((), ())), preferred_element_type=F32)


def dot(a, b):
    return jnp.dot(a, b, preferred_element_type=F32)


def three_parts(x):
    high = x.astype(BF16).astype(F32)
    rest = x - high
    middle = rest.astype(BF16).astype(F32)
    return high, middle, rest - middle


def log_sum(logs):
    highest = jnp.max(logs, axis=0)
    return highest + jnp.log(jnp.sum(jnp.exp(logs - highest[None]), axis=0))


def log_sum_pieces(logs_ref):
    pieces = logs_ref.shape[0]
    highest = functools.reduce(jnp.maximum, [logs_ref[p] for p in range(pieces)])
    totals = functools.reduce(jnp.add, [jnp.exp(logs_ref[p] - highest) for p in range(pieces)])
    return highest + jnp.log(totals)


def chunk(c):
    return pl.ds(c * CHUNK if isinstance(c, int) else pl.multiple_of(c * CHUNK, CHUNK), CHUNK)


def halves(combine, x):
    return combine(x[:, :LANES], x[:, LANES:])


def points_kernel(spot_ref, block_ref, head_ref, points_ref):
    rows = points_ref.shape[0]
    half = COMP // 2
    own = pl.multiple_of(spot_ref[1] * half, half)
    lane = iota((LANES, LANES - COMP), 1)
    ones = jnp.where((lane >= 3) & (lane < 6), 1.0, 0.0)
    for b in range(rows // LANES):
        at = slice(b * LANES, (b + 1) * LANES)
        mine = block_ref[pl.ds(own, half), at].astype(F32)
        other = block_ref[pl.ds(pl.multiple_of(half - own, half), half), at].astype(F32)
        high, middle, low = three_parts(jnp.concatenate([mine, other], 0).T * -LOG2E)
        head_ref[at, :] = jnp.concatenate([high, middle], 1).astype(BF16)
        points_ref[at, :] = jnp.concatenate([low, ones], 1).astype(BF16)


def count_kernel(*refs):
    blocks_refs, (place_ref, meta_ref, log_count_ref) = refs[:-3], refs[-3:]
    groups = place_ref.shape[0]
    slots = log_count_ref.shape[0]
    width = blocks_refs[0].shape[2]
    counts = jnp.zeros((groups, LANES), F32)
    for blocks_ref, s in [(r, s) for r in blocks_refs for s in range(r.shape[0])]:
        window = blocks_ref[s, 0:1, :]
        fill = blocks_ref[s, 1:2, :]
        of_group = jnp.where(iota((groups, width), 0) == window >> 7, fill, 0).astype(F32).astype(BF16)
        of_lane = jnp.where(iota((LANES, width), 0) == (window & 127), 1.0, 0.0).astype(BF16)
        counts = counts + dot_nt(of_group, of_lane)
    counted = counts > 0
    packed = jnp.where(counted, 1.0, 0.0).astype(BF16)
    before = jnp.where(iota((LANES, LANES), 0) < iota((LANES, LANES), 1), 1.0, 0.0).astype(BF16)
    within = dot(packed, before)
    total = dot(packed, jnp.ones((LANES, LANES), BF16))
    earlier = jnp.where(iota((groups, groups), 1) < iota((groups, groups), 0), 1.0, 0.0).astype(BF16)
    offset_int = dot(earlier, total.astype(BF16)).astype(jnp.int32)
    within_int = within.astype(jnp.int32)
    place_ref[...] = jnp.where(counted, (offset_int & 127) + within_int, -1)
    meta_ref[0:groups, :] = offset_int >> 7
    everything = jnp.sum(total, axis=0, keepdims=True).astype(jnp.int32)
    meta_ref[groups : groups + 8, :] = jnp.broadcast_to(everything, (8, LANES))
    whole = jnp.where(counted, offset_int + within_int, -1)
    counts_int = counts.astype(jnp.int32)
    digits = (counts_int >> 14, (counts_int >> 7) & 127, counts_int & 127)
    gathered = jnp.zeros((3 * slots, LANES), F32)
    for t in range(groups):
        row = whole[t : t + 1, :]
        slot = iota((slots, LANES), 0) == row >> 7
        parts = [jnp.where(slot, d[t : t + 1, :], 0).astype(F32) for d in digits]
        of_lane = jnp.where(iota((LANES, LANES), 0) == (row & 127), 1.0, 0.0).astype(BF16)
        gathered = gathered + dot_nt(jnp.concatenate(parts, 0).astype(BF16), of_lane)
    compact = gathered[0:slots] * 16384.0 + gathered[slots : 2 * slots] * 128.0 + gathered[2 * slots :]
    log_count_ref[...] = jnp.where(compact > 0, jnp.log2(jnp.maximum(compact, 1.0)), NEGATIVE)


def tail_rows(weight):
    row = iota((TAIL, TILE), 0)
    rows = jnp.where(row < 3, 1.0, 0.0)
    if weight is not None:
        for k, part in enumerate(three_parts(weight)):
            rows = jnp.where(row == 3 + k, part, rows)
    return jnp.concatenate([rows.astype(BF16), jnp.zeros((LANES - COMP - TAIL, TILE), BF16)], 0)


def whole_tile(coefs, tail):
    return jnp.concatenate([coefs] * PARTS + [tail], 0)


def against(head_ref, points_ref, c, tile):
    return dot(jnp.concatenate([head_ref[chunk(c), :], points_ref[chunk(c), :]], 1), tile)


def with_shift(points, shift):
    lane = iota(points.shape, 1)
    for k, part in enumerate(three_parts(shift)):
        points = jnp.where(lane == COMP + k, part, points)
    return points


def tile_row(rows, j):
    return jnp.concatenate([rows[2 * j : 2 * j + 1, :], rows[2 * j + 1 : 2 * j + 2, :]], 1)


def over_tiles(tile_count, pairs, body, carry):
    if tile_count * TILE == SMALL_ROWS * LANES:
        for j in range(tile_count):
            carry = body(j, carry)
        return carry
    return lax.fori_loop(0, 2 * pairs, body, carry)


def exact_denominators(c, head_ref, points_ref, coefs_ref, tails_ref, pairs, energy_ref):
    def find(j, top):
        exponents = against(head_ref, points_ref, c, whole_tile(coefs_ref[j], tails_ref[j]))
        energy_ref[j] = exponents
        return jnp.maximum(top, halves(jnp.maximum, exponents))

    tile_count = coefs_ref.shape[0]
    top = over_tiles(tile_count, pairs, find, jnp.full((CHUNK, LANES), 4 * NEGATIVE, F32))
    top = jnp.max(top, axis=1, keepdims=True)

    def add(j, sums):
        return sums + halves(jnp.add, jnp.exp2(energy_ref[j] - top))

    sums = over_tiles(tile_count, pairs, add, jnp.zeros((CHUNK, LANES), F32))
    return jnp.broadcast_to(top + jnp.log2(jnp.sum(sums, axis=1, keepdims=True)), (CHUNK, LANES))


def near_denominators(c, base_ref, head_ref, anchored_ref, coefs_ref, tails_ref, pairs):
    def add(j, sums):
        tile = whole_tile(coefs_ref[j], tails_ref[j])
        return sums + halves(jnp.add, jnp.exp2(against(head_ref, anchored_ref, c, tile)))

    sums = over_tiles(coefs_ref.shape[0], pairs, add, jnp.zeros((CHUNK, LANES), F32))
    return base_ref[chunk(c), :] + jnp.log2(jnp.sum(sums, axis=1, keepdims=True))


def put_live(c, points_ref, logden, live_ref, fill_ref, first_block):
    row = iota((BLOCK, LANES), 0)
    for b in range(CHUNK // BLOCK):
        at = pl.ds(pl.multiple_of(c * CHUNK + b * BLOCK, BLOCK), BLOCK)
        here = -logden[b * BLOCK : (b + 1) * BLOCK, :]
        shift = jnp.where(row < fill_ref[first_block + c * (CHUNK // BLOCK) + b], here, NEGATIVE)
        live_ref[at, :] = with_shift(points_ref[at, :].astype(F32), shift).astype(BF16)


def each_chunk(rows, body):
    def one(c, carry):
        body(c)
        return carry

    lax.fori_loop(0, rows // CHUNK, one, 0)


def exponents_and_highest(tile, head_ref, live_ref, exponent_ref):
    highest = None
    for c in range(live_ref.shape[0] // CHUNK):
        exponents = against(head_ref, live_ref, c, tile)
        exponent_ref[chunk(c), :] = exponents
        top = jnp.max(exponents.reshape(CHUNK // 8, 8, TILE), axis=0)
        highest = top if highest is None else jnp.maximum(highest, top)
    return jnp.max(highest, axis=0, keepdims=True)


def log_of_sum(highest, exponent_ref):
    totals = jnp.zeros((8, TILE), F32)
    for c in range(exponent_ref.shape[0] // CHUNK):
        grown = jnp.exp2(exponent_ref[chunk(c), :] - highest)
        totals = totals + jnp.sum(grown.reshape(CHUNK // 8, 8, TILE), axis=0)
    return highest + jnp.log2(jnp.sum(totals, axis=0, keepdims=True))


def put_rows(logs_ref, first, logs):
    logs = logs * LN2
    logs_ref[pl.ds(first, 1), :] = logs[:, :LANES]
    logs_ref[pl.ds(first + 1, 1), :] = logs[:, LANES:]


def counted_log_sums(total, weight_ref, coefs_ref, tails_ref, pairs, head_ref, live_ref, exponent_ref, logs_ref, low_ref):
    low_ref[...] = jnp.zeros(low_ref.shape, F32)
    logs_ref[0 : weight_ref.shape[0], :] = jnp.zeros(weight_ref.shape, F32)

    def finish(j, logs):
        weight = jnp.concatenate([weight_ref[pl.ds(2 * j, 1), :], weight_ref[pl.ds(2 * j + 1, 1), :]], 1)
        valid = iota((1, TILE), 1) < total - j * TILE
        put_rows(logs_ref, 2 * j, jnp.where(valid, logs - weight, 0.0))
        return valid

    def one(i, carry):
        for k in range(2):
            j = 2 * i + k
            totals = jnp.zeros((8, TILE), F32)
            tile = whole_tile(coefs_ref[j], tails_ref[j])
            for c in range(live_ref.shape[0] // CHUNK):
                grown = jnp.exp2(against(head_ref, live_ref, c, tile))
                totals = totals + jnp.sum(grown.reshape(CHUNK // 8, 8, TILE), axis=0)
            totals = jnp.sum(totals, axis=0, keepdims=True)
            valid = finish(j, jnp.log2(totals))
            low_ref[0:1, :] = jnp.maximum(low_ref[0:1, :], jnp.where(valid & (totals < LEAST), 1.0, 0.0))
        return carry

    lax.fori_loop(0, pairs, one, 0)

    @pl.when(jnp.max(low_ref[...]) > 0)
    def _():
        def again(j, carry):
            highest = exponents_and_highest(whole_tile(coefs_ref[j], tails_ref[j]), head_ref, live_ref, exponent_ref)
            finish(j, log_of_sum(highest, exponent_ref))
            return carry

        lax.fori_loop(0, 2 * pairs, again, 0)


def weighted_tails(total, logs, log_count_ref, tails_ref, weight_ref):
    valid = iota(logs.shape, 0) * LANES + iota(logs.shape, 1) < total
    free = jnp.where(valid, logs * -LOG2E, 4 * NEGATIVE)
    highest = jnp.max(jnp.max(free, axis=0, keepdims=True), axis=1, keepdims=True)
    free = jnp.where(valid, free - highest, 0.0)
    weight = log_count_ref[0 : weight_ref.shape[0], :] + free
    weight_ref[...] = weight
    for j in range(tails_ref.shape[0]):
        tails_ref[j] = tail_rows(tile_row(weight, j))
    return highest, jnp.min(free)


def first_kernel(
    meta_ref, fill_ref, mine_ref, other_ref, place_ref, log_count_ref, head_ref, points_ref,
    logs_ref, coefs_ref, anchored_ref, base_ref,
    tails_ref, packed_ref, energy_ref, live_ref, exponent_ref, low_ref, rows_ref, weight_ref,
):
    groups = mine_ref.shape[0]
    total = meta_ref[groups]
    pairs = (total + 2 * TILE - 1) // (2 * TILE)
    packed_ref[...] = jnp.zeros(packed_ref.shape, F32)
    for t in range(groups):
        chosen = jnp.where(iota((2 * LANES, LANES), 0) == place_ref[t : t + 1, :], 1.0, 0.0).astype(BF16)
        moved = dot_nt(jnp.concatenate([mine_ref[t], other_ref[t]], 0), chosen)
        at = meta_ref[t]
        packed_ref[at] += moved[:, :LANES]
        packed_ref[at + 1] += moved[:, LANES:]
    log_count = log_count_ref[0 : logs_ref.shape[1], :]
    weight_ref[...] = log_count
    for j in range(coefs_ref.shape[0]):
        coefs_ref[j] = jnp.concatenate([packed_ref[2 * j], packed_ref[2 * j + 1]], 1).astype(BF16)
        tails_ref[j] = tail_rows(tile_row(log_count, j))
    first_block = meta_ref[groups + 1] * (points_ref.shape[0] // BLOCK)

    def denominators(c):
        logden = exact_denominators(c, head_ref, points_ref, coefs_ref, tails_ref, pairs, energy_ref)
        base_ref[chunk(c), :] = logden
        anchored_ref[chunk(c), :] = with_shift(points_ref[chunk(c), :].astype(F32), -logden).astype(BF16)
        put_live(c, points_ref, logden, live_ref, fill_ref, first_block)

    each_chunk(points_ref.shape[0], denominators)
    counted_log_sums(
        total, weight_ref, coefs_ref, tails_ref, pairs, head_ref, live_ref, exponent_ref, rows_ref, low_ref
    )
    logs_ref[...] = jnp.broadcast_to(rows_ref[...][None], logs_ref.shape)


def new_denominators(least, base_ref, head_ref, anchored_ref, points_ref, coefs_ref, tails_ref, pairs, energy_ref, put):
    rows = points_ref.shape[0]
    near = least > -SPREAD

    @pl.when(near)
    def _():
        each_chunk(
            rows,
            lambda c: put(c, near_denominators(c, base_ref, head_ref, anchored_ref, coefs_ref, tails_ref, pairs)),
        )

    @pl.when(jnp.logical_not(near))
    def _():
        each_chunk(
            rows, lambda c: put(c, exact_denominators(c, head_ref, points_ref, coefs_ref, tails_ref, pairs, energy_ref))
        )


def second_kernel(
    meta_ref, fill_ref, logs_in_ref, mine_ref, other_ref, log_count_ref, coefs_ref, head_ref, points_ref, anchored_ref,
    base_ref,
    logs_ref,
    tails_ref, weight_ref, energy_ref, live_ref, exponent_ref, low_ref, rows_ref,
):
    groups = mine_ref.shape[0]
    slot_rows = weight_ref.shape[0]
    total = meta_ref[groups]
    pairs = (total + 2 * TILE - 1) // (2 * TILE)
    logs = log_sum_pieces(logs_in_ref)
    _, least = weighted_tails(total, logs, log_count_ref, tails_ref, weight_ref)
    first_block = meta_ref[groups + 1] * (points_ref.shape[0] // BLOCK)
    new_denominators(
        least, base_ref, head_ref, anchored_ref, points_ref, coefs_ref, tails_ref, pairs, energy_ref,
        lambda c, logden: put_live(c, points_ref, logden, live_ref, fill_ref, first_block),
    )
    counted_log_sums(
        total, weight_ref, coefs_ref, tails_ref, pairs, head_ref, live_ref, exponent_ref, rows_ref, low_ref
    )
    tail = tail_rows(None)
    last = groups * LANES // TILE - 1

    def every_tile(t):
        parts = [jnp.concatenate([mine_ref[2 * t + k], other_ref[2 * t + k]], 0) for k in range(2)]
        return whole_tile(jnp.concatenate(parts, 1), tail)

    def step(t, highest):
        tile = every_tile(jnp.minimum(t + 1, last))
        totals = jnp.zeros((8, TILE), F32)
        tops = []
        for c in range(live_ref.shape[0] // CHUNK):
            grown = jnp.exp2(exponent_ref[chunk(c), :] - highest)
            totals = totals + jnp.sum(grown.reshape(CHUNK // 8, 8, TILE), axis=0)
            exponents = against(head_ref, live_ref, c, tile)
            exponent_ref[chunk(c), :] = exponents
            tops.append(jnp.max(exponents.reshape(CHUNK // 8, 8, TILE), axis=0))
        logs = highest + jnp.log2(jnp.sum(totals, axis=0, keepdims=True))
        put_rows(rows_ref, slot_rows + 2 * t, logs)
        return jnp.max(functools.reduce(jnp.maximum, tops), axis=0, keepdims=True)

    start = exponents_and_highest(every_tile(0), head_ref, live_ref, exponent_ref)
    lax.fori_loop(0, last + 1, step, start, unroll=2)
    logs_ref[...] = jnp.broadcast_to(rows_ref[...][None], logs_ref.shape)


def message_kernel(logs_ref, message_ref):
    groups = message_ref.shape[0]
    slot_rows = logs_ref.shape[1] - groups
    (own_row, zero_row), zero_lane = places(slot_rows)
    logs = log_sum_pieces(logs_ref)
    rows = message_ref.shape[1]
    common = logs[0:slot_rows, :]
    if rows > slot_rows:
        common = jnp.concatenate([common, jnp.zeros((rows - slot_rows, LANES), F32)], 0)
    row, lane = iota(common.shape, 0), iota(common.shape, 1)
    common = jnp.where((row == zero_row) & (lane == zero_lane), logs[slot_rows : slot_rows + 1, 0:1], common)
    for t in range(groups):
        own = logs[slot_rows + t : slot_rows + t + 1, :]
        message_ref[t] = jnp.where(row == own_row, own, common)


def places(slot_rows):
    if slot_rows == SMALL_ROWS:
        return (slot_rows - 1, slot_rows - 2), LANES - 1
    return (slot_rows, slot_rows + 1), 0


def third_kernel(
    meta_ref, logs_in_ref, log_count_ref, coefs_ref, head_ref, points_ref, anchored_ref, base_ref,
    free_ref, logden_ref,
    tails_ref, weight_ref, energy_ref, totals_ref,
):
    copies = logden_ref.shape[0]
    slot_rows = weight_ref.shape[0]
    total = meta_ref[copies]
    pairs = (total + 2 * TILE - 1) // (2 * TILE)
    logs = log_sum_pieces(logs_in_ref)
    (own_row, zero_row), zero_lane = places(slot_rows)
    zero = logs[zero_row : zero_row + 1, zero_lane : zero_lane + 1]
    free_ref[...] = zero - logs[own_row : own_row + 1, :]
    highest, least = weighted_tails(total, logs[:slot_rows], log_count_ref, tails_ref, weight_ref)

    def put(c, logden):
        totals_ref[chunk(c), :] = logden

    new_denominators(
        least, base_ref, head_ref, anchored_ref, points_ref, coefs_ref, tails_ref, pairs, energy_ref, put
    )
    turned = [totals_ref[pl.ds(b * LANES, LANES), :].T[0:1, :] for b in range(points_ref.shape[0] // LANES)]
    logden = (jnp.concatenate(turned, 0) + highest) * LN2 + zero
    logden_ref[...] = jnp.broadcast_to(logden[None], logden_ref.shape)


def iterated(slot_rows, meta, block_fill, mine, other, place, log_count, head, points):
    samps = lax.axis_size(SAMP)
    groups = mine.shape[0]
    rows = points.shape[0]
    tile_count = slot_rows * LANES // TILE
    shape = jax.ShapeDtypeStruct
    vmem = pl.BlockSpec(memory_space=pltpu.VMEM)
    smem = pl.BlockSpec(memory_space=pltpu.SMEM)
    params = pltpu.CompilerParams(vmem_limit_bytes=24 << 20)
    tails_work = pltpu.VMEM((tile_count, LANES - COMP, TILE), BF16)
    weight_work = pltpu.VMEM((slot_rows, LANES), F32)
    energy_work = pltpu.VMEM((tile_count, CHUNK, TILE), F32)
    live_work = pltpu.VMEM((rows, LANES), BF16)
    exponent_work = pltpu.VMEM((rows, TILE), F32)
    low_work = pltpu.VMEM((8, TILE), F32)
    logs, coefs, anchored, base = pl.pallas_call(
        first_kernel,
        out_shape=(
            shape((samps, slot_rows, LANES), F32), shape((tile_count, COMP, TILE), BF16), shape((rows, LANES), BF16),
            shape((rows, LANES), F32),
        ),
        in_specs=[smem, smem] + [vmem] * 6, out_specs=(vmem,) * 4,
        scratch_shapes=[
            tails_work, pltpu.VMEM((slot_rows + 2, COMP, LANES), F32), energy_work, live_work, exponent_work, low_work,
            weight_work, weight_work,
        ],
        compiler_params=params, name="first",
    )(meta, block_fill, mine, other, place, log_count, head, points)
    logs = log_sum(exchanged(logs, SAMP))
    logs = copies_of_each(logs, STATE)
    logs = pl.pallas_call(
        second_kernel,
        out_shape=shape((samps, slot_rows + groups, LANES), F32),
        in_specs=[smem, smem] + [vmem] * 9, out_specs=vmem,
        scratch_shapes=[
            tails_work, weight_work, energy_work, live_work, exponent_work,
            low_work, pltpu.VMEM((slot_rows + groups, LANES), F32),
        ],
        compiler_params=params, name="second",
    )(meta, block_fill, logs, mine, other, log_count, coefs, head, points, anchored, base)
    logs = pl.pallas_call(
        message_kernel,
        out_shape=shape((groups, slot_rows if slot_rows == SMALL_ROWS else slot_rows + 8, LANES), F32),
        in_specs=[vmem], out_specs=vmem, compiler_params=params, name="message",
    )(exchanged(logs, SAMP))
    logs = exchanged(logs, STATE)
    return pl.pallas_call(
        third_kernel,
        out_shape=(shape((1, LANES), F32), shape((groups, rows // LANES, LANES), F32)),
        in_specs=[smem] + [vmem] * 7, out_specs=(vmem, vmem),
        scratch_shapes=[tails_work, weight_work, energy_work, pltpu.VMEM((rows, LANES), F32)],
        compiler_params=params, name="third",
    )(meta, logs, log_count, coefs, head, points, anchored, base)


def shards(components, coefficients, block_window, block_fill):
    groups = lax.axis_size(STATE)
    samps = lax.axis_size(SAMP)
    position = lax.axis_index(STATE)
    core = lax.axis_index(SAMP[1])
    rows = components.shape[1] // groups
    slot_rows = min(samps * block_window.shape[0] // LANES, groups)
    shape = jax.ShapeDtypeStruct
    vmem = pl.BlockSpec(memory_space=pltpu.VMEM)
    params = pltpu.CompilerParams(vmem_limit_bytes=24 << 20)
    spot = jnp.stack([position, core]).astype(jnp.int32)

    half = COMP // 2
    mine = copies_of_each(lax.dynamic_slice_in_dim(coefficients, core * half, half, 0), STATE)
    blocks = jnp.stack([block_window, block_fill])[None]
    blocks = jnp.concatenate([blocks, lax.ppermute(blocks, SAMP[1], [(0, 1), (1, 0)])], 0)
    along = lax.axis_size(SAMP[0])
    turns = [[(i, (i + k) % along) for i in range(along)] for k in range(1, along)]
    pieces = [blocks] + [lax.ppermute(blocks, SAMP[0], turn) for turn in turns]
    head, points = pl.pallas_call(
        points_kernel,
        out_shape=(shape((rows, LANES), BF16), shape((rows, LANES), BF16)),
        in_specs=[pl.BlockSpec(memory_space=pltpu.SMEM), vmem], out_specs=(vmem, vmem),
        compiler_params=params, name="points",
    )(spot, lax.dynamic_slice_in_dim(components, position * rows, rows, 1))
    other = lax.ppermute(mine, SAMP[1], [(0, 1), (1, 0)])
    place, meta, log_count = pl.pallas_call(
        count_kernel,
        out_shape=(
            shape((groups, LANES), jnp.int32), shape((groups + 8, LANES), jnp.int32),
            shape((slot_rows, LANES), F32),
        ),
        in_specs=[vmem] * len(pieces), out_specs=(vmem, vmem, vmem), compiler_params=params, name="count",
    )(*pieces)
    total = meta[groups, 0]
    meta = jnp.concatenate([meta[: groups + 1, 0], spot[:1]])
    free, logden = lax.cond(
        total <= SMALL,
        functools.partial(iterated, SMALL_ROWS), functools.partial(iterated, slot_rows),
        meta, block_fill, mine, other, place, log_count, head, points,
    )
    return free.reshape(-1), exchanged(logden, STATE).reshape(-1)


def solution(mesh):
    torus = Mesh(mesh.devices.reshape(4, 2, 8, 4), ("samp_0", "samp_1", "state_0", "state_1"))
    placed = (P(None, SAMP), P(None, STATE), P(SAMP), P(SAMP))
    return jax.shard_map(
        shards, mesh=torus, in_specs=placed, out_specs=(P(STATE), P(SAMP)), check_vma=False
    )
```

time: 109 us -> 106 us (0.972)
  Pallas kernels: 19 us -> 16.5 us
    pallas_call x1, Pallas kernels: 9.11 us -> 7.2 us  [iterated(): pl.pallas_call(second_kernel, out_shape=shape((samps, slot_rows + groups,...]
where the time goes in v6:
time: 106 us; the launch traced here: 105 us
  blocking collectives  60.2 us (57%)
  Pallas kernels  16.5 us (16%)
  starting transfers between devices  16.2 us (15%)
  waiting for transfers between devices  6.42 us (6%)
  local copies, waits for them, and re-layouts  3.65 us (3%)
  between operations  1.36 us (1%)
    all_to_all x5, blocking collectives, exchanged(): return lax.all_to_all(copies, axes, split_axis=0, concat_axis=0, tiled=True)  60.2 us
    all_to_all x1, starting transfers between devices, exchanged(): return lax.all_to_all(copies, axes, split_axis=0, concat_axis=0, tiled=True)  11.5 us
    pallas_call x1, Pallas kernels, iterated(): pl.pallas_call(second_kernel, out_shape=shape((samps, slot_rows + groups,...  7.2 us
    all_to_all x1, waiting for transfers between devices, exchanged(): return lax.all_to_all(copies, axes, split_axis=0, concat_axis=0, tiled=True)  6.18 us
    ppermute x3, starting transfers between devices, shards(): pieces = [blocks] + [lax.ppermute(blocks, SAMP[0], turn) for turn in turns]  4.76 us
    pallas_call x1, Pallas kernels, iterated(): pl.pallas_call(first_kernel, out_shape=(shape((samps, slot_rows, LANES),...  4.36 us
    pallas_call x1, Pallas kernels, iterated(): pl.pallas_call(third_kernel, out_shape=(shape((1, LANES), F32), shape((gr...  2.44 us
  transfers between devices with their start and end apart: 6, of which 2 were waited for; matrix products, arithmetic and copies ran while one was open for 2% of the time, Pallas kernels for 2%

profile of v6, /device:TPU:2, one launch (start us, length us, event | category | flops | bytes accessed | tf_op | source)
XLA Modules:
  0.0 105.4 jit_solution(7938214464133619869)
XLA Ops:
  0.6 0.0 copy-start
  0.7 0.7 copy-done
  1.4 0.7 broadcast_in_dim.15
  2.1 11.5 %all-to-all-start.8 = ((bf16[32,32,128]{2,1,0:T(8,128)(2,1)}), bf16[32,32,128]{2,1,0:T(8,128)(2,1)S(1)}, u32[]{:S(2)}, u32[]{:S(2)}) async-start(bf16[32,32,128]{2,1,0:T(8,128)(2,1)} %broadcast_in_dim.15), calls=%async_computation.8 | async-start | bytes 524288 | tf_op jit(solution)/shard_map/all_to_all | solution.py:33
  13.6 0.7 add_bitcast_fusion
  14.3 0.0 collective-permute-start
  14.3 0.9 constant_dynamic-slice_fusion.block_ref
  15.2 0.2 collective-permute-done
  15.4 0.5 collective-permute-start.3
  16.0 2.4 %collective-permute-start.2 = (s32[2,2,256]{2,1,0:T(2,128)S(1)}, s32[2,2,256]{2,1,0:T(2,128)S(1)}, u32[]{:S(2)}, u32[]{:S(2)}) collective-permute-start(s32[2,2,256]{2,1,0:T(2,128)S(1)} %pad_add_fusion.refs_0_), channel_id=1, source_target_pairs={{0,128},{64,192},{128,0},{192,64},{1,129},{65,193},{129,1},{193,65... | collective-permute-start | bytes 12296 | tf_op jit(solution)/shard_map/ppermute | solution.py:502
  18.4 1.8 %collective-permute-start.1 = (s32[2,2,256]{2,1,0:T(2,128)S(1)}, s32[2,2,256]{2,1,0:T(2,128)S(1)}, u32[]{:S(2)}, u32[]{:S(2)}) collective-permute-start(s32[2,2,256]{2,1,0:T(2,128)S(1)} %pad_add_fusion.refs_0_), channel_id=1, source_target_pairs={{0,64},{64,128},{128,192},{192,0},{1,65},{65,129},{129,193},{193,1... | collective-permute-start | bytes 12296 | tf_op jit(solution)/shard_map/ppermute | solution.py:502
  20.2 6.2 %all-to-all-done.8 = bf16[32,32,128]{2,1,0:T(8,128)(2,1)S(1)} async-done(((bf16[32,32,128]{2,1,0:T(8,128)(2,1)}), bf16[32,32,128]{2,1,0:T(8,128)(2,1)S(1)}, u32[]{:S(2)}, u32[]{:S(2)}) %all-to-all-start.8) | async-done | bytes 262176 | tf_op jit(solution)/shard_map/all_to_all | solution.py:33
  26.4 0.0 collective-permute-start.4
  26.4 0.1 pad_add_fusion.2.spot_ref
  26.5 0.9 points.1
  27.3 0.0 collective-permute-done.3.refs_3_
  27.3 0.0 collective-permute-done.2.refs_2_
  27.4 1.6 %count.1 = (s32[32,128]{1,0:T(8,128)S(1)}, s32[40,128]{1,0:T(8,128)S(1)}, f32[16,128]{1,0:T(8,128)S(1)}) custom-call(s32[2,2,256]{2,1,0:T(2,128)S(1)} %pad_add_fusion.refs_0_, s32[2,2,256]{2,1,0:T(2,128)S(1)} %collective-permute-done.1.refs_1_, s32[2,2,256]{2,1,0:T(2,128)S(1)} %collective-permute-done.2.refs_2_, s32[2,2,256]{2,1,0:T(2,128)S(1)} %collective-permute-done.3.refs_3_), custom_call_target="tpu_custom_call" | custom-call | tf_op jit(solution)/shard_map/count/pallas_call | solution.py:510
  28.9 0.5 slice.6
  30.1 0.1 slice_reduce_fusion
  30.2 0.1 pad_add_fusion.1
  30.3 60.7 %conditional.1 = (f32[32,8,128]{2,1,0:T(8,128)S(1)}, f32[128]{0:T(128)}) conditional(s32[]{:T(128)} %bitcast.5, (s32[34]{0:T(128)S(1)}, s32[256]{0:T(256)}, bf16[32,32,128]{2,1,0:T(8,128)(2,1)S(1)}, bf16[32,32,128]{2,1,0:T(8,128)(2,1)S(1)}, s32[32,128]{1,0:T(8,128)S(1)}, /*index=5*/f32[16,128]{1,0:T(8,128)S(1)}, bf16[1024,128]{1,0:T(8,128)(2,1)S(1)}, ...), branch_computations={%region_0.0_spmd, %region_3.0_spmd} | conditional | flops 47104 | bytes 2285588 | solution.py:520
  30.4 4.4 %first.3 = (f32[8,8,128]{2,1,0:T(8,128)S(1)}, bf16[4,64,256]{2,1,0:T(8,128)(2,1)S(1)}, bf16[1024,128]{1,0:T(8,128)(2,1)S(1)}, f32[1024,128]{1,0:T(8,128)S(1)}) custom-call(s32[34]{0:T(128)S(1)} %get-tuple-element.51.meta_ref, s32[256]{0:T(256)} %get-tuple-element.52.fill_ref, bf16[32,32,128]{2,1,0:T(8,128)(2,1)S(1)} %get-tuple-element.53.mine_ref, ...), custom_call_target="tpu_custom_call" | custom-call | tf_op jit(solution)/shard_map/cond/branch_1_fun/first/pallas_call | solution.py:444
  34.8 8.7 %all_to_all.46 = f32[8,8,128]{2,1,0:T(8,128)S(1)} all-to-all(f32[8,8,128]{2,1,0:T(8,128)S(1)} %get-tuple-element.59), channel_id=1, replica_groups=mesh['samp_0'=4,'samp_1'=2,'state_0'=8,'state_1'=4] {'samp_0','samp_1'}, dimensions={0} | all-to-all | bytes 65536 | tf_op jit(solution)/shard_map/cond/branch_1_fun/all_to_all | solution.py:33
  43.6 14.9 %all_to_all.47.logs_in_ref = f32[32,8,128]{2,1,0:T(8,128)S(1)} all-to-all(f32[32,8,128]{2,1,0:T(8,128)S(1)} %broadcast_in_dim.2), channel_id=1, replica_groups=mesh['samp_0'=4,'samp_1'=2,'state_0'=8,'state_1'=4] {'state_0','state_1'}, dimensions={0} | all-to-all | bytes 262144 | tf_op jit(solution)/shard_map/cond/branch_1_fun/all_to_all | solution.py:33
  58.5 7.2 %second.3 = f32[8,40,128]{2,1,0:T(8,128)S(1)} custom-call(s32[34]{0:T(128)S(1)} %get-tuple-element.51.meta_ref, s32[256]{0:T(256)} %get-tuple-element.52.fill_ref, f32[32,8,128]{2,1,0:T(8,128)S(1)} %all_to_all.47.logs_in_ref, bf16[32,32,128]{2,1,0:T(8,128)(2,1)S(1)} %get-tuple-element.53.mine_ref, bf16[32,32,128]{2,1,0:T(8,128)(2,1)S(1)} %get-tuple-element.54.other_ref, ...), custom_call_target="tpu_custom_call" | custom-call | tf_op jit(solution)/shard_map/cond/branch_1_fun/second/pallas_call | solution.py:459
  65.7 8.9 %all_to_all.48.logs_ref = f32[8,40,128]{2,1,0:T(8,128)S(1)} all-to-all(f32[8,40,128]{2,1,0:T(8,128)S(1)} %second.3), channel_id=1, replica_groups=mesh['samp_0'=4,'samp_1'=2,'state_0'=8,'state_1'=4] {'samp_0','samp_1'}, dimensions={0} | all-to-all | bytes 327680 | tf_op jit(solution)/shard_map/cond/branch_1_fun/all_to_all | solution.py:33
  74.6 0.1 message.3
  74.7 13.8 %all_to_all.49.logs_in_ref = f32[32,8,128]{2,1,0:T(8,128)S(1)} all-to-all(f32[32,8,128]{2,1,0:T(8,128)S(1)} %message.3), channel_id=1, replica_groups=mesh['samp_0'=4,'samp_1'=2,'state_0'=8,'state_1'=4] {'state_0','state_1'}, dimensions={0} | all-to-all | bytes 262144 | tf_op jit(solution)/shard_map/cond/branch_1_fun/all_to_all | solution.py:33
  88.6 2.4 %third.3 = (f32[1,128]{1,0:T(1,128)}, f32[32,8,128]{2,1,0:T(8,128)S(1)}) custom-call(s32[34]{0:T(128)S(1)} %get-tuple-element.51.meta_ref, f32[32,8,128]{2,1,0:T(8,128)S(1)} %all_to_all.49.logs_in_ref, f32[16,128]{1,0:T(8,128)S(1)} %get-tuple-element.56.log_count_ref, bf16[4,64,256]{2,1,0:T(8,128)(2,1)S(1)} %get-tuple-element.60.coefs_ref, ...), custom_call_target="tpu_custom_call" | custom-call | tf_op jit(solution)/shard_map/cond/branch_1_fun/third/pallas_call | solution.py:475
  91.0 13.8 %all_to_all.50 = f32[32,8,128]{2,1,0:T(8,128)S(1)} all-to-all(f32[32,8,128]{2,1,0:T(8,128)S(1)} %get-tuple-element.80), channel_id=1, replica_groups=mesh['samp_0'=4,'samp_1'=2,'state_0'=8,'state_1'=4] {'state_0','state_1'}, dimensions={0} | all-to-all | bytes 262144 | tf_op jit(solution)/shard_map/all_to_all | solution.py:33
  104.8 0.7 copy.11
  (8 shorter events, 0.1 us)
Async XLA Ops:
  0.6 0.7 copy-start
  2.1 24.3 %all-to-all-start.8 = ((bf16[32,32,128]{2,1,0:T(8,128)(2,1)}), bf16[32,32,128]{2,1,0:T(8,128)(2,1)S(1)}, u32[]{:S(2)}, u32[]{:S(2)}) async-start(bf16[32,32,128]{2,1,0:T(8,128)(2,1)} %broadcast_in_dim.15), calls=%async_computation.8 | async-start | bytes 524288 | tf_op jit(solution)/shard_map/all_to_all | solution.py:33
  14.3 1.2 %collective-permute-start = (s32[1,2,256]{2,1,0:T(2,128)S(1)}, s32[1,2,256]{2,1,0:T(2,128)S(1)}, u32[]{:S(2)}, u32[]{:S(2)}) collective-permute-start(s32[1,2,256]{2,1,0:T(2,128)S(1)} %add_bitcast_fusion), channel_id=1, source_target_pairs={{0,32},{32,0},{1,33},{33,1},{2,34},{34,2},{3,35},{35,3},{4,36},{36... | collective-permute-start | bytes 6152 | tf_op jit(solution)/shard_map/ppermute | solution.py:499
  15.4 11.9 %collective-permute-start.3 = (s32[2,2,256]{2,1,0:T(2,128)S(1)}, s32[2,2,256]{2,1,0:T(2,128)S(1)}, u32[]{:S(2)}, u32[]{:S(2)}) collective-permute-start(s32[2,2,256]{2,1,0:T(2,128)S(1)} %pad_add_fusion.refs_0_), channel_id=1, source_target_pairs={{0,192},{64,0},{128,64},{192,128},{1,193},{65,1},{129,65},{193,129... | collective-permute-start | bytes 12296 | tf_op jit(solution)/shard_map/ppermute | solution.py:502
  16.0 11.4 %collective-permute-start.2 = (s32[2,2,256]{2,1,0:T(2,128)S(1)}, s32[2,2,256]{2,1,0:T(2,128)S(1)}, u32[]{:S(2)}, u32[]{:S(2)}) collective-permute-start(s32[2,2,256]{2,1,0:T(2,128)S(1)} %pad_add_fusion.refs_0_), channel_id=1, source_target_pairs={{0,128},{64,192},{128,0},{192,64},{1,129},{65,193},{129,1},{193,65... | collective-permute-start | bytes 12296 | tf_op jit(solution)/shard_map/ppermute | solution.py:502
  18.4 9.0 %collective-permute-start.1 = (s32[2,2,256]{2,1,0:T(2,128)S(1)}, s32[2,2,256]{2,1,0:T(2,128)S(1)}, u32[]{:S(2)}, u32[]{:S(2)}) collective-permute-start(s32[2,2,256]{2,1,0:T(2,128)S(1)} %pad_add_fusion.refs_0_), channel_id=1, source_target_pairs={{0,64},{64,128},{128,192},{192,0},{1,65},{65,129},{129,193},{193,1... | collective-permute-start | bytes 12296 | tf_op jit(solution)/shard_map/ppermute | solution.py:502
  26.4 3.9 %collective-permute-start.4 = (bf16[32,32,128]{2,1,0:T(8,128)(2,1)S(1)}, bf16[32,32,128]{2,1,0:T(8,128)(2,1)S(1)}, u32[]{:S(2)}, u32[]{:S(2)}) collective-permute-start(bf16[32,32,128]{2,1,0:T(8,128)(2,1)S(1)} %all-to-all-done.8), channel_id=1, source_target_pairs={{0,32},{32,0},{1,33},{33,1},{2,34},{34,2},{3,35},{35,3},{4,36},{36... | collective-permute-start | bytes 786440 | tf_op jit(solution)/shard_map/ppermute | solution.py:509

commit v7 on v6

--- a/solution.py
+++ b/solution.py
@@ -76,7 +76,7 @@
     return combine(x[:, :LANES], x[:, LANES:])
 
 
-def points_kernel(spot_ref, block_ref, head_ref, points_ref):
+def points_kernel(spot_ref, fill_ref, block_ref, head_ref, points_ref, dead_ref):
     rows = points_ref.shape[0]
     half = COMP // 2
     own = pl.multiple_of(spot_ref[1] * half, half)
@@ -89,6 +89,8 @@
         high, middle, low = three_parts(jnp.concatenate([mine, other], 0).T * -LOG2E)
         head_ref[at, :] = jnp.concatenate([high, middle], 1).astype(BF16)
         points_ref[at, :] = jnp.concatenate([low, ones], 1).astype(BF16)
+        fill = fill_ref[spot_ref[0] * (rows // BLOCK) + b]
+        dead_ref[at, :] = jnp.where(iota((BLOCK, LANES), 0) < fill, 0.0, NEGATIVE)
 
 
 def count_kernel(*refs):
@@ -157,47 +159,43 @@
     return jnp.concatenate([rows[2 * j : 2 * j + 1, :], rows[2 * j + 1 : 2 * j + 2, :]], 1)
 
 
-def over_tiles(tile_count, pairs, body, carry):
+def over_tiles(tile_count, body, carry):
     if tile_count * TILE == SMALL_ROWS * LANES:
         for j in range(tile_count):
             carry = body(j, carry)
         return carry
-    return lax.fori_loop(0, 2 * pairs, body, carry)
-
-
-def exact_denominators(c, head_ref, points_ref, coefs_ref, tails_ref, pairs, energy_ref):
+    return lax.fori_loop(0, tile_count, body, carry)
+
+
+def exact_denominators(c, head_ref, points_ref, coefs_ref, tails_ref, energy_ref):
     def find(j, top):
         exponents = against(head_ref, points_ref, c, whole_tile(coefs_ref[j], tails_ref[j]))
         energy_ref[j] = exponents
         return jnp.maximum(top, halves(jnp.maximum, exponents))
 
     tile_count = coefs_ref.shape[0]
-    top = over_tiles(tile_count, pairs, find, jnp.full((CHUNK, LANES), 4 * NEGATIVE, F32))
+    top = over_tiles(tile_count, find, jnp.full((CHUNK, LANES), 4 * NEGATIVE, F32))
     top = jnp.max(top, axis=1, keepdims=True)
 
     def add(j, sums):
         return sums + halves(jnp.add, jnp.exp2(energy_ref[j] - top))
 
-    sums = over_tiles(tile_count, pairs, add, jnp.zeros((CHUNK, LANES), F32))
+    sums = over_tiles(tile_count, add, jnp.zeros((CHUNK, LANES), F32))
     return jnp.broadcast_to(top + jnp.log2(jnp.sum(sums, axis=1, keepdims=True)), (CHUNK, LANES))
 
 
-def near_denominators(c, base_ref, head_ref, anchored_ref, coefs_ref, tails_ref, pairs):
+def near_denominators(c, base_ref, head_ref, anchored_ref, coefs_ref, tails_ref):
     def add(j, sums):
         tile = whole_tile(coefs_ref[j], tails_ref[j])
         return sums + halves(jnp.add, jnp.exp2(against(head_ref, anchored_ref, c, tile)))
 
-    sums = over_tiles(coefs_ref.shape[0], pairs, add, jnp.zeros((CHUNK, LANES), F32))
+    sums = over_tiles(coefs_ref.shape[0], add, jnp.zeros((CHUNK, LANES), F32))
     return base_ref[chunk(c), :] + jnp.log2(jnp.sum(sums, axis=1, keepdims=True))
 
 
-def put_live(c, points_ref, logden, live_ref, fill_ref, first_block):
-    row = iota((BLOCK, LANES), 0)
-    for b in range(CHUNK // BLOCK):
-        at = pl.ds(pl.multiple_of(c * CHUNK + b * BLOCK, BLOCK), BLOCK)
-        here = -logden[b * BLOCK : (b + 1) * BLOCK, :]
-        shift = jnp.where(row < fill_ref[first_block + c * (CHUNK // BLOCK) + b], here, NEGATIVE)
-        live_ref[at, :] = with_shift(points_ref[at, :].astype(F32), shift).astype(BF16)
+def put_live(c, points_ref, logden, live_ref, dead_ref):
+    shift = dead_ref[chunk(c), :] - logden
+    live_ref[chunk(c), :] = with_shift(points_ref[chunk(c), :].astype(F32), shift).astype(BF16)
 
 
 def each_chunk(rows, body):
@@ -232,13 +230,13 @@
     logs_ref[pl.ds(first + 1, 1), :] = logs[:, LANES:]
 
 
-def counted_log_sums(total, weight_ref, coefs_ref, tails_ref, pairs, head_ref, live_ref, exponent_ref, logs_ref, low_ref):
+def counted_log_sums(weight_ref, coefs_ref, tails_ref, head_ref, live_ref, exponent_ref, logs_ref, low_ref):
     low_ref[...] = jnp.zeros(low_ref.shape, F32)
     logs_ref[0 : weight_ref.shape[0], :] = jnp.zeros(weight_ref.shape, F32)
 
     def finish(j, logs):
         weight = jnp.concatenate([weight_ref[pl.ds(2 * j, 1), :], weight_ref[pl.ds(2 * j + 1, 1), :]], 1)
-        valid = iota((1, TILE), 1) < total - j * TILE
+        valid = weight > NEGATIVE / 2
         put_rows(logs_ref, 2 * j, jnp.where(valid, logs - weight, 0.0))
         return valid
 
@@ -255,7 +253,7 @@
             low_ref[0:1, :] = jnp.maximum(low_ref[0:1, :], jnp.where(valid & (totals < LEAST), 1.0, 0.0))
         return carry
 
-    lax.fori_loop(0, pairs, one, 0)
+    lax.fori_loop(0, coefs_ref.shape[0] // 2, one, 0)
 
     @pl.when(jnp.max(low_ref[...]) > 0)
     def _():
@@ -264,15 +262,16 @@
             finish(j, log_of_sum(highest, exponent_ref))
             return carry
 
-        lax.fori_loop(0, 2 * pairs, again, 0)
-
-
-def weighted_tails(total, logs, log_count_ref, tails_ref, weight_ref):
-    valid = iota(logs.shape, 0) * LANES + iota(logs.shape, 1) < total
+        lax.fori_loop(0, coefs_ref.shape[0], again, 0)
+
+
+def weighted_tails(logs, log_count_ref, tails_ref, weight_ref):
+    log_count = log_count_ref[0 : weight_ref.shape[0], :]
+    valid = log_count > NEGATIVE / 2
     free = jnp.where(valid, logs * -LOG2E, 4 * NEGATIVE)
     highest = jnp.max(jnp.max(free, axis=0, keepdims=True), axis=1, keepdims=True)
     free = jnp.where(valid, free - highest, 0.0)
-    weight = log_count_ref[0 : weight_ref.shape[0], :] + free
+    weight = log_count + free
     weight_ref[...] = weight
     for j in range(tails_ref.shape[0]):
         tails_ref[j] = tail_rows(tile_row(weight, j))
@@ -280,13 +279,11 @@
 
 
 def first_kernel(
-    meta_ref, fill_ref, mine_ref, other_ref, place_ref, log_count_ref, head_ref, points_ref,
+    meta_ref, mine_ref, other_ref, place_ref, log_count_ref, head_ref, points_ref, dead_ref,
     logs_ref, coefs_ref, anchored_ref, base_ref,
     tails_ref, packed_ref, energy_ref, live_ref, exponent_ref, low_ref, rows_ref, weight_ref,
 ):
     groups = mine_ref.shape[0]
-    total = meta_ref[groups]
-    pairs = (total + 2 * TILE - 1) // (2 * TILE)
     packed_ref[...] = jnp.zeros(packed_ref.shape, F32)
     for t in range(groups):
         chosen = jnp.where(iota((2 * LANES, LANES), 0) == place_ref[t : t + 1, :], 1.0, 0.0).astype(BF16)
@@ -299,22 +296,21 @@
     for j in range(coefs_ref.shape[0]):
         coefs_ref[j] = jnp.concatenate([packed_ref[2 * j], packed_ref[2 * j + 1]], 1).astype(BF16)
         tails_ref[j] = tail_rows(tile_row(log_count, j))
-    first_block = meta_ref[groups + 1] * (points_ref.shape[0] // BLOCK)
 
     def denominators(c):
-        logden = exact_denominators(c, head_ref, points_ref, coefs_ref, tails_ref, pairs, energy_ref)
+        logden = exact_denominators(c, head_ref, points_ref, coefs_ref, tails_ref, energy_ref)
         base_ref[chunk(c), :] = logden
         anchored_ref[chunk(c), :] = with_shift(points_ref[chunk(c), :].astype(F32), -logden).astype(BF16)
-        put_live(c, points_ref, logden, live_ref, fill_ref, first_block)
+        put_live(c, points_ref, logden, live_ref, dead_ref)
 
     each_chunk(points_ref.shape[0], denominators)
     counted_log_sums(
-        total, weight_ref, coefs_ref, tails_ref, pairs, head_ref, live_ref, exponent_ref, rows_ref, low_ref
+        weight_ref, coefs_ref, tails_ref, head_ref, live_ref, exponent_ref, rows_ref, low_ref
     )
     logs_ref[...] = jnp.broadcast_to(rows_ref[...][None], logs_ref.shape)
 
 
-def new_denominators(least, base_ref, head_ref, anchored_ref, points_ref, coefs_ref, tails_ref, pairs, energy_ref, put):
+def new_denominators(least, base_ref, head_ref, anchored_ref, points_ref, coefs_ref, tails_ref, energy_ref, put):
     rows = points_ref.shape[0]
     near = least > -SPREAD
 
@@ -322,35 +318,32 @@
     def _():
         each_chunk(
             rows,
-            lambda c: put(c, near_denominators(c, base_ref, head_ref, anchored_ref, coefs_ref, tails_ref, pairs)),
+            lambda c: put(c, near_denominators(c, base_ref, head_ref, anchored_ref, coefs_ref, tails_ref)),
         )
 
     @pl.when(jnp.logical_not(near))
     def _():
         each_chunk(
-            rows, lambda c: put(c, exact_denominators(c, head_ref, points_ref, coefs_ref, tails_ref, pairs, energy_ref))
+            rows, lambda c: put(c, exact_denominators(c, head_ref, points_ref, coefs_ref, tails_ref, energy_ref))
         )
 
 
 def second_kernel(
-    meta_ref, fill_ref, logs_in_ref, mine_ref, other_ref, log_count_ref, coefs_ref, head_ref, points_ref, anchored_ref,
+    logs_in_ref, mine_ref, other_ref, log_count_ref, coefs_ref, head_ref, points_ref, dead_ref, anchored_ref,
     base_ref,
     logs_ref,
     tails_ref, weight_ref, energy_ref, live_ref, exponent_ref, low_ref, rows_ref,
 ):
     groups = mine_ref.shape[0]
     slot_rows = weight_ref.shape[0]
-    total = meta_ref[groups]
-    pairs = (total + 2 * TILE - 1) // (2 * TILE)
     logs = log_sum_pieces(logs_in_ref)
-    _, least = weighted_tails(total, logs, log_count_ref, tails_ref, weight_ref)
-    first_block = meta_ref[groups + 1] * (points_ref.shape[0] // BLOCK)
+    _, least = weighted_tails(logs, log_count_ref, tails_ref, weight_ref)
     new_denominators(
-        least, base_ref, head_ref, anchored_ref, points_ref, coefs_ref, tails_ref, pairs, energy_ref,
-        lambda c, logden: put_live(c, points_ref, logden, live_ref, fill_ref, first_block),
+        least, base_ref, head_ref, anchored_ref, points_ref, coefs_ref, tails_ref, energy_ref,
+        lambda c, logden: put_live(c, points_ref, logden, live_ref, dead_ref),
     )
     counted_log_sums(
-        total, weight_ref, coefs_ref, tails_ref, pairs, head_ref, live_ref, exponent_ref, rows_ref, low_ref
+        weight_ref, coefs_ref, tails_ref, head_ref, live_ref, exponent_ref, rows_ref, low_ref
     )
     tail = tail_rows(None)
     last = groups * LANES // TILE - 1
@@ -401,32 +394,29 @@
 
 
 def third_kernel(
-    meta_ref, logs_in_ref, log_count_ref, coefs_ref, head_ref, points_ref, anchored_ref, base_ref,
+    logs_in_ref, log_count_ref, coefs_ref, head_ref, points_ref, anchored_ref, base_ref,
     free_ref, logden_ref,
     tails_ref, weight_ref, energy_ref, totals_ref,
 ):
-    copies = logden_ref.shape[0]
     slot_rows = weight_ref.shape[0]
-    total = meta_ref[copies]
-    pairs = (total + 2 * TILE - 1) // (2 * TILE)
     logs = log_sum_pieces(logs_in_ref)
     (own_row, zero_row), zero_lane = places(slot_rows)
     zero = logs[zero_row : zero_row + 1, zero_lane : zero_lane + 1]
     free_ref[...] = zero - logs[own_row : own_row + 1, :]
-    highest, least = weighted_tails(total, logs[:slot_rows], log_count_ref, tails_ref, weight_ref)
+    highest, least = weighted_tails(logs[:slot_rows], log_count_ref, tails_ref, weight_ref)
 
     def put(c, logden):
         totals_ref[chunk(c), :] = logden
 
     new_denominators(
-        least, base_ref, head_ref, anchored_ref, points_ref, coefs_ref, tails_ref, pairs, energy_ref, put
+        least, base_ref, head_ref, anchored_ref, points_ref, coefs_ref, tails_ref, energy_ref, put
     )
     turned = [totals_ref[pl.ds(b * LANES, LANES), :].T[0:1, :] for b in range(points_ref.shape[0] // LANES)]
     logden = (jnp.concatenate(turned, 0) + highest) * LN2 + zero
     logden_ref[...] = jnp.broadcast_to(logden[None], logden_ref.shape)
 
 
-def iterated(slot_rows, meta, block_fill, mine, other, place, log_count, head, points):
+def iterated(slot_rows, meta, mine, other, place, log_count, head, points, dead):
     samps = lax.axis_size(SAMP)
     groups = mine.shape[0]
     rows = points.shape[0]
@@ -447,25 +437,25 @@
             shape((samps, slot_rows, LANES), F32), shape((tile_count, COMP, TILE), BF16), shape((rows, LANES), BF16),
             shape((rows, LANES), F32),
         ),
-        in_specs=[smem, smem] + [vmem] * 6, out_specs=(vmem,) * 4,
+        in_specs=[smem] + [vmem] * 7, out_specs=(vmem,) * 4,
         scratch_shapes=[
             tails_work, pltpu.VMEM((slot_rows + 2, COMP, LANES), F32), energy_work, live_work, exponent_work, low_work,
             weight_work, weight_work,
         ],
         compiler_params=params, name="first",
-    )(meta, block_fill, mine, other, place, log_count, head, points)
+    )(meta, mine, other, place, log_count, head, points, dead)
     logs = log_sum(exchanged(logs, SAMP))
     logs = copies_of_each(logs, STATE)
     logs = pl.pallas_call(
         second_kernel,
         out_shape=shape((samps, slot_rows + groups, LANES), F32),
-        in_specs=[smem, smem] + [vmem] * 9, out_specs=vmem,
+        in_specs=[vmem] * 10, out_specs=vmem,
         scratch_shapes=[
             tails_work, weight_work, energy_work, live_work, exponent_work,
             low_work, pltpu.VMEM((slot_rows + groups, LANES), F32),
         ],
         compiler_params=params, name="second",
-    )(meta, block_fill, logs, mine, other, log_count, coefs, head, points, anchored, base)
+    )(logs, mine, other, log_count, coefs, head, points, dead, anchored, base)
     logs = pl.pallas_call(
         message_kernel,
         out_shape=shape((groups, slot_rows if slot_rows == SMALL_ROWS else slot_rows + 8, LANES), F32),
@@ -475,10 +465,10 @@
     return pl.pallas_call(
         third_kernel,
         out_shape=(shape((1, LANES), F32), shape((groups, rows // LANES, LANES), F32)),
-        in_specs=[smem] + [vmem] * 7, out_specs=(vmem, vmem),
+        in_specs=[vmem] * 7, out_specs=(vmem, vmem),
         scratch_shapes=[tails_work, weight_work, energy_work, pltpu.VMEM((rows, LANES), F32)],
         compiler_params=params, name="third",
-    )(meta, logs, log_count, coefs, head, points, anchored, base)
+    )(logs, log_count, coefs, head, points, anchored, base)
 
 
 def shards(components, coefficients, block_window, block_fill):
@@ -490,6 +480,7 @@
     slot_rows = min(samps * block_window.shape[0] // LANES, groups)
     shape = jax.ShapeDtypeStruct
     vmem = pl.BlockSpec(memory_space=pltpu.VMEM)
+    smem = pl.BlockSpec(memory_space=pltpu.SMEM)
     params = pltpu.CompilerParams(vmem_limit_bytes=24 << 20)
     spot = jnp.stack([position, core]).astype(jnp.int32)
 
@@ -500,12 +491,12 @@
     along = lax.axis_size(SAMP[0])
     turns = [[(i, (i + k) % along) for i in range(along)] for k in range(1, along)]
     pieces = [blocks] + [lax.ppermute(blocks, SAMP[0], turn) for turn in turns]
-    head, points = pl.pallas_call(
+    head, points, dead = pl.pallas_call(
         points_kernel,
-        out_shape=(shape((rows, LANES), BF16), shape((rows, LANES), BF16)),
-        in_specs=[pl.BlockSpec(memory_space=pltpu.SMEM), vmem], out_specs=(vmem, vmem),
+        out_shape=(shape((rows, LANES), BF16), shape((rows, LANES), BF16), shape((rows, LANES), F32)),
+        in_specs=[smem, smem, vmem], out_specs=(vmem, vmem, vmem),
         compiler_params=params, name="points",
-    )(spot, lax.dynamic_slice_in_dim(components, position * rows, rows, 1))
+    )(spot, block_fill, lax.dynamic_slice_in_dim(components, position * rows, rows, 1))
     other = lax.ppermute(mine, SAMP[1], [(0, 1), (1, 0)])
     place, meta, log_count = pl.pallas_call(
         count_kernel,
@@ -516,11 +507,11 @@
         in_specs=[vmem] * len(pieces), out_specs=(vmem, vmem, vmem), compiler_params=params, name="count",
     )(*pieces)
     total = meta[groups, 0]
-    meta = jnp.concatenate([meta[: groups + 1, 0], spot[:1]])
+    meta = meta[:groups, 0]
     free, logden = lax.cond(
         total <= SMALL,
         functools.partial(iterated, SMALL_ROWS), functools.partial(iterated, slot_rows),
-        meta, block_fill, mine, other, place, log_count, head, points,
+        meta, mine, other, place, log_count, head, points, dead,
     )
     return free.reshape(-1), exchanged(logden, STATE).reshape(-1)
 

time: 106 us -> 111 us (1.047)
  waiting for transfers between devices: 6.42 us -> 12.3 us
  Pallas kernels: 16.5 us -> 15.1 us
    all_to_all x1, waiting for transfers between devices: 6.18 us -> 12.1 us  [exchanged(): return lax.all_to_all(copies, axes, split_axis=0, concat_axis=0, tiled=True)]
where the time goes in v7:
time: 111 us; the launch traced here: 110 us
  blocking collectives  59.6 us (54%)
  starting transfers between devices  16.3 us (15%)
  Pallas kernels  15.1 us (14%)
  waiting for transfers between devices  12.3 us (11%)
  local copies, waits for them, and re-layouts  4.33 us (4%)
  between operations  1.38 us (1%)
    all_to_all x5, blocking collectives, exchanged(): return lax.all_to_all(copies, axes, split_axis=0, concat_axis=0, tiled=True)  59.6 us
    all_to_all x1, waiting for transfers between devices, exchanged(): return lax.all_to_all(copies, axes, split_axis=0, concat_axis=0, tiled=True)  12.1 us
    all_to_all x1, starting transfers between devices, exchanged(): return lax.all_to_all(copies, axes, split_axis=0, concat_axis=0, tiled=True)  11.5 us
    pallas_call x1, Pallas kernels, iterated(): pl.pallas_call(second_kernel, out_shape=shape((samps, slot_rows + groups,...  6.56 us
    ppermute x3, starting transfers between devices, shards(): pieces = [blocks] + [lax.ppermute(blocks, SAMP[0], turn) for turn in turns]  4.83 us
    pallas_call x1, Pallas kernels, iterated(): pl.pallas_call(first_kernel, out_shape=(shape((samps, slot_rows, LANES),...  4.17 us
  transfers between devices with their start and end apart: 6, of which 2 were waited for; matrix products, arithmetic and copies ran while one was open for 2% of the time, Pallas kernels for 2%

profile of v7, /device:TPU:2, one launch (start us, length us, event | category | flops | bytes accessed | tf_op | source)
XLA Modules:
  0.0 110.1 jit_solution(2483879783792713570)
XLA Ops:
  0.6 0.0 copy-start
  0.7 0.7 copy-done
  1.4 0.7 broadcast_in_dim.15
  2.1 11.5 %all-to-all-start.8 = ((bf16[32,32,128]{2,1,0:T(8,128)(2,1)}), bf16[32,32,128]{2,1,0:T(8,128)(2,1)S(1)}, u32[]{:S(2)}, u32[]{:S(2)}) async-start(bf16[32,32,128]{2,1,0:T(8,128)(2,1)} %broadcast_in_dim.15), calls=%async_computation.8 | async-start | bytes 524288 | tf_op jit(solution)/shard_map/all_to_all | solution.py:33
  13.6 0.7 add_bitcast_fusion
  14.3 0.0 collective-permute-start
  14.3 12.1 %all-to-all-done.8 = bf16[32,32,128]{2,1,0:T(8,128)(2,1)S(1)} async-done(((bf16[32,32,128]{2,1,0:T(8,128)(2,1)}), bf16[32,32,128]{2,1,0:T(8,128)(2,1)S(1)}, u32[]{:S(2)}, u32[]{:S(2)}) %all-to-all-start.8) | async-done | bytes 262176 | tf_op jit(solution)/shard_map/all_to_all | solution.py:33
  26.4 0.0 collective-permute-start.4
  26.4 0.9 constant_dynamic-slice_fusion.block_ref
  27.3 0.0 collective-permute-done
  27.3 0.6 collective-permute-start.3
  27.9 2.4 %collective-permute-start.2 = (s32[2,2,256]{2,1,0:T(2,128)S(1)}, s32[2,2,256]{2,1,0:T(2,128)S(1)}, u32[]{:S(2)}, u32[]{:S(2)}) collective-permute-start(s32[2,2,256]{2,1,0:T(2,128)S(1)} %pad_add_fusion.refs_0_), channel_id=1, source_target_pairs={{0,128},{64,192},{128,0},{192,64},{1,129},{65,193},{129,1},{193,65... | collective-permute-start | bytes 12296 | tf_op jit(solution)/shard_map/ppermute | solution.py:493
  30.4 1.8 %collective-permute-start.1 = (s32[2,2,256]{2,1,0:T(2,128)S(1)}, s32[2,2,256]{2,1,0:T(2,128)S(1)}, u32[]{:S(2)}, u32[]{:S(2)}) collective-permute-start(s32[2,2,256]{2,1,0:T(2,128)S(1)} %pad_add_fusion.refs_0_), channel_id=1, source_target_pairs={{0,64},{64,128},{128,192},{192,0},{1,65},{65,129},{129,193},{193,1... | collective-permute-start | bytes 12296 | tf_op jit(solution)/shard_map/ppermute | solution.py:493
  32.2 0.1 pad_add_fusion.1.spot_ref
  32.2 0.7 copy-done.1
  32.9 0.9 points.1
  33.8 0.0 collective-permute-done.3.refs_3_
  33.8 0.2 collective-permute-done.1.refs_1_
  34.0 1.6 %count.1 = (s32[32,128]{1,0:T(8,128)S(1)}, s32[40,128]{1,0:T(8,128)S(1)}, f32[16,128]{1,0:T(8,128)S(1)}) custom-call(s32[2,2,256]{2,1,0:T(2,128)S(1)} %pad_add_fusion.refs_0_, s32[2,2,256]{2,1,0:T(2,128)S(1)} %collective-permute-done.1.refs_1_, s32[2,2,256]{2,1,0:T(2,128)S(1)} %collective-permute-done.2.refs_2_, s32[2,2,256]{2,1,0:T(2,128)S(1)} %collective-permute-done.3.refs_3_), custom_call_target="tpu_custom_call" | custom-call | tf_op jit(solution)/shard_map/count/pallas_call | solution.py:501
  35.5 0.5 slice.10
  36.7 59.0 %conditional.1 = (f32[32,8,128]{2,1,0:T(8,128)S(1)}, f32[128]{0:T(128)}) conditional(s32[]{:T(128)} %bitcast.7, (s32[40,128]{1,0:T(8,128)S(1)}, bf16[32,32,128]{2,1,0:T(8,128)(2,1)S(1)}, bf16[32,32,128]{2,1,0:T(8,128)(2,1)S(1)}, s32[32,128]{1,0:T(8,128)S(1)}, f32[16,128]{1,0:T(8,128)S(1)}, /*index=5*/bf16[1024,128]{1,0:T(8,128)(2,1)S(1)}, ...), branch_computations={%region_0.0_spmd, %region_3.0_spmd} | conditional | flops 47104 | bytes 2326804 | solution.py:511
  36.9 0.1 copy.7
  37.0 4.2 %first.3 = (f32[8,8,128]{2,1,0:T(8,128)S(1)}, bf16[4,64,256]{2,1,0:T(8,128)(2,1)S(1)}, bf16[1024,128]{1,0:T(8,128)(2,1)S(1)}, f32[1024,128]{1,0:T(8,128)S(1)}) custom-call(s32[32]{0:T(128)S(1)} %slice_bitcast_fusion.1.meta_ref, bf16[32,32,128]{2,1,0:T(8,128)(2,1)S(1)} %get-tuple-element.56.mine_ref, bf16[32,32,128]{2,1,0:T(8,128)(2,1)S(1)} %get-tuple-element.57.other_ref, ...), custom_call_target="tpu_custom_call" | custom-call | tf_op jit(solution)/shard_map/cond/branch_1_fun/first/pallas_call | solution.py:434
  41.2 8.9 %all_to_all.46 = f32[8,8,128]{2,1,0:T(8,128)S(1)} all-to-all(f32[8,8,128]{2,1,0:T(8,128)S(1)} %get-tuple-element.63), channel_id=1, replica_groups=mesh['samp_0'=4,'samp_1'=2,'state_0'=8,'state_1'=4] {'samp_0','samp_1'}, dimensions={0} | all-to-all | bytes 65536 | tf_op jit(solution)/shard_map/cond/branch_1_fun/all_to_all | solution.py:33
  50.2 14.3 %all_to_all.47.logs_in_ref = f32[32,8,128]{2,1,0:T(8,128)S(1)} all-to-all(f32[32,8,128]{2,1,0:T(8,128)S(1)} %broadcast_in_dim.2), channel_id=1, replica_groups=mesh['samp_0'=4,'samp_1'=2,'state_0'=8,'state_1'=4] {'state_0','state_1'}, dimensions={0} | all-to-all | bytes 262144 | tf_op jit(solution)/shard_map/cond/branch_1_fun/all_to_all | solution.py:33
  64.5 6.6 %second.3 = f32[8,40,128]{2,1,0:T(8,128)S(1)} custom-call(f32[32,8,128]{2,1,0:T(8,128)S(1)} %all_to_all.47.logs_in_ref, bf16[32,32,128]{2,1,0:T(8,128)(2,1)S(1)} %get-tuple-element.56.mine_ref, bf16[32,32,128]{2,1,0:T(8,128)(2,1)S(1)} %get-tuple-element.57.other_ref, f32[16,128]{1,0:T(8,128)S(1)} %get-tuple-element.59.log_count_ref, ...), custom_call_target="tpu_custom_call" | custom-call | tf_op jit(solution)/shard_map/cond/branch_1_fun/second/pallas_call | solution.py:449
  71.0 8.8 %all_to_all.48.logs_ref = f32[8,40,128]{2,1,0:T(8,128)S(1)} all-to-all(f32[8,40,128]{2,1,0:T(8,128)S(1)} %second.3), channel_id=1, replica_groups=mesh['samp_0'=4,'samp_1'=2,'state_0'=8,'state_1'=4] {'samp_0','samp_1'}, dimensions={0} | all-to-all | bytes 327680 | tf_op jit(solution)/shard_map/cond/branch_1_fun/all_to_all | solution.py:33
  79.8 0.1 message.3
  79.9 13.9 %all_to_all.49.logs_in_ref = f32[32,8,128]{2,1,0:T(8,128)S(1)} all-to-all(f32[32,8,128]{2,1,0:T(8,128)S(1)} %message.3), channel_id=1, replica_groups=mesh['samp_0'=4,'samp_1'=2,'state_0'=8,'state_1'=4] {'state_0','state_1'}, dimensions={0} | all-to-all | bytes 262144 | tf_op jit(solution)/shard_map/cond/branch_1_fun/all_to_all | solution.py:33
  93.8 1.9 %third.3 = (f32[1,128]{1,0:T(1,128)}, f32[32,8,128]{2,1,0:T(8,128)S(1)}) custom-call(f32[32,8,128]{2,1,0:T(8,128)S(1)} %all_to_all.49.logs_in_ref, f32[16,128]{1,0:T(8,128)S(1)} %get-tuple-element.59.log_count_ref, bf16[4,64,256]{2,1,0:T(8,128)(2,1)S(1)} %get-tuple-element.64.coefs_ref, bf16[1024,128]{1,0:T(8,128)(2,1)S(1)} %get-tuple-element.60.head_ref, ...), custom_call_target="tpu_custom_call" | custom-call | tf_op jit(solution)/shard_map/cond/branch_1_fun/third/pallas_call | solution.py:465
  95.7 13.8 %all_to_all.50 = f32[32,8,128]{2,1,0:T(8,128)S(1)} all-to-all(f32[32,8,128]{2,1,0:T(8,128)S(1)} %get-tuple-element.86), channel_id=1, replica_groups=mesh['samp_0'=4,'samp_1'=2,'state_0'=8,'state_1'=4] {'state_0','state_1'}, dimensions={0} | all-to-all | bytes 262144 | tf_op jit(solution)/shard_map/all_to_all | solution.py:33
  109.5 0.7 copy.13
  (10 shorter events, 0.1 us)
Async XLA Ops:
  0.6 0.7 copy-start
  2.1 24.3 %all-to-all-start.8 = ((bf16[32,32,128]{2,1,0:T(8,128)(2,1)}), bf16[32,32,128]{2,1,0:T(8,128)(2,1)S(1)}, u32[]{:S(2)}, u32[]{:S(2)}) async-start(bf16[32,32,128]{2,1,0:T(8,128)(2,1)} %broadcast_in_dim.15), calls=%async_computation.8 | async-start | bytes 524288 | tf_op jit(solution)/shard_map/all_to_all | solution.py:33
  14.3 13.0 %collective-permute-start = (s32[1,2,256]{2,1,0:T(2,128)S(1)}, s32[1,2,256]{2,1,0:T(2,128)S(1)}, u32[]{:S(2)}, u32[]{:S(2)}) collective-permute-start(s32[1,2,256]{2,1,0:T(2,128)S(1)} %add_bitcast_fusion), channel_id=1, source_target_pairs={{0,32},{32,0},{1,33},{33,1},{2,34},{34,2},{3,35},{35,3},{4,36},{36... | collective-permute-start | bytes 6152 | tf_op jit(solution)/shard_map/ppermute | solution.py:490
  26.4 10.3 %collective-permute-start.4 = (bf16[32,32,128]{2,1,0:T(8,128)(2,1)S(1)}, bf16[32,32,128]{2,1,0:T(8,128)(2,1)S(1)}, u32[]{:S(2)}, u32[]{:S(2)}) collective-permute-start(bf16[32,32,128]{2,1,0:T(8,128)(2,1)S(1)} %all-to-all-done.8), channel_id=1, source_target_pairs={{0,32},{32,0},{1,33},{33,1},{2,34},{34,2},{3,35},{35,3},{4,36},{36... | collective-permute-start | bytes 786440 | tf_op jit(solution)/shard_map/ppermute | solution.py:500
  27.3 6.5 %collective-permute-start.3 = (s32[2,2,256]{2,1,0:T(2,128)S(1)}, s32[2,2,256]{2,1,0:T(2,128)S(1)}, u32[]{:S(2)}, u32[]{:S(2)}) collective-permute-start(s32[2,2,256]{2,1,0:T(2,128)S(1)} %pad_add_fusion.refs_0_), channel_id=1, source_target_pairs={{0,192},{64,0},{128,64},{192,128},{1,193},{65,1},{129,65},{193,129... | collective-permute-start | bytes 12296 | tf_op jit(solution)/shard_map/ppermute | solution.py:493
  27.9 5.9 %collective-permute-start.2 = (s32[2,2,256]{2,1,0:T(2,128)S(1)}, s32[2,2,256]{2,1,0:T(2,128)S(1)}, u32[]{:S(2)}, u32[]{:S(2)}) collective-permute-start(s32[2,2,256]{2,1,0:T(2,128)S(1)} %pad_add_fusion.refs_0_), channel_id=1, source_target_pairs={{0,128},{64,192},{128,0},{192,64},{1,129},{65,193},{129,1},{193,65... | collective-permute-start | bytes 12296 | tf_op jit(solution)/shard_map/ppermute | solution.py:493
  30.4 3.6 %collective-permute-start.1 = (s32[2,2,256]{2,1,0:T(2,128)S(1)}, s32[2,2,256]{2,1,0:T(2,128)S(1)}, u32[]{:S(2)}, u32[]{:S(2)}) collective-permute-start(s32[2,2,256]{2,1,0:T(2,128)S(1)} %pad_add_fusion.refs_0_), channel_id=1, source_target_pairs={{0,64},{64,128},{128,192},{192,0},{1,65},{65,129},{129,193},{193,1... | collective-permute-start | bytes 12296 | tf_op jit(solution)/shard_map/ppermute | solution.py:493
  32.2 0.7 copy-start.1

commit v8 on v7

--- a/solution.py
+++ b/solution.py
@@ -76,7 +76,7 @@
     return combine(x[:, :LANES], x[:, LANES:])
 
 
-def points_kernel(spot_ref, fill_ref, block_ref, head_ref, points_ref, dead_ref):
+def points_kernel(spot_ref, own_ref, block_ref, head_ref, points_ref, dead_ref):
     rows = points_ref.shape[0]
     half = COMP // 2
     own = pl.multiple_of(spot_ref[1] * half, half)
@@ -89,14 +89,15 @@
         high, middle, low = three_parts(jnp.concatenate([mine, other], 0).T * -LOG2E)
         head_ref[at, :] = jnp.concatenate([high, middle], 1).astype(BF16)
         points_ref[at, :] = jnp.concatenate([low, ones], 1).astype(BF16)
-        fill = fill_ref[spot_ref[0] * (rows // BLOCK) + b]
-        dead_ref[at, :] = jnp.where(iota((BLOCK, LANES), 0) < fill, 0.0, NEGATIVE)
+        fills = own_ref[0, 1:2, :]
+        chosen = iota(fills.shape, 1) == spot_ref[0] * (rows // BLOCK) + b
+        fill = jnp.sum(jnp.where(chosen, fills.astype(F32), 0.0), axis=1, keepdims=True)
+        dead_ref[at, :] = jnp.where(iota((BLOCK, LANES), 0).astype(F32) < fill, 0.0, NEGATIVE)
 
 
 def count_kernel(*refs):
-    blocks_refs, (place_ref, meta_ref, log_count_ref) = refs[:-3], refs[-3:]
+    blocks_refs, (place_ref, meta_ref, digits_ref) = refs[:-3], refs[-3:]
     groups = place_ref.shape[0]
-    slots = log_count_ref.shape[0]
     width = blocks_refs[0].shape[2]
     counts = jnp.zeros((groups, LANES), F32)
     for blocks_ref, s in [(r, s) for r in blocks_refs for s in range(r.shape[0])]:
@@ -117,18 +118,14 @@
     meta_ref[0:groups, :] = offset_int >> 7
     everything = jnp.sum(total, axis=0, keepdims=True).astype(jnp.int32)
     meta_ref[groups : groups + 8, :] = jnp.broadcast_to(everything, (8, LANES))
-    whole = jnp.where(counted, offset_int + within_int, -1)
     counts_int = counts.astype(jnp.int32)
-    digits = (counts_int >> 14, (counts_int >> 7) & 127, counts_int & 127)
-    gathered = jnp.zeros((3 * slots, LANES), F32)
+    digits = [d.astype(F32) for d in (counts_int >> 14, (counts_int >> 7) & 127, counts_int & 127)]
+    row = iota((TAIL, LANES), 0)
     for t in range(groups):
-        row = whole[t : t + 1, :]
-        slot = iota((slots, LANES), 0) == row >> 7
-        parts = [jnp.where(slot, d[t : t + 1, :], 0).astype(F32) for d in digits]
-        of_lane = jnp.where(iota((LANES, LANES), 0) == (row & 127), 1.0, 0.0).astype(BF16)
-        gathered = gathered + dot_nt(jnp.concatenate(parts, 0).astype(BF16), of_lane)
-    compact = gathered[0:slots] * 16384.0 + gathered[slots : 2 * slots] * 128.0 + gathered[2 * slots :]
-    log_count_ref[...] = jnp.where(compact > 0, jnp.log2(jnp.maximum(compact, 1.0)), NEGATIVE)
+        rows = jnp.zeros((TAIL, LANES), F32)
+        for k, digit in enumerate(digits):
+            rows = jnp.where(row == k, digit[t : t + 1, :], rows)
+        digits_ref[t] = rows.astype(BF16)
 
 
 def tail_rows(weight):
@@ -266,7 +263,7 @@
 
 
 def weighted_tails(logs, log_count_ref, tails_ref, weight_ref):
-    log_count = log_count_ref[0 : weight_ref.shape[0], :]
+    log_count = log_count_ref[...]
     valid = log_count > NEGATIVE / 2
     free = jnp.where(valid, logs * -LOG2E, 4 * NEGATIVE)
     highest = jnp.max(jnp.max(free, axis=0, keepdims=True), axis=1, keepdims=True)
@@ -279,22 +276,25 @@
 
 
 def first_kernel(
-    meta_ref, mine_ref, other_ref, place_ref, log_count_ref, head_ref, points_ref, dead_ref,
-    logs_ref, coefs_ref, anchored_ref, base_ref,
-    tails_ref, packed_ref, energy_ref, live_ref, exponent_ref, low_ref, rows_ref, weight_ref,
+    meta_ref, mine_ref, other_ref, place_ref, digits_ref, head_ref, points_ref, dead_ref,
+    logs_ref, log_count_ref, coefs_ref, anchored_ref, base_ref,
+    tails_ref, packed_ref, energy_ref, live_ref, exponent_ref, low_ref, rows_ref,
 ):
     groups = mine_ref.shape[0]
     packed_ref[...] = jnp.zeros(packed_ref.shape, F32)
     for t in range(groups):
         chosen = jnp.where(iota((2 * LANES, LANES), 0) == place_ref[t : t + 1, :], 1.0, 0.0).astype(BF16)
-        moved = dot_nt(jnp.concatenate([mine_ref[t], other_ref[t]], 0), chosen)
+        moved = dot_nt(jnp.concatenate([mine_ref[t], other_ref[t], digits_ref[t]], 0), chosen)
         at = meta_ref[t]
         packed_ref[at] += moved[:, :LANES]
         packed_ref[at + 1] += moved[:, LANES:]
-    log_count = log_count_ref[0 : logs_ref.shape[1], :]
-    weight_ref[...] = log_count
+    for h in range(log_count_ref.shape[0]):
+        digits = [packed_ref[h, COMP + k : COMP + k + 1, :] for k in range(3)]
+        counts = digits[0] * 16384.0 + digits[1] * 128.0 + digits[2]
+        log_count_ref[h : h + 1, :] = jnp.where(counts > 0, jnp.log2(jnp.maximum(counts, 1.0)), NEGATIVE)
+    log_count = log_count_ref[...]
     for j in range(coefs_ref.shape[0]):
-        coefs_ref[j] = jnp.concatenate([packed_ref[2 * j], packed_ref[2 * j + 1]], 1).astype(BF16)
+        coefs_ref[j] = jnp.concatenate([packed_ref[2 * j, 0:COMP, :], packed_ref[2 * j + 1, 0:COMP, :]], 1).astype(BF16)
         tails_ref[j] = tail_rows(tile_row(log_count, j))
 
     def denominators(c):
@@ -305,7 +305,7 @@
 
     each_chunk(points_ref.shape[0], denominators)
     counted_log_sums(
-        weight_ref, coefs_ref, tails_ref, head_ref, live_ref, exponent_ref, rows_ref, low_ref
+        log_count_ref, coefs_ref, tails_ref, head_ref, live_ref, exponent_ref, rows_ref, low_ref
     )
     logs_ref[...] = jnp.broadcast_to(rows_ref[...][None], logs_ref.shape)
 
@@ -416,7 +416,7 @@
     logden_ref[...] = jnp.broadcast_to(logden[None], logden_ref.shape)
 
 
-def iterated(slot_rows, meta, mine, other, place, log_count, head, points, dead):
+def iterated(slot_rows, meta, mine, other, place, digits, head, points, dead):
     samps = lax.axis_size(SAMP)
     groups = mine.shape[0]
     rows = points.shape[0]
@@ -431,19 +431,19 @@
     live_work = pltpu.VMEM((rows, LANES), BF16)
     exponent_work = pltpu.VMEM((rows, TILE), F32)
     low_work = pltpu.VMEM((8, TILE), F32)
-    logs, coefs, anchored, base = pl.pallas_call(
+    logs, log_count, coefs, anchored, base = pl.pallas_call(
         first_kernel,
         out_shape=(
-            shape((samps, slot_rows, LANES), F32), shape((tile_count, COMP, TILE), BF16), shape((rows, LANES), BF16),
+            shape((samps, slot_rows, LANES), F32), shape((slot_rows, LANES), F32), shape((tile_count, COMP, TILE), BF16), shape((rows, LANES), BF16),
             shape((rows, LANES), F32),
         ),
-        in_specs=[smem] + [vmem] * 7, out_specs=(vmem,) * 4,
+        in_specs=[smem] + [vmem] * 7, out_specs=(vmem,) * 5,
         scratch_shapes=[
-            tails_work, pltpu.VMEM((slot_rows + 2, COMP, LANES), F32), energy_work, live_work, exponent_work, low_work,
-            weight_work, weight_work,
+            tails_work, pltpu.VMEM((slot_rows + 2, COMP + TAIL, LANES), F32), energy_work, live_work, exponent_work, low_work,
+            weight_work,
         ],
         compiler_params=params, name="first",
-    )(meta, mine, other, place, log_count, head, points, dead)
+    )(meta, mine, other, place, digits, head, points, dead)
     logs = log_sum(exchanged(logs, SAMP))
     logs = copies_of_each(logs, STATE)
     logs = pl.pallas_call(
@@ -486,23 +486,23 @@
 
     half = COMP // 2
     mine = copies_of_each(lax.dynamic_slice_in_dim(coefficients, core * half, half, 0), STATE)
-    blocks = jnp.stack([block_window, block_fill])[None]
-    blocks = jnp.concatenate([blocks, lax.ppermute(blocks, SAMP[1], [(0, 1), (1, 0)])], 0)
+    pair = jnp.stack([block_window, block_fill])[None]
+    blocks = jnp.concatenate([pair, lax.ppermute(pair, SAMP[1], [(0, 1), (1, 0)])], 0)
     along = lax.axis_size(SAMP[0])
     turns = [[(i, (i + k) % along) for i in range(along)] for k in range(1, along)]
     pieces = [blocks] + [lax.ppermute(blocks, SAMP[0], turn) for turn in turns]
     head, points, dead = pl.pallas_call(
         points_kernel,
         out_shape=(shape((rows, LANES), BF16), shape((rows, LANES), BF16), shape((rows, LANES), F32)),
-        in_specs=[smem, smem, vmem], out_specs=(vmem, vmem, vmem),
+        in_specs=[smem, vmem, vmem], out_specs=(vmem, vmem, vmem),
         compiler_params=params, name="points",
-    )(spot, block_fill, lax.dynamic_slice_in_dim(components, position * rows, rows, 1))
+    )(spot, pair, lax.dynamic_slice_in_dim(components, position * rows, rows, 1))
     other = lax.ppermute(mine, SAMP[1], [(0, 1), (1, 0)])
-    place, meta, log_count = pl.pallas_call(
+    place, meta, digits = pl.pallas_call(
         count_kernel,
         out_shape=(
             shape((groups, LANES), jnp.int32), shape((groups + 8, LANES), jnp.int32),
-            shape((slot_rows, LANES), F32),
+            shape((groups, TAIL, LANES), BF16),
         ),
         in_specs=[vmem] * len(pieces), out_specs=(vmem, vmem, vmem), compiler_params=params, name="count",
     )(*pieces)
@@ -511,7 +511,7 @@
     free, logden = lax.cond(
         total <= SMALL,
         functools.partial(iterated, SMALL_ROWS), functools.partial(iterated, slot_rows),
-        meta, mine, other, place, log_count, head, points, dead,
+        meta, mine, other, place, digits, head, points, dead,
     )
     return free.reshape(-1), exchanged(logden, STATE).reshape(-1)
 

time: 111 us -> 110 us (level)
  transfers between devices with their start and end apart: 6 -> 6, of which waited for: 2 -> 2; matrix products, arithmetic and copies ran while one was open for 2% -> 2% of each run, Pallas kernels for 2% -> 1%
where the time goes in v8:
time: 110 us; the launch traced here: 109 us
  blocking collectives  59.6 us (54%)
  starting transfers between devices  16.3 us (15%)
  Pallas kernels  14.2 us (13%)
  waiting for transfers between devices  12.9 us (12%)
  local copies, waits for them, and re-layouts  3.64 us (3%)
  between operations  1.37 us (1%)
    all_to_all x5, blocking collectives, exchanged(): return lax.all_to_all(copies, axes, split_axis=0, concat_axis=0, tiled=True)  59.6 us
    all_to_all x1, waiting for transfers between devices, exchanged(): return lax.all_to_all(copies, axes, split_axis=0, concat_axis=0, tiled=True)  12.1 us
    all_to_all x1, starting transfers between devices, exchanged(): return lax.all_to_all(copies, axes, split_axis=0, concat_axis=0, tiled=True)  11.5 us
    pallas_call x1, Pallas kernels, iterated(): pl.pallas_call(second_kernel, out_shape=shape((samps, slot_rows + groups,...  6.54 us
    ppermute x3, starting transfers between devices, shards(): pieces = [blocks] + [lax.ppermute(blocks, SAMP[0], turn) for turn in turns]  4.83 us
    pallas_call x1, Pallas kernels, iterated(): pl.pallas_call(first_kernel, out_shape=(shape((samps, slot_rows, LANES),...  4.17 us
  transfers between devices with their start and end apart: 6, of which 2 were waited for; matrix products, arithmetic and copies ran while one was open for 2% of the time, Pallas kernels for 1%

profile of v8, /device:TPU:2, one launch (start us, length us, event | category | flops | bytes accessed | tf_op | source)
XLA Modules:
  0.0 109.1 jit_solution(3396439024142556075)
XLA Ops:
  0.6 0.0 copy-start
  0.7 0.7 copy-done
  1.4 0.7 broadcast_in_dim.15
  2.1 11.5 %all-to-all-start.8 = ((bf16[32,32,128]{2,1,0:T(8,128)(2,1)}), bf16[32,32,128]{2,1,0:T(8,128)(2,1)S(1)}, u32[]{:S(2)}, u32[]{:S(2)}) async-start(bf16[32,32,128]{2,1,0:T(8,128)(2,1)} %broadcast_in_dim.15), calls=%async_computation.8 | async-start | bytes 524288 | tf_op jit(solution)/shard_map/all_to_all | solution.py:33
  13.6 0.7 add_bitcast_fusion.own_ref
  14.3 0.0 collective-permute-start
  14.3 12.1 %all-to-all-done.8 = bf16[32,32,128]{2,1,0:T(8,128)(2,1)S(1)} async-done(((bf16[32,32,128]{2,1,0:T(8,128)(2,1)}), bf16[32,32,128]{2,1,0:T(8,128)(2,1)S(1)}, u32[]{:S(2)}, u32[]{:S(2)}) %all-to-all-start.8) | async-done | bytes 262176 | tf_op jit(solution)/shard_map/all_to_all | solution.py:33
  26.4 0.0 collective-permute-start.4
  26.4 0.9 constant_dynamic-slice_fusion.block_ref
  27.3 0.0 collective-permute-done
  27.3 0.6 collective-permute-start.3
  27.9 2.4 %collective-permute-start.2 = (s32[2,2,256]{2,1,0:T(2,128)S(1)}, s32[2,2,256]{2,1,0:T(2,128)S(1)}, u32[]{:S(2)}, u32[]{:S(2)}) collective-permute-start(s32[2,2,256]{2,1,0:T(2,128)S(1)} %pad_add_fusion.refs_0_), channel_id=1, source_target_pairs={{0,128},{64,192},{128,0},{192,64},{1,129},{65,193},{129,1},{193,65... | collective-permute-start | bytes 12296 | tf_op jit(solution)/shard_map/ppermute | solution.py:493
  30.4 1.8 %collective-permute-start.1 = (s32[2,2,256]{2,1,0:T(2,128)S(1)}, s32[2,2,256]{2,1,0:T(2,128)S(1)}, u32[]{:S(2)}, u32[]{:S(2)}) collective-permute-start(s32[2,2,256]{2,1,0:T(2,128)S(1)} %pad_add_fusion.refs_0_), channel_id=1, source_target_pairs={{0,64},{64,128},{128,192},{192,0},{1,65},{65,129},{129,193},{193,1... | collective-permute-start | bytes 12296 | tf_op jit(solution)/shard_map/ppermute | solution.py:493
  32.2 0.1 pad_add_fusion.1.spot_ref
  32.2 0.9 points.1
  33.2 0.0 collective-permute-done.2.refs_2_
  33.2 0.8 collective-permute-done.1.refs_1_
  34.0 0.6 count.1
  34.6 0.5 slice.10
  35.7 0.0 collective-permute-done.4
  35.7 59.0 %conditional.1 = (f32[32,8,128]{2,1,0:T(8,128)S(1)}, f32[128]{0:T(128)}) conditional(s32[]{:T(128)} %bitcast.7, (s32[40,128]{1,0:T(8,128)S(1)}, bf16[32,32,128]{2,1,0:T(8,128)(2,1)S(1)}, bf16[32,32,128]{2,1,0:T(8,128)(2,1)S(1)}, s32[32,128]{1,0:T(8,128)S(1)}, bf16[32,16,128]{2,1,0:T(8,128)(2,1)S(1)}, /*index=5*/bf16[1024,128]{1,0:T(8,128)(2,1)S(1)}, ...), branch_computations={%region_0.0_spmd, %region_3.0_spmd} | conditional | flops 47104 | bytes 2326804 | solution.py:511
  35.9 0.1 copy.7
  36.0 4.2 %first.3 = (f32[8,8,128]{2,1,0:T(8,128)S(1)}, f32[8,128]{1,0:T(8,128)S(1)}, bf16[4,64,256]{2,1,0:T(8,128)(2,1)S(1)}, bf16[1024,128]{1,0:T(8,128)(2,1)S(1)}, f32[1024,128]{1,0:T(8,128)S(1)}) custom-call(s32[32]{0:T(128)S(1)} %slice_bitcast_fusion.1.meta_ref, bf16[32,32,128]{2,1,0:T(8,128)(2,1)S(1)} %get-tuple-element.57.mine_ref, ...), custom_call_target="tpu_custom_call" | custom-call | tf_op jit(solution)/shard_map/cond/branch_1_fun/first/pallas_call | solution.py:434
  40.2 8.9 %all_to_all.46 = f32[8,8,128]{2,1,0:T(8,128)S(1)} all-to-all(f32[8,8,128]{2,1,0:T(8,128)S(1)} %get-tuple-element.64), channel_id=1, replica_groups=mesh['samp_0'=4,'samp_1'=2,'state_0'=8,'state_1'=4] {'samp_0','samp_1'}, dimensions={0} | all-to-all | bytes 65536 | tf_op jit(solution)/shard_map/cond/branch_1_fun/all_to_all | solution.py:33
  49.2 14.3 %all_to_all.47.logs_in_ref = f32[32,8,128]{2,1,0:T(8,128)S(1)} all-to-all(f32[32,8,128]{2,1,0:T(8,128)S(1)} %broadcast_in_dim.2), channel_id=1, replica_groups=mesh['samp_0'=4,'samp_1'=2,'state_0'=8,'state_1'=4] {'state_0','state_1'}, dimensions={0} | all-to-all | bytes 262144 | tf_op jit(solution)/shard_map/cond/branch_1_fun/all_to_all | solution.py:33
  63.5 6.5 %second.3 = f32[8,40,128]{2,1,0:T(8,128)S(1)} custom-call(f32[32,8,128]{2,1,0:T(8,128)S(1)} %all_to_all.47.logs_in_ref, bf16[32,32,128]{2,1,0:T(8,128)(2,1)S(1)} %get-tuple-element.57.mine_ref, bf16[32,32,128]{2,1,0:T(8,128)(2,1)S(1)} %get-tuple-element.58.other_ref, f32[8,128]{1,0:T(8,128)S(1)} %get-tuple-element.65.log_count_ref, ...), custom_call_target="tpu_custom_call" | custom-call | tf_op jit(solution)/shard_map/cond/branch_1_fun/second/pallas_call | solution.py:449
  70.0 8.9 %all_to_all.48.logs_ref = f32[8,40,128]{2,1,0:T(8,128)S(1)} all-to-all(f32[8,40,128]{2,1,0:T(8,128)S(1)} %second.3), channel_id=1, replica_groups=mesh['samp_0'=4,'samp_1'=2,'state_0'=8,'state_1'=4] {'samp_0','samp_1'}, dimensions={0} | all-to-all | bytes 327680 | tf_op jit(solution)/shard_map/cond/branch_1_fun/all_to_all | solution.py:33
  78.9 0.1 message.3
  79.0 13.8 %all_to_all.49.logs_in_ref = f32[32,8,128]{2,1,0:T(8,128)S(1)} all-to-all(f32[32,8,128]{2,1,0:T(8,128)S(1)} %message.3), channel_id=1, replica_groups=mesh['samp_0'=4,'samp_1'=2,'state_0'=8,'state_1'=4] {'state_0','state_1'}, dimensions={0} | all-to-all | bytes 262144 | tf_op jit(solution)/shard_map/cond/branch_1_fun/all_to_all | solution.py:33
  92.8 1.9 %third.3 = (f32[1,128]{1,0:T(1,128)}, f32[32,8,128]{2,1,0:T(8,128)S(1)}) custom-call(f32[32,8,128]{2,1,0:T(8,128)S(1)} %all_to_all.49.logs_in_ref, f32[8,128]{1,0:T(8,128)S(1)} %get-tuple-element.65.log_count_ref, bf16[4,64,256]{2,1,0:T(8,128)(2,1)S(1)} %get-tuple-element.66.coefs_ref, bf16[1024,128]{1,0:T(8,128)(2,1)S(1)} %get-tuple-element.61.head_ref, ...), custom_call_target="tpu_custom_call" | custom-call | tf_op jit(solution)/shard_map/cond/branch_1_fun/third/pallas_call | solution.py:465
  94.7 13.8 %all_to_all.50 = f32[32,8,128]{2,1,0:T(8,128)S(1)} all-to-all(f32[32,8,128]{2,1,0:T(8,128)S(1)} %get-tuple-element.88), channel_id=1, replica_groups=mesh['samp_0'=4,'samp_1'=2,'state_0'=8,'state_1'=4] {'state_0','state_1'}, dimensions={0} | all-to-all | bytes 262144 | tf_op jit(solution)/shard_map/all_to_all | solution.py:33
  108.5 0.7 copy.13
  (8 shorter events, 0.1 us)
Async XLA Ops:
  0.6 0.7 copy-start
  2.1 24.3 %all-to-all-start.8 = ((bf16[32,32,128]{2,1,0:T(8,128)(2,1)}), bf16[32,32,128]{2,1,0:T(8,128)(2,1)S(1)}, u32[]{:S(2)}, u32[]{:S(2)}) async-start(bf16[32,32,128]{2,1,0:T(8,128)(2,1)} %broadcast_in_dim.15), calls=%async_computation.8 | async-start | bytes 524288 | tf_op jit(solution)/shard_map/all_to_all | solution.py:33
  14.3 13.0 %collective-permute-start = (s32[1,2,256]{2,1,0:T(2,128)S(1)}, s32[1,2,256]{2,1,0:T(2,128)S(1)}, u32[]{:S(2)}, u32[]{:S(2)}) collective-permute-start(s32[1,2,256]{2,1,0:T(2,128)S(1)} %add_bitcast_fusion.own_ref), channel_id=1, source_target_pairs={{0,32},{32,0},{1,33},{33,1},{2,34},{34,2},{3,35},{35,3},{4,36},{36... | collective-permute-start | bytes 6152 | tf_op jit(solution)/shard_map/ppermute | solution.py:490
  26.4 9.3 %collective-permute-start.4 = (bf16[32,32,128]{2,1,0:T(8,128)(2,1)S(1)}, bf16[32,32,128]{2,1,0:T(8,128)(2,1)S(1)}, u32[]{:S(2)}, u32[]{:S(2)}) collective-permute-start(bf16[32,32,128]{2,1,0:T(8,128)(2,1)S(1)} %all-to-all-done.8), channel_id=1, source_target_pairs={{0,32},{32,0},{1,33},{33,1},{2,34},{34,2},{3,35},{35,3},{4,36},{36... | collective-permute-start | bytes 786440 | tf_op jit(solution)/shard_map/ppermute | solution.py:500
  27.3 5.8 %collective-permute-start.3 = (s32[2,2,256]{2,1,0:T(2,128)S(1)}, s32[2,2,256]{2,1,0:T(2,128)S(1)}, u32[]{:S(2)}, u32[]{:S(2)}) collective-permute-start(s32[2,2,256]{2,1,0:T(2,128)S(1)} %pad_add_fusion.refs_0_), channel_id=1, source_target_pairs={{0,192},{64,0},{128,64},{192,128},{1,193},{65,1},{129,65},{193,129... | collective-permute-start | bytes 12296 | tf_op jit(solution)/shard_map/ppermute | solution.py:493
  27.9 5.2 %collective-permute-start.2 = (s32[2,2,256]{2,1,0:T(2,128)S(1)}, s32[2,2,256]{2,1,0:T(2,128)S(1)}, u32[]{:S(2)}, u32[]{:S(2)}) collective-permute-start(s32[2,2,256]{2,1,0:T(2,128)S(1)} %pad_add_fusion.refs_0_), channel_id=1, source_target_pairs={{0,128},{64,192},{128,0},{192,64},{1,129},{65,193},{129,1},{193,65... | collective-permute-start | bytes 12296 | tf_op jit(solution)/shard_map/ppermute | solution.py:493
  30.4 3.6 %collective-permute-start.1 = (s32[2,2,256]{2,1,0:T(2,128)S(1)}, s32[2,2,256]{2,1,0:T(2,128)S(1)}, u32[]{:S(2)}, u32[]{:S(2)}) collective-permute-start(s32[2,2,256]{2,1,0:T(2,128)S(1)} %pad_add_fusion.refs_0_), channel_id=1, source_target_pairs={{0,64},{64,128},{128,192},{192,0},{1,65},{65,129},{129,193},{193,1... | collective-permute-start | bytes 12296 | tf_op jit(solution)/shard_map/ppermute | solution.py:493
